TPU v7x, 8 devices: a whole 2x2x1 slice. The times are simulated.
8 devices in a mesh: dp: 1 (over z), row: 2 (over y), col: 4 (over x, core).
Axes of the slice: x: 2, y: 2, z: 1, core: 2. Of those that a mesh axis runs over, the one named last changes fastest.
Arguments:
- x: bfloat16 [2048, 896], P(('dp', 'row', 'col'))
- route_idx: int32 [2048, 8], P(('dp', 'row', 'col'))
- gates: float32 [2048, 8], P(('dp', 'row', 'col'))
- w1: bfloat16 [384, 896, 256], P(('row', 'col'))
- w3: bfloat16 [384, 896, 256], P(('row', 'col'))
- w2: bfloat16 [384, 256, 896], P(('row', 'col'))
- dy: bfloat16 [2048, 896], P(('dp', 'row', 'col'))
Outputs:
- output 1: bfloat16 [2048, 896], P(('dp', 'row', 'col'))
- output 2: bfloat16 [2048, 896], P(('dp', 'row', 'col'))
- output 3: float32 [2048, 8], P(('dp', 'row', 'col'))
- output 4: float32 [384, 896, 256], P(('dp', 'row', 'col'))
- output 5: float32 [384, 896, 256], P(('dp', 'row', 'col'))
- output 6: float32 [384, 256, 896], P(('dp', 'row', 'col'))
All inputs are finite; a program needn't handle non-finite values.
Results may differ from a plain program's by a relative error of at most 0.00783231.
Values are sent between devices in bfloat16 or wider.
A program may use at most 1 GiB of HBM per device.

v0:
```python
import jax
import jax.numpy as jnp
from jax import lax
from jax.sharding import PartitionSpec as P


def slot_positions(ridx, ne, cap):
    tok, top = ridx.shape
    n = tok * top
    ef = ridx.reshape(n)
    order = jnp.argsort(ef, stable=True).astype(jnp.int32)
    es = ef[order]
    first = jnp.searchsorted(es, es, side='left').astype(jnp.int32)
    rank = jnp.arange(n, dtype=jnp.int32) - first
    pos = jnp.zeros((n,), jnp.int32).at[order].set(es * cap + rank)
    inv = jnp.full((ne * cap,), n, jnp.int32).at[pos].set(jnp.arange(n, dtype=jnp.int32))
    return pos, inv


def to_experts(buf, nd, el, cap):
    d = buf.shape[-1]
    return buf.reshape(nd, el, cap, d).transpose(1, 0, 2, 3).reshape(el, nd * cap, d)


def from_experts(buf, nd, el, cap):
    d = buf.shape[-1]
    return buf.reshape(el, nd, cap, d).transpose(1, 0, 2, 3).reshape(nd, el * cap, d)


def expert_forward(xe, w1, w3, w2):
    u = jnp.einsum('ecd,edf->ecf', xe, w1, preferred_element_type=jnp.float32).astype(jnp.bfloat16)
    v = jnp.einsum('ecd,edf->ecf', xe, w3, preferred_element_type=jnp.float32).astype(jnp.bfloat16)
    uf = u.astype(jnp.float32)
    a = (uf * jax.nn.sigmoid(uf) * v.astype(jnp.float32)).astype(jnp.bfloat16)
    o = jnp.einsum('ecf,efd->ecd', a, w2, preferred_element_type=jnp.float32).astype(jnp.bfloat16)
    return u, v, a, o


def expert_backward(xe, u, v, a, doe, w1, w3, w2):
    gw2 = jnp.einsum('ecf,ecd->efd', a, doe, preferred_element_type=jnp.float32)
    da = jnp.einsum('ecd,efd->ecf', doe, w2, preferred_element_type=jnp.float32)
    uf = u.astype(jnp.float32)
    vf = v.astype(jnp.float32)
    sg = jax.nn.sigmoid(uf)
    du = (da * vf * sg * (1.0 + uf * (1.0 - sg))).astype(jnp.bfloat16)
    dv = (da * uf * sg).astype(jnp.bfloat16)
    gw1 = jnp.einsum('ecd,ecf->edf', xe, du, preferred_element_type=jnp.float32)
    gw3 = jnp.einsum('ecd,ecf->edf', xe, dv, preferred_element_type=jnp.float32)
    dxe = (jnp.einsum('ecf,edf->ecd', du, w1, preferred_element_type=jnp.float32) + jnp.einsum('ecf,edf->ecd', dv, w3, preferred_element_type=jnp.float32)).astype(jnp.bfloat16)
    return gw1, gw3, gw2, dxe


def solution(mesh):
    nd = mesh.shape['row'] * mesh.shape['col']
    grp = ('row', 'col')
    tspec = P(('dp', 'row', 'col'), None)
    wspec = P(grp, None, None)
    gspec = P(('dp', 'row', 'col'), None, None)

    def exchange(buf):
        return lax.all_to_all(buf, grp, 0, 0, tiled=True)

    def local(x, ridx, gates, w1, w3, w2, dy):
        tok, d = x.shape
        top = ridx.shape[1]
        el = w1.shape[0]
        ne = el * nd
        cap = (4 * tok * top + ne - 1) // ne
        n = tok * top
        pos, inv = slot_positions(ridx, ne, cap)
        zrow = jnp.zeros((1, d), x.dtype)
        send = jnp.concatenate([x, zrow])[inv // top].reshape(nd, el * cap, d)
        xe = to_experts(exchange(send), nd, el, cap)
        u, v, a, oe = expert_forward(xe, w1, w3, w2)
        ret = exchange(from_experts(oe, nd, el, cap)).reshape(ne * cap, d)
        ob = ret[pos].reshape(tok, top, d)
        y = jnp.sum(gates[:, :, None] * ob.astype(jnp.float32), axis=1).astype(jnp.bfloat16)
        dgates = jnp.einsum('td,tjd->tj', dy, ob, preferred_element_type=jnp.float32)
        do = (gates[:, :, None] * dy[:, None, :].astype(jnp.float32)).astype(jnp.bfloat16).reshape(n, d)
        dsend = jnp.concatenate([do, zrow])[inv].reshape(nd, el * cap, d)
        doe = to_experts(exchange(dsend), nd, el, cap)
        gw1, gw3, gw2, dxe = expert_backward(xe, u, v, a, doe, w1, w3, w2)
        dret = exchange(from_experts(dxe, nd, el, cap)).reshape(ne * cap, d)
        dx = jnp.sum(dret[pos].reshape(tok, top, d).astype(jnp.float32), axis=1).astype(jnp.bfloat16)
        return y, dx, dgates, gw1, gw3, gw2

    return jax.shard_map(local, mesh=mesh, in_specs=(tspec, tspec, tspec, wspec, wspec, wspec, tspec), out_specs=(tspec, tspec, tspec, gspec, gspec, gspec), check_vma=False)
```

profile of v0, /device:TPU:0, one launch (start us, length us, event | category | flops | bytes accessed | tf_op | source)
XLA Modules:
  0.0 911.0 jit_solution(3267743537271552848)
XLA Ops:
  1.6 5.0 sort.17
  6.6 11.8 %gather_fusion.1 = s32[2048]{0:T(1024)S(1)} fusion(s32[2048]{0:T(1024)S(1)} %reshape.63, s32[2048]{0:T(1024)S(1)} %get-tuple-element.105), kind=kCustom, calls=%fused_computation.1 | custom fusion | bytes 24576 | tf_op jit(solution)/shard_map/gather | solution.py:12
  18.4 142.4 %while.25 = (s32[]{:T(128)}, u32[2048]{0:T(1024)S(1)}, u32[2048]{0:T(1024)S(1)}, s32[2048]{0:T(1024)S(1)}, s32[]{:T(128)}, /*index=5*/s32[]{:T(128)}, s32[]{}) while((s32[]{:T(128)}, u32[2048]{0:T(1024)S(1)}, u32[2048]{0:T(1024)S(1)}, s32[2048]{0:T(1024)S(1)}, s32[]{:T(128)}, /*index=5*/s32[]{:T(128)}, s32[]{}) %tuple.45), condition=%wide.region_2.3_spmd.clone, body=%wide.region_1.2_spmd.clone.sunk | while | flops 38916 | bytes 135269 | solution.py:13
  18.5 11.8 %gather_fusion = s32[2048]{0:T(1024)S(1)} fusion(s32[2048]{0:T(1024)S(1)} %get-tuple-element.157, u32[2048]{0:T(1024)S(1)} %broadcast_clamp_fusion.4), kind=kCustom, calls=%fused_computation.clone.clone.1 | custom fusion | bytes 24576 | tf_op jit(solution)/shard_map/jit(searchsorted)/jit(_searchsorted_scan_impl)/vmap(jit(_searchsorted_scan_impl))/while/body/eval_jaxpr/gather | solution.py:13
  30.3 11.8 %gather_fusion = s32[2048]{0:T(1024)S(1)} fusion(s32[2048]{0:T(1024)S(1)} %get-tuple-element.157, u32[2048]{0:T(1024)S(1)} %broadcast_clamp_fusion.4), kind=kCustom, calls=%fused_computation.clone.clone.1 | custom fusion | bytes 24576 | tf_op jit(solution)/shard_map/jit(searchsorted)/jit(_searchsorted_scan_impl)/vmap(jit(_searchsorted_scan_impl))/while/body/eval_jaxpr/gather | solution.py:13
  42.2 11.8 %gather_fusion = s32[2048]{0:T(1024)S(1)} fusion(s32[2048]{0:T(1024)S(1)} %get-tuple-element.157, u32[2048]{0:T(1024)S(1)} %broadcast_clamp_fusion.4), kind=kCustom, calls=%fused_computation.clone.clone.1 | custom fusion | bytes 24576 | tf_op jit(solution)/shard_map/jit(searchsorted)/jit(_searchsorted_scan_impl)/vmap(jit(_searchsorted_scan_impl))/while/body/eval_jaxpr/gather | solution.py:13
  54.1 11.8 %gather_fusion = s32[2048]{0:T(1024)S(1)} fusion(s32[2048]{0:T(1024)S(1)} %get-tuple-element.157, u32[2048]{0:T(1024)S(1)} %broadcast_clamp_fusion.4), kind=kCustom, calls=%fused_computation.clone.clone.1 | custom fusion | bytes 24576 | tf_op jit(solution)/shard_map/jit(searchsorted)/jit(_searchsorted_scan_impl)/vmap(jit(_searchsorted_scan_impl))/while/body/eval_jaxpr/gather | solution.py:13
  65.9 11.8 %gather_fusion = s32[2048]{0:T(1024)S(1)} fusion(s32[2048]{0:T(1024)S(1)} %get-tuple-element.157, u32[2048]{0:T(1024)S(1)} %broadcast_clamp_fusion.4), kind=kCustom, calls=%fused_computation.clone.clone.1 | custom fusion | bytes 24576 | tf_op jit(solution)/shard_map/jit(searchsorted)/jit(_searchsorted_scan_impl)/vmap(jit(_searchsorted_scan_impl))/while/body/eval_jaxpr/gather | solution.py:13
  77.8 11.8 %gather_fusion = s32[2048]{0:T(1024)S(1)} fusion(s32[2048]{0:T(1024)S(1)} %get-tuple-element.157, u32[2048]{0:T(1024)S(1)} %broadcast_clamp_fusion.4), kind=kCustom, calls=%fused_computation.clone.clone.1 | custom fusion | bytes 24576 | tf_op jit(solution)/shard_map/jit(searchsorted)/jit(_searchsorted_scan_impl)/vmap(jit(_searchsorted_scan_impl))/while/body/eval_jaxpr/gather | solution.py:13
  89.7 11.8 %gather_fusion = s32[2048]{0:T(1024)S(1)} fusion(s32[2048]{0:T(1024)S(1)} %get-tuple-element.157, u32[2048]{0:T(1024)S(1)} %broadcast_clamp_fusion.4), kind=kCustom, calls=%fused_computation.clone.clone.1 | custom fusion | bytes 24576 | tf_op jit(solution)/shard_map/jit(searchsorted)/jit(_searchsorted_scan_impl)/vmap(jit(_searchsorted_scan_impl))/while/body/eval_jaxpr/gather | solution.py:13
  101.5 11.8 %gather_fusion = s32[2048]{0:T(1024)S(1)} fusion(s32[2048]{0:T(1024)S(1)} %get-tuple-element.157, u32[2048]{0:T(1024)S(1)} %broadcast_clamp_fusion.4), kind=kCustom, calls=%fused_computation.clone.clone.1 | custom fusion | bytes 24576 | tf_op jit(solution)/shard_map/jit(searchsorted)/jit(_searchsorted_scan_impl)/vmap(jit(_searchsorted_scan_impl))/while/body/eval_jaxpr/gather | solution.py:13
  113.4 11.8 %gather_fusion = s32[2048]{0:T(1024)S(1)} fusion(s32[2048]{0:T(1024)S(1)} %get-tuple-element.157, u32[2048]{0:T(1024)S(1)} %broadcast_clamp_fusion.4), kind=kCustom, calls=%fused_computation.clone.clone.1 | custom fusion | bytes 24576 | tf_op jit(solution)/shard_map/jit(searchsorted)/jit(_searchsorted_scan_impl)/vmap(jit(_searchsorted_scan_impl))/while/body/eval_jaxpr/gather | solution.py:13
  125.3 11.8 %gather_fusion = s32[2048]{0:T(1024)S(1)} fusion(s32[2048]{0:T(1024)S(1)} %get-tuple-element.157, u32[2048]{0:T(1024)S(1)} %broadcast_clamp_fusion.4), kind=kCustom, calls=%fused_computation.clone.clone.1 | custom fusion | bytes 24576 | tf_op jit(solution)/shard_map/jit(searchsorted)/jit(_searchsorted_scan_impl)/vmap(jit(_searchsorted_scan_impl))/while/body/eval_jaxpr/gather | solution.py:13
  137.1 11.8 %gather_fusion = s32[2048]{0:T(1024)S(1)} fusion(s32[2048]{0:T(1024)S(1)} %get-tuple-element.157, u32[2048]{0:T(1024)S(1)} %broadcast_clamp_fusion.4), kind=kCustom, calls=%fused_computation.clone.clone.1 | custom fusion | bytes 24576 | tf_op jit(solution)/shard_map/jit(searchsorted)/jit(_searchsorted_scan_impl)/vmap(jit(_searchsorted_scan_impl))/while/body/eval_jaxpr/gather | solution.py:13
  149.0 11.8 %gather_fusion = s32[2048]{0:T(1024)S(1)} fusion(s32[2048]{0:T(1024)S(1)} %get-tuple-element.157, u32[2048]{0:T(1024)S(1)} %broadcast_clamp_fusion.4), kind=kCustom, calls=%fused_computation.clone.clone.1 | custom fusion | bytes 24576 | tf_op jit(solution)/shard_map/jit(searchsorted)/jit(_searchsorted_scan_impl)/vmap(jit(_searchsorted_scan_impl))/while/body/eval_jaxpr/gather | solution.py:13
  160.9 8.0 scatter_custom_fusion
  169.5 8.0 scatter_custom_fusion.1
  177.7 25.5 %gather_fusion.2 = bf16[8448,896]{1,0:T(8,128)(2,1)} fusion(bf16[257,896]{1,0:T(8,128)(2,1)S(1)} %concatenate.6, s32[9216]{0:T(1024)S(1)} %get-tuple-element.110), kind=kCustom, calls=%fused_computation.2 | custom fusion | bytes 30311424 | tf_op jit(solution)/shard_map/gather | solution.py:72
  210.8 35.6 %gather_fusion.4 = bf16[8448,896]{1,0:T(8,128)(2,1)} fusion(bf16[2049,896]{1,0:T(8,128)(2,1)} %concatenate.7, s32[9216]{0:T(1024)S(1)} %get-tuple-element.109), kind=kCustom, calls=%fused_computation.4 | custom fusion | bytes 30311424 | tf_op jit(solution)/shard_map/gather | solution.py:80
  246.4 128.8 %all-to-all-done = bf16[8,1056,896]{2,1,0:T(8,128)(2,1)} async-done(((bf16[8,1056,896]{2,1,0:T(8,128)(2,1)}), bf16[8,1056,896]{2,1,0:T(8,128)(2,1)}, u32[]{:S(2)}, u32[]{:S(2)}) %all-to-all-start) | async-done | bytes 15138848 | tf_op jit(solution)/shard_map/all_to_all | solution.py:61
  375.1 4.5 all-to-all-start.2
  379.6 24.7 %copy.35 = bf16[8,1056,896]{2,0,1:T(8,128)(2,1)S(1)} copy(bf16[8,1056,896]{2,1,0:T(8,128)(2,1)} %all-to-all-done) | data formatting | bytes 30277632 | tf_op jit(solution)/shard_map/all_to_all | solution.py:61
  404.3 7.6 copy.36
  411.9 18.1 %fusion.25 = bf16[48,176,256]{2,1,0:T(8,128)(2,1)} fusion(bf16[48,896,256]{2,1,0:T(8,128)(2,1)} %param.12, bf16[48,176,896]{2,0,1:T(8,128)(2,1)} %bitcast.42), kind=kOutput, calls=%fused_computation.48 | convolution fusion | flops 3877699584 | bytes 41484288 | tf_op jit(solution)/shard_map/ecd,edf->ecf/dot_general | solution.py:31
  430.0 18.2 %fusion.28 = bf16[48,176,256]{2,1,0:T(8,128)(2,1)} fusion(bf16[48,896,256]{2,1,0:T(8,128)(2,1)} %param.13, bf16[48,176,896]{2,0,1:T(8,128)(2,1)} %bitcast.43), kind=kOutput, calls=%fused_computation.49 | convolution fusion | flops 3877699584 | bytes 41484288 | tf_op jit(solution)/shard_map/ecd,edf->ecf/dot_general | solution.py:32
  448.2 17.7 %convolution_convert_fusion = bf16[48,176,896]{2,1,0:T(8,128)(2,1)} fusion(bf16[48,256,896]{2,1,0:T(8,128)(2,1)} %param.14, bf16[48,176,256]{2,1,0:T(8,128)(2,1)} %fusion.28, bf16[48,176,256]{2,1,0:T(8,128)(2,1)} %fusion.25), kind=kOutput, calls=%fused_computation.23 | convolution fusion | flops 3900407808 | bytes 45809664 | tf_op jit(solution)/shard_map/ecf,efd->ecd/dot_general | solution.py:35
  465.9 10.2 %copy.39 = bf16[48,176,896]{2,0,1:T(8,128)(2,1)S(1)} copy(bf16[48,176,896]{2,1,0:T(8,128)(2,1)} %convolution_convert_fusion) | data formatting | bytes 30277632 | tf_op jit(solution)/shard_map/convert_element_type | solution.py:35
  476.1 12.6 %copy.40 = bf16[8,48,22,896]{3,0,2,1:T(8,128)(2,1)S(1)} copy(bf16[8,48,22,896]{3,1,2,0:T(8,128)(2,1)S(1)} %bitcast.47) | data formatting | bytes 30277632 | tf_op jit(solution)/shard_map/transpose | solution.py:27
  488.7 6.5 copy.41
  495.2 50.8 %all-to-all-done.2 = bf16[8,1056,896]{2,1,0:T(8,128)(2,1)} async-done(((bf16[8,1056,896]{2,1,0:T(8,128)(2,1)}), bf16[8,1056,896]{2,1,0:T(8,128)(2,1)}, u32[]{:S(2)}, u32[]{:S(2)}) %all-to-all-start.2) | async-done | bytes 15138848 | tf_op jit(solution)/shard_map/all_to_all | solution.py:61
  546.0 4.7 all-to-all-start.1
  550.7 24.7 %copy.43 = bf16[8,1056,896]{2,0,1:T(8,128)(2,1)S(1)} copy(bf16[8,1056,896]{2,1,0:T(8,128)(2,1)} %all-to-all-done.2) | data formatting | bytes 30277632 | tf_op jit(solution)/shard_map/all_to_all | solution.py:61
  575.4 7.5 copy.44
  582.9 22.7 %fusion.15 = (bf16[48,176,256]{2,1,0:T(8,128)(2,1)}, f32[48,176,256]{2,1,0:T(8,128)}) fusion(bf16[48,176,256]{2,1,0:T(8,128)(2,1)} %fusion.28, bf16[48,176,256]{2,1,0:T(8,128)(2,1)} %fusion.25, bf16[48,256,896]{2,1,0:T(8,128)(2,1)} %param.14, bf16[48,176,896]{2,0,1:T(8,128)(2,1)} %bitcast.54), kind=kOutput, calls=%fused_computation.35 | convolution fusion | flops 3901489152 | bytes 58785792 | tf_op jit(solution)/shard_map/ecd,efd->ecf/dot_general | solution.py:41
  605.5 21.9 %fusion.42 = f32[48,176,896]{2,1,0:T(8,128)} fusion(bf16[48,176,256]{2,1,0:T(8,128)(2,1)} %get-tuple-element.107, bf16[48,896,256]{2,1,0:T(8,128)(2,1)} %param.12), kind=kOutput, calls=%fused_computation.71 | convolution fusion | flops 3875536896 | bytes 56623104 | tf_op jit(solution)/shard_map/ecf,edf->ecd/dot_general | solution.py:49
  627.4 27.6 %add_convert_fusion = bf16[48,176,896]{2,1,0:T(8,128)(2,1)} fusion(f32[48,176,896]{2,1,0:T(8,128)} %fusion.42, bf16[48,896,256]{2,1,0:T(8,128)(2,1)} %param.13, f32[48,176,256]{2,1,0:T(8,128)} %get-tuple-element.108, bf16[48,176,256]{2,1,0:T(8,128)(2,1)} %fusion.25), kind=kOutput, calls=%fused_computation.12 | convolution fusion | flops 3905814528 | bytes 80412672 | tf_op jit(solution)/shard_map/ecf,edf->ecd/dot_general | solution.py:49
  655.0 10.2 %copy.46 = bf16[48,176,896]{2,0,1:T(8,128)(2,1)S(1)} copy(bf16[48,176,896]{2,1,0:T(8,128)(2,1)} %add_convert_fusion) | data formatting | bytes 30277632 | tf_op jit(solution)/shard_map/convert_element_type | solution.py:49
  665.2 12.7 %copy.47 = bf16[8,48,22,896]{3,0,2,1:T(8,128)(2,1)S(1)} copy(bf16[8,48,22,896]{3,1,2,0:T(8,128)(2,1)S(1)} %bitcast.50) | data formatting | bytes 30277632 | tf_op jit(solution)/shard_map/transpose | solution.py:27
  678.0 6.9 copy.48
  684.9 32.3 %all-to-all-done.1 = bf16[8,1056,896]{2,1,0:T(8,128)(2,1)} async-done(((bf16[8,1056,896]{2,1,0:T(8,128)(2,1)}), bf16[8,1056,896]{2,1,0:T(8,128)(2,1)}, u32[]{:S(2)}, u32[]{:S(2)}) %all-to-all-start.1) | async-done | bytes 15138848 | tf_op jit(solution)/shard_map/all_to_all | solution.py:61
  721.4 23.1 %fusion.6 = f32[48,896,256]{2,1,0:T(8,128)} fusion(bf16[48,176,256]{2,1,0:T(8,128)(2,1)} %get-tuple-element.107, bf16[48,176,896]{2,0,1:T(8,128)(2,1)} %bitcast.44), kind=kOutput, calls=%fused_computation.26 | convolution fusion | flops 3875536896 | bytes 63504384 | tf_op jit(solution)/shard_map/ecd,ecf->edf/dot_general | solution.py:47
  744.6 26.0 %fusion = f32[48,256,896]{2,1,0:T(8,128)} fusion(bf16[48,176,896]{2,0,1:T(8,128)(2,1)} %bitcast.55, bf16[48,176,256]{2,1,0:T(8,128)(2,1)} %fusion.28, bf16[48,176,256]{2,1,0:T(8,128)(2,1)} %fusion.25), kind=kOutput, calls=%fused_computation.17 | convolution fusion | flops 3892838400 | bytes 67829760 | tf_op jit(solution)/shard_map/ecf,ecd->efd/dot_general | solution.py:40
  770.6 27.3 %fusion.4 = f32[48,896,256]{2,1,0:T(8,128)} fusion(bf16[48,176,896]{2,0,1:T(8,128)(2,1)} %bitcast.45, f32[48,176,256]{2,1,0:T(8,128)} %get-tuple-element.108, bf16[48,176,256]{2,1,0:T(8,128)(2,1)} %fusion.25), kind=kOutput, calls=%fused_computation.24 | convolution fusion | flops 3890675712 | bytes 72155136 | tf_op jit(solution)/shard_map/ecd,ecf->edf/dot_general | solution.py:48
  797.9 17.8 %gather_fusion.3 = bf16[2048,896]{1,0:T(8,128)(2,1)} fusion(bf16[8448,896]{1,0:T(8,128)(2,1)} %bitcast.7, s32[2048]{0:T(1024)S(1)} %copy-done.5), kind=kCustom, calls=%fused_computation.3 | custom fusion | bytes 7348224 | tf_op jit(solution)/shard_map/gather | solution.py:76
  820.8 5.1 multiply_reduce_fusion
  825.9 61.9 %all-to-all-done.3 = bf16[8,1056,896]{2,1,0:T(8,128)(2,1)} async-done(((bf16[8,1056,896]{2,1,0:T(8,128)(2,1)}), bf16[8,1056,896]{2,1,0:T(8,128)(2,1)}, u32[]{:S(2)}, u32[]{:S(2)}) %all-to-all-start.3) | async-done | bytes 15138848 | tf_op jit(solution)/shard_map/all_to_all | solution.py:61
  887.8 17.7 %gather_fusion.5 = bf16[2048,896]{1,0:T(8,128)(2,1)} fusion(bf16[8448,896]{1,0:T(8,128)(2,1)} %bitcast.17, s32[2048]{0:T(1024)S(1)} %copy-done.5), kind=kCustom, calls=%fused_computation.5 | custom fusion | bytes 7348224 | tf_op jit(solution)/shard_map/gather | solution.py:84
  905.5 5.3 bitcast_reduce_fusion
  (83 shorter events, 19.0 us)
Async XLA Ops:
  18.4 159.2 %copy-start.2 = (bf16[256,896]{1,0:T(8,128)(2,1)S(1)}, bf16[256,896]{1,0:T(8,128)(2,1)}, u32[]{:S(2)}) copy-start(bf16[256,896]{1,0:T(8,128)(2,1)} %param.9) | copy-start | bytes 1376260
  203.2 4.5 copy-start.6
  203.2 4.7 copy-start.3
  203.2 171.9 %all-to-all-start = ((bf16[8,1056,896]{2,1,0:T(8,128)(2,1)}), bf16[8,1056,896]{2,1,0:T(8,128)(2,1)}, u32[]{:S(2)}, u32[]{:S(2)}) async-start(bf16[8,1056,896]{2,1,0:T(8,128)(2,1)} %bitcast.53), calls=%async_computation | async-start | bytes 30277632 | tf_op jit(solution)/shard_map/all_to_all | solution.py:61
  207.8 38.5 %copy-start = (f32[256,8]{1,0:T(8,128)}, f32[256,8]{1,0:T(8,128)S(1)}, u32[]{:S(2)}) copy-start(f32[256,8]{1,0:T(8,128)S(1)} %copy.33) | copy-start | bytes 24580
  375.1 170.9 %all-to-all-start.2 = ((bf16[8,1056,896]{2,1,0:T(8,128)(2,1)}), bf16[8,1056,896]{2,1,0:T(8,128)(2,1)}, u32[]{:S(2)}, u32[]{:S(2)}) async-start(bf16[8,1056,896]{2,1,0:T(8,128)(2,1)} %bitcast.52), calls=%async_computation.2 | async-start | bytes 30277632 | tf_op jit(solution)/shard_map/all_to_all | solution.py:61
  546.0 171.1 %all-to-all-start.1 = ((bf16[8,1056,896]{2,1,0:T(8,128)(2,1)}), bf16[8,1056,896]{2,1,0:T(8,128)(2,1)}, u32[]{:S(2)}, u32[]{:S(2)}) async-start(bf16[8,1056,896]{2,1,0:T(8,128)(2,1)} %copy.41), calls=%async_computation.1 | async-start | bytes 30277632 | tf_op jit(solution)/shard_map/all_to_all | solution.py:61
  717.1 170.7 %all-to-all-start.3 = ((bf16[8,1056,896]{2,1,0:T(8,128)(2,1)}), bf16[8,1056,896]{2,1,0:T(8,128)(2,1)}, u32[]{:S(2)}, u32[]{:S(2)}) async-start(bf16[8,1056,896]{2,1,0:T(8,128)(2,1)} %copy.48), calls=%async_computation.3 | async-start | bytes 30277632 | tf_op jit(solution)/shard_map/all_to_all | solution.py:61
  770.6 27.3 %copy-start.5 = (s32[2048]{0:T(1024)S(1)}, s32[2048]{0:T(1024)}, u32[]{:S(2)}) copy-start(s32[2048]{0:T(1024)} %get-tuple-element.103) | copy-start | bytes 24580
  797.9 17.8 %copy-start.4 = (bf16[256,896]{1,0:T(8,128)(2,1)S(1)}, bf16[256,896]{1,0:T(8,128)(2,1)}, u32[]{:S(2)}) copy-start(bf16[256,896]{1,0:T(8,128)(2,1)} %param.15) | copy-start | bytes 1376260
  815.7 5.1 copy-start.1
where the time goes:
time: 917 us; the launch traced here: 911 us
  local copies, waits for them, and re-layouts  393 us (43%)
  waiting for transfers between devices  274 us (30%)
  matrix products  207 us (23%)
  starting transfers between devices  17.9 us (2%)
  other arithmetic  17.1 us (2%)
    all_to_all x4, waiting for transfers between devices, exchange(): return lax.all_to_all(buf, grp, 0, 0, tiled=True)  274 us
    gather x12, local copies, waits for them, and re-layouts, slot_positions(): first = jnp.searchsorted(es, es, side='left').astype(jnp.int32)  141 us
    all_to_all x2, local copies, waits for them, and re-layouts, exchange(): return lax.all_to_all(buf, grp, 0, 0, tiled=True)  49.3 us
    gather x1, local copies, waits for them, and re-layouts, local(): dsend = jnp.concatenate([do, zrow])[inv].reshape(nd, el * cap, d)  35.6 us
    dot_general x1, matrix products, expert_backward(): jnp.einsum('ecf,edf->ecd', dv, w3, preferred_element_type=jnp.float32)  27.6 us
    dot_general x1, matrix products, expert_backward(): gw3 = jnp.einsum('ecd,ecf->edf', xe, dv, preferred_element_type=jnp.float32)  27.3 us
    dot_general x1, matrix products, expert_backward(): gw2 = jnp.einsum('ecf,ecd->efd', a, doe, preferred_element_type=jnp.float32)  26 us
    gather x1, local copies, waits for them, and re-layouts, local(): send = jnp.concatenate([x, zrow])[inv // top].reshape(nd, el * cap, d)  25.5 us
  transfers between devices with their start and end apart: 4, of which 4 were waited for; matrix products, arithmetic and copies ran while one was open for 43% of the time, Pallas kernels for 0%

commit v1 on v0

v1 whole, which is shorter than its diff:
```python
import functools

import jax
import jax.numpy as jnp
from jax import lax
from jax.experimental import pallas as pl
from jax.experimental.pallas import tpu as pltpu
from jax.sharding import PartitionSpec as P

F32 = jnp.float32
BF16 = jnp.bfloat16
NP = 8
TOK = 256
CAP = 24
PAD = 32
GRP = 8
NROW = NP * CAP


def nt(a, b):
    return lax.dot_general(a, b, (((1,), (1,)), ((), ())), preferred_element_type=F32)


def nn(a, b):
    return lax.dot_general(a, b, (((1,), (0,)), ((), ())), preferred_element_type=F32)


def tn(a, b):
    return lax.dot_general(a, b, (((0,), (0,)), ((), ())), preferred_element_type=F32)


def onehot(rows, cap):
    n = rows.shape[0]
    it = lax.broadcasted_iota(jnp.int32, (cap, TOK), 0).astype(F32)
    return [jnp.broadcast_to(rows[k:k + 1], (cap, TOK)) == it for k in range(n)]


def kernel(ne, el, x_hbm, dy_hbm, rt_ref, gt_ref, w1_ref, w3_ref, w2_ref,
           y_hbm, dx_hbm, dg_ref, gw1_ref, gw3_ref, gw2_ref,
           xs, dys, xe_s, dye_s, o_s, d_s, yacc, dxacc, cm, gm, dgm, sem):
    s = pl.program_id(0)
    ng = el // GRP
    steps = pl.num_programs(0)
    e0 = (lax.axis_index('row') * 4 + lax.axis_index('col')) * el

    @pl.when(s == 0)
    def _():
        cx = pltpu.make_async_copy(x_hbm, xs, sem.at[0])
        cd = pltpu.make_async_copy(dy_hbm, dys, sem.at[1])
        cx.start()
        cd.start()
        o_s[...] = jnp.zeros_like(o_s)
        d_s[...] = jnp.zeros_like(d_s)
        yacc[...] = jnp.zeros_like(yacc)
        dxacc[...] = jnp.zeros_like(dxacc)
        tr = lax.broadcasted_iota(jnp.int32, (TOK, TOK), 0)
        tc = lax.broadcasted_iota(jnp.int32, (TOK, TOK), 1)
        tri = jnp.where(tr < tc, 1.0, 0.0).astype(BF16)
        ee = lax.broadcasted_iota(jnp.int32, (el, TOK), 0) + e0

        def prep(p, _):
            r = rt_ref[p]
            g = gt_ref[p]
            m = jnp.zeros((el, TOK), F32)
            gs = jnp.zeros((el, TOK), F32)
            for j in range(r.shape[0]):
                hit = jnp.broadcast_to(r[j:j + 1], (el, TOK)) == ee
                m = jnp.where(hit, 1.0, m)
                gs = jnp.where(hit, jnp.broadcast_to(g[j:j + 1], (el, TOK)), gs)
            rank = nn(m.astype(BF16), tri)
            cm[p] = jnp.where(m > 0.0, rank, -1.0)
            gm[p] = gs
            return 0

        lax.fori_loop(0, NP, prep, 0)
        cx.wait()
        cd.wait()

    def gather(g, i):
        base = pl.multiple_of(g * GRP, GRP)
        slot = lax.rem(g, 2)
        q = lax.rem(i, 4)

        def pair(src, dst):
            res = []
            for h in range(2):
                p = q * 2 + h
                oh = onehot(cm[p, pl.ds(base, GRP), :], CAP)
                oh = jnp.concatenate([jnp.where(m, 1.0, 0.0) for m in oh], axis=0).astype(BF16)
                res.append(nn(oh, src[p]))
            for k in range(GRP):
                blk = jnp.concatenate([r[k * CAP:(k + 1) * CAP] for r in res], axis=0)
                dst[slot, k, pl.ds(pl.multiple_of(q * 2 * CAP, 2 * CAP), 2 * CAP), :] = blk.astype(BF16)

        @pl.when(i < 4)
        def _():
            pair(xs, xe_s)

        @pl.when(i >= 4)
        def _():
            pair(dys, dye_s)

    def scatter(g, p):
        base = pl.multiple_of(g * GRP, GRP)
        slot = lax.rem(g, 2)
        oh = onehot(cm[p, pl.ds(base, GRP), :], PAD)
        gr = gm[p, pl.ds(base, GRP), :]
        g1 = gr.astype(BF16).astype(F32)
        r1 = gr - g1
        g2 = r1.astype(BF16).astype(F32)
        g3 = r1 - g2
        sl = pl.ds(pl.multiple_of(p * PAD, PAD), PAD)
        ob = jnp.concatenate([o_s[slot, k, sl, :] for k in range(GRP)], axis=0)
        db = jnp.concatenate([d_s[slot, k, sl, :] for k in range(GRP)], axis=0)

        def spread(part):
            return jnp.concatenate(
                [jnp.where(oh[k], jnp.broadcast_to(part[k:k + 1], (PAD, TOK)), 0.0) for k in range(GRP)],
                axis=0).astype(BF16)

        gs = jnp.concatenate([spread(g1), spread(g2), spread(g3)], axis=0)
        yacc[p] += tn(gs, jnp.concatenate([ob, ob, ob], axis=0))
        one = jnp.concatenate([jnp.where(m, 1.0, 0.0) for m in oh], axis=0).astype(BF16)
        dxacc[p] += tn(one, db)

    def core(g, i):
        slot = lax.rem(g, 2)
        e = g * GRP + i
        xe = xe_s[slot, i]
        dye = dye_s[slot, i]
        w13 = jnp.concatenate([w1_ref[0], w3_ref[0]], axis=1)
        w2 = w2_ref[0]
        ff = w2.shape[0]
        uv = nn(xe, w13).astype(BF16).astype(F32)
        u, v = uv[:, :ff], uv[:, ff:]
        sg = jax.nn.sigmoid(u)
        us = u * sg
        a = (us * v).astype(BF16)
        o = nn(a, w2).astype(BF16)
        of = o.astype(F32)
        dyf = dye.astype(F32)
        dgc = jnp.sum(dyf * of, axis=1, keepdims=True)
        it = lax.broadcasted_iota(jnp.int32, (CAP, TOK), 0).astype(F32)
        gcol = []
        for p in range(NP):
            m = jnp.broadcast_to(cm[p, pl.ds(e, 1), :], (CAP, TOK)) == it
            gb = jnp.broadcast_to(gm[p, pl.ds(e, 1), :], (CAP, TOK))
            gcol.append(jnp.sum(jnp.where(m, gb, 0.0), axis=1, keepdims=True))
            db = jnp.broadcast_to(dgc[p * CAP:(p + 1) * CAP], (CAP, TOK))
            dgm[p, pl.ds(e, 1), :] = jnp.sum(jnp.where(m, db, 0.0), axis=0, keepdims=True)
        do = (jnp.concatenate(gcol, axis=0) * dyf).astype(BF16)
        da = nt(do, w2)
        du = (da * v * sg * (1.0 + u * (1.0 - sg))).astype(BF16)
        dv = (da * u * sg).astype(BF16)
        duv = jnp.concatenate([du, dv], axis=1)
        dx = nt(duv, w13)
        gw2_ref[0] = tn(a, do)
        g13 = tn(xe, duv)
        gw1_ref[0] = g13[:, :ff]
        gw3_ref[0] = g13[:, ff:]
        zero = jnp.zeros((PAD - CAP, o.shape[1]), F32)
        for p in range(NP):
            rows = slice(p * CAP, (p + 1) * CAP)
            o_s[slot, i, p * PAD:(p + 1) * PAD, :] = jnp.concatenate([of[rows], zero], axis=0).astype(BF16)
            d_s[slot, i, p * PAD:(p + 1) * PAD, :] = jnp.concatenate([dx[rows], zero], axis=0).astype(BF16)

    t = s - GRP
    g = lax.div(t, GRP)
    i = lax.rem(s, GRP)

    @pl.when(s < ng * GRP)
    def _():
        gather(lax.div(s, GRP), i)

    @pl.when(jnp.logical_and(s >= GRP, s < GRP + el))
    def _():
        core(g, i)

    @pl.when(s >= 2 * GRP)
    def _():
        scatter(lax.div(s, GRP) - 2, i)

    @pl.when(s == steps - 1)
    def _():
        cy = pltpu.make_async_copy(yacc, y_hbm, sem.at[0])
        cd = pltpu.make_async_copy(dxacc, dx_hbm, sem.at[1])
        cy.start()
        cd.start()

        def fin(p, _):
            r = rt_ref[p]
            acc = jnp.zeros(r.shape, F32)
            for e in range(el):
                acc = acc + jnp.where(r == e + e0, jnp.broadcast_to(dgm[p, e:e + 1, :], r.shape), 0.0)
            dg_ref[p] = acc
            return 0

        lax.fori_loop(0, NP, fin, 0)
        cy.wait()
        cd.wait()


def solution(mesh):
    grp = ('row', 'col')
    tspec = P(('dp', 'row', 'col'), None)
    wspec = P(grp, None, None)
    gspec = P(('dp', 'row', 'col'), None, None)

    def local(x, ridx, gates, w1, w3, w2, dy):
        tok, d = x.shape
        top = ridx.shape[1]
        el, _, ff = w1.shape
        ne = el * NP
        xa = lax.all_gather(x, grp)
        dya = lax.all_gather(dy, grp)
        rt = lax.all_gather(ridx.T, grp)
        gt = lax.all_gather(gates.T, grp)
        steps = el + 2 * GRP

        def eidx(s):
            return (jnp.clip(s - GRP, 0, el - 1), 0, 0)

        wide = pl.BlockSpec((1, d, ff), eidx)
        tall = pl.BlockSpec((1, ff, d), eidx)
        anyspec = pl.BlockSpec(memory_space=pl.ANY)
        vm = pl.BlockSpec(memory_space=pltpu.VMEM)
        yp, dxp, dgp, gw1, gw3, gw2 = pl.pallas_call(
            functools.partial(kernel, ne, el),
            grid=(steps,),
            in_specs=[anyspec, anyspec, vm, vm, wide, wide, tall],
            out_specs=[anyspec, anyspec, vm, wide, wide, tall],
            out_shape=[
                jax.ShapeDtypeStruct((NP, tok, d), F32),
                jax.ShapeDtypeStruct((NP, tok, d), F32),
                jax.ShapeDtypeStruct((NP, top, tok), F32),
                jax.ShapeDtypeStruct((el, d, ff), F32),
                jax.ShapeDtypeStruct((el, d, ff), F32),
                jax.ShapeDtypeStruct((el, ff, d), F32),
            ],
            scratch_shapes=[
                pltpu.VMEM((NP, tok, d), BF16),
                pltpu.VMEM((NP, tok, d), BF16),
                pltpu.VMEM((2, GRP, NROW, d), BF16),
                pltpu.VMEM((2, GRP, NROW, d), BF16),
                pltpu.VMEM((2, GRP, NP * PAD, d), BF16),
                pltpu.VMEM((2, GRP, NP * PAD, d), BF16),
                pltpu.VMEM((NP, tok, d), F32),
                pltpu.VMEM((NP, tok, d), F32),
                pltpu.VMEM((NP, el, tok), F32),
                pltpu.VMEM((NP, el, tok), F32),
                pltpu.VMEM((NP, el, tok), F32),
                pltpu.SemaphoreType.DMA((2,)),
            ],
            compiler_params=pltpu.CompilerParams(
                dimension_semantics=('arbitrary',), vmem_limit_bytes=67_000_000),
            cost_estimate=pl.CostEstimate(flops=60_000_000_000, bytes_accessed=200_000_000, transcendentals=0),
        )(xa, dya, rt, gt, w1, w3, w2)
        y = lax.psum_scatter(yp, grp, scatter_dimension=0, tiled=False).astype(BF16)
        dx = lax.psum_scatter(dxp, grp, scatter_dimension=0, tiled=False).astype(BF16)
        dg = lax.psum_scatter(dgp, grp, scatter_dimension=0, tiled=False).T
        return y, dx, dg, gw1, gw3, gw2

    return jax.shard_map(local, mesh=mesh, in_specs=(tspec, tspec, tspec, wspec, wspec, wspec, tspec), out_specs=(tspec, tspec, tspec, gspec, gspec, gspec), check_vma=False)
```

time: 917 us -> 385 us (0.42)
  local copies, waits for them, and re-layouts: 393 us -> 0 us
  matrix products: 207 us -> 0 us
  Pallas kernels: 0 us -> 158 us
  waiting for transfers between devices: 274 us -> 182 us
  blocking collectives: 0 us -> 26.5 us
  starting transfers between devices: 17.9 us -> 0.19 us
  other arithmetic: 17.1 us -> 3.99 us
  between operations: 1.14 us -> 13.8 us
    all_to_all x4 -> x0, waiting for transfers between devices: 274 us -> none  [exchange(): return lax.all_to_all(buf, grp, 0, 0, tiled=True)]
    gather x17 -> x0, local copies, waits for them, and re-layouts: 250 us -> none  [the longest x12 141 us: slot_positions(): first = jnp.searchsorted(es, es, side='left').astype(jnp.int32)]
    dot_general x10 -> x0, matrix products: 207 us -> none  [the longest x1 27.6 us: expert_backward(): jnp.einsum('ecf,edf->ecd', dv, w3, preferred_element_type=jnp.float32)]
    pallas_call x0 -> x1, Pallas kernels: none -> 158 us  [local(): pl.pallas_call(functools.partial(kernel, ne, el), grid=(steps,), in_specs...]
    reduce_scatter x0 -> x3, waiting for transfers between devices: none -> 143 us  [the longest x1 59.1 us: local(): lax.psum_scatter(dxp, grp, scatter_dimension=0, tiled=False).astype(BF16)]
    all_to_all x2 -> x0, local copies, waits for them, and re-layouts: 49.3 us -> none  [exchange(): return lax.all_to_all(buf, grp, 0, 0, tiled=True)]
    transpose x4 -> x0, local copies, waits for them, and re-layouts: 40.4 us -> none  [the longest x2 25.3 us: from_experts(): buf.reshape(el, nd, cap, d).transpose(1, 0, 2, 3).reshape(nd, el * cap, d)]
    all_gather x0 -> x2, waiting for transfers between devices: none -> 37.2 us  [the longest x1 30.4 us: local(): dya = lax.all_gather(dy, grp)]
  transfers between devices with their start and end apart: 4 -> 5, of which waited for: 4 -> 5; matrix products, arithmetic and copies ran while one was open for 43% -> 1% of each run, Pallas kernels for 0% -> 0%
where the time goes in v1:
time: 385 us; the launch traced here: 384 us
  waiting for transfers between devices  182 us (47%)
  Pallas kernels  158 us (41%)
  blocking collectives  26.5 us (7%)
  between operations  13.8 us (4%)
  other arithmetic  3.99 us (1%)
    pallas_call x1, Pallas kernels, local(): pl.pallas_call(functools.partial(kernel, ne, el), grid=(steps,), in_specs...  158 us
    reduce_scatter x1, waiting for transfers between devices, local(): lax.psum_scatter(dxp, grp, scatter_dimension=0, tiled=False).astype(BF16)  59.1 us
    reduce_scatter x1, waiting for transfers between devices, local(): y = lax.psum_scatter(yp, grp, scatter_dimension=0, tiled=False).astype(BF16)  56.9 us
    all_gather x1, waiting for transfers between devices, local(): dya = lax.all_gather(dy, grp)  30.4 us
    reduce_scatter x1, waiting for transfers between devices, local(): dg = lax.psum_scatter(dgp, grp, scatter_dimension=0, tiled=False).T  26.6 us
    all_gather x1, blocking collectives, local(): rt = lax.all_gather(ridx.T, grp)  14.4 us
    all_gather x1, blocking collectives, local(): gt = lax.all_gather(gates.T, grp)  12.1 us
  transfers between devices with their start and end apart: 5, of which 5 were waited for; matrix products, arithmetic and copies ran while one was open for 1% of the time, Pallas kernels for 0%

profile of v1, /device:TPU:0, one launch (start us, length us, event | category | flops | bytes accessed | tf_op | source)
XLA Modules:
  0.0 384.4 jit_solution(9245301598617849408)
XLA Ops:
  7.2 0.0 all-gather.7.cloned.1.call-start
  7.2 0.7 all-gather.7.cloned.1.call-update
  7.9 0.0 all-gather.9.cloned.1.call-start
  7.9 0.7 all-gather.9.cloned.1.call-update
  8.6 0.0 reduce-scatter.4.cloned.1.call-start
  8.7 14.4 %all-gather.2 = s32[64,256]{1,0:T(8,128)} all-gather(s32[8,256]{1,0:T(8,128)} %bitcast.15), channel_id=4, replica_groups=mesh['dp'=1,'row'=2,'col'=4] {'row','col'}, dimensions={0}, use_global_device_ids=true | all-gather | bytes 73728 | tf_op jit(solution)/shard_map/all_gather | solution.py:216
  23.1 12.1 %all-gather.3 = f32[64,256]{1,0:T(8,128)} all-gather(f32[8,256]{1,0:T(8,128)} %bitcast.16), channel_id=5, replica_groups=mesh['dp'=1,'row'=2,'col'=4] {'row','col'}, dimensions={0}, use_global_device_ids=true | all-gather | bytes 73728 | tf_op jit(solution)/shard_map/all_gather | solution.py:217
  35.2 6.8 %all-gather.7.cloned.1.call-done = bf16[2048,896]{1,0:T(8,128)(2,1)} async-done(((bf16[256,896]{1,0:T(8,128)(2,1)}), bf16[2048,896]{1,0:T(8,128)(2,1)}) %all-gather.7.cloned.1.call-update) | async-done | bytes 3670032 | tf_op jit(solution)/shard_map/all_gather | solution.py:214
  42.0 30.4 %all-gather.9.cloned.1.call-done = bf16[2048,896]{1,0:T(8,128)(2,1)} async-done(((bf16[256,896]{1,0:T(8,128)(2,1)}), bf16[2048,896]{1,0:T(8,128)(2,1)}) %all-gather.9.cloned.1.call-update) | async-done | bytes 3670032 | tf_op jit(solution)/shard_map/all_gather | solution.py:215
  72.4 157.8 %shard_map.118 = (f32[8,256,896]{2,1,0:T(8,128)}, f32[8,256,896]{2,1,0:T(8,128)}, f32[8,8,256]{2,1,0:T(8,128)}, f32[48,896,256]{2,1,0:T(8,128)}, f32[48,896,256]{2,1,0:T(8,128)}, /*index=5*/f32[48,256,896]{2,1,0:T(8,128)}) custom-call(bf16[8,256,896]{2,1,0:T(8,128)(2,1)} %bitcast.17, bf16[8,256,896]{2,1,0:T(8,128)(2,1)} %bitcast.18, s32[8,8,256]{2,1,0:T(8,128)} %bitcast.13, ...), custom_call_target="tpu_custom_call" | custom-call | flops 60000002048 | bytes 200000000 | tf_op jit(solution)/shard_map/pallas_call | solution.py:227
  230.2 0.0 reduce-scatter.4.cloned.1.call-update
  230.2 0.0 reduce-scatter.6.cloned.1.call-start
  230.3 0.5 reduce-scatter.6.cloned.1.call-update
  230.8 0.0 reduce-scatter.8.cloned.1.call-start
  230.8 0.5 reduce-scatter.8.cloned.1.call-update
  231.4 56.9 %reduce-scatter.4.cloned.1.call-done = f32[1,256,896]{2,1,0:T(8,128)} async-done(((f32[8,256,896]{2,1,0:T(8,128)}), f32[1,256,896]{2,1,0:T(8,128)}) %reduce-scatter.4.cloned.1.call-update) | async-done | bytes 917520 | tf_op jit(solution)/shard_map/reduce_scatter | solution.py:258
  288.3 2.0 convert_bitcast_fusion.1
  290.3 59.1 %reduce-scatter.6.cloned.1.call-done = f32[1,256,896]{2,1,0:T(8,128)} async-done(((f32[8,256,896]{2,1,0:T(8,128)}), f32[1,256,896]{2,1,0:T(8,128)}) %reduce-scatter.6.cloned.1.call-update) | async-done | bytes 917520 | tf_op jit(solution)/shard_map/reduce_scatter | solution.py:259
  349.3 2.0 convert_bitcast_fusion
  351.3 26.6 %reduce-scatter.8.cloned.1.call-done = f32[1,8,256]{2,1,0:T(8,128)} async-done(((f32[8,8,256]{2,1,0:T(8,128)}), f32[1,8,256]{2,1,0:T(8,128)}) %reduce-scatter.8.cloned.1.call-update) | async-done | bytes 8208 | tf_op jit(solution)/shard_map/reduce_scatter | solution.py:260
Async XLA Ops:
  7.2 34.8 %all-gather.7.cloned.1.call-start = ((), (), s32[]{:S(2)}) async-start(), calls=%async_computation.6 | async-start | bytes 4128768 | tf_op jit(solution)/shard_map/all_gather | solution.py:214
  7.9 64.5 %all-gather.9.cloned.1.call-start = ((), (), s32[]{:S(2)}) async-start(), calls=%async_computation.7 | async-start | bytes 4128768 | tf_op jit(solution)/shard_map/all_gather | solution.py:215
  8.6 279.6 %reduce-scatter.4.cloned.1.call-start = ((), (), s32[]{:S(2)}) async-start(), calls=%async_computation.3 | async-start | bytes 8257536 | tf_op jit(solution)/shard_map/reduce_scatter | solution.py:258
  230.2 119.1 %reduce-scatter.6.cloned.1.call-start = ((), (), s32[]{:S(2)}) async-start(), calls=%async_computation.4 | async-start | bytes 8257536 | tf_op jit(solution)/shard_map/reduce_scatter | solution.py:259
  230.8 147.1 %reduce-scatter.8.cloned.1.call-start = ((), (), s32[]{:S(2)}) async-start(), calls=%async_computation.5 | async-start | bytes 73728 | tf_op jit(solution)/shard_map/reduce_scatter | solution.py:260
Sparse Core Ops, SparseCore 0:
  9.8 32.1 all-gather.6
  43.8 28.5 all-gather.8
  230.3 57.9 reduce-scatter.3
  291.5 57.8 reduce-scatter.5
  352.7 25.1 reduce-scatter.7

commit v2 on v0

v2 whole, which is shorter than its diff:
```python
import functools

import jax
import jax.numpy as jnp
from jax import lax
from jax.experimental import pallas as pl
from jax.experimental.pallas import tpu as pltpu
from jax.sharding import PartitionSpec as P

F32 = jnp.float32
BF16 = jnp.bfloat16
MESH = pl.DeviceIdType.MESH
NP = 8
TOK = 256
HALF = TOK // 2
CAP = 24
PAD = 32
GRP = 8
NROW = NP * CAP
NBUF = 4


def nt(a, b):
    return lax.dot_general(a, b, (((1,), (1,)), ((), ())), preferred_element_type=F32)


def nn(a, b):
    return lax.dot_general(a, b, (((1,), (0,)), ((), ())), preferred_element_type=F32)


def tn(a, b):
    return lax.dot_general(a, b, (((0,), (0,)), ((), ())), preferred_element_type=F32)


def onehot(rows, cap):
    n = rows.shape[0]
    it = lax.broadcasted_iota(jnp.int32, (cap, TOK), 0).astype(F32)
    return [jnp.broadcast_to(rows[k:k + 1], (cap, TOK)) == it for k in range(n)]


def ds(i, n):
    return pl.ds(pl.multiple_of(i * n, n), n)


def gather_pair(cm, g, q, src, store):
    res = []
    for h in range(2):
        p = q * 2 + h
        oh = onehot(cm[p, ds(g, GRP), :], CAP)
        oh = jnp.concatenate([jnp.where(m, 1.0, 0.0) for m in oh], axis=0).astype(BF16)
        res.append(nn(oh, src[p]))
    for k in range(GRP):
        blk = jnp.concatenate([r[k * CAP:(k + 1) * CAP] for r in res], axis=0)
        store(k, ds(q, 2 * CAP), blk.astype(BF16))


def gate_column(cm, gm, e):
    it = lax.broadcasted_iota(jnp.int32, (CAP, TOK), 0).astype(F32)
    cols = []
    for p in range(NP):
        m = jnp.broadcast_to(cm[p, pl.ds(e, 1), :], (CAP, TOK)) == it
        gb = jnp.broadcast_to(gm[p, pl.ds(e, 1), :], (CAP, TOK))
        cols.append(jnp.sum(jnp.where(m, gb, 0.0), axis=1, keepdims=True))
    return jnp.concatenate(cols, axis=0)


def main_kernel(el, x_hbm, dy_hbm, rg_ref, w1_hbm, w3_hbm, w2_hbm,
                y_ref, dx_ref, dg_ref, xa_hbm, dya_hbm, cm_hbm, gm_hbm, duv_hbm, a_hbm,
                xs, dys, rgs, xe_s, o_s, uv_s, a_s, yacc, dxacc, cm, gm, dgm, dgo, dgr,
                w1b, w3b, w2b, rd, r1, r2,
                wsem, lsem, osem, rg_ss, rg_rs, ag_ss, ag_rs, dd_ss, dd_rs, s1_ss, s1_rs, s2_ss, s2_rs, dg_ss, dg_rs):
    ng = el // GRP
    ff = w2b.shape[1]
    Z = lax.axis_index('dp')
    Y = lax.axis_index('row')
    col = lax.axis_index('col')
    X = lax.div(col, 2)
    C = lax.rem(col, 2)
    me = Y * 4 + col
    e0 = me * el

    def pos(fy, fx, fc):
        return (1 - Y if fy else Y), (1 - X if fx else X), (1 - C if fc else C)

    def blk(fy, fx, fc):
        yy, xx, cc = pos(fy, fx, fc)
        return yy * 4 + xx * 2 + cc

    def dev(fy, fx, fc):
        yy, xx, cc = pos(fy, fx, fc)
        return (Z, yy, xx * 2 + cc)

    peers = [(a, b, c) for a in range(2) for b in range(2) for c in range(2)][1:]

    def remote(src, dst, ss, rs, to):
        return pltpu.make_async_remote_copy(src_ref=src, dst_ref=dst, send_sem=ss, recv_sem=rs,
                                            device_id=dev(*to), device_id_type=MESH)

    lx = pltpu.make_async_copy(x_hbm, xs.at[me], lsem.at[0])
    ld = pltpu.make_async_copy(dy_hbm, dys.at[me], lsem.at[1])
    lx.start()
    ld.start()

    def wcopies(e):
        b = lax.rem(e, NBUF)
        k = lax.rem(e, el)
        return [pltpu.make_async_copy(h.at[k], v.at[b], wsem.at[n, b])
                for n, (h, v) in enumerate(((w1_hbm, w1b), (w3_hbm, w3b), (w2_hbm, w2b)))]

    for e in range(NBUF - 1):
        for c in wcopies(e):
            c.start()

    barrier = pltpu.get_barrier_semaphore()
    for to in peers:
        pl.semaphore_signal(barrier, inc=1, device_id=dev(*to), device_id_type=MESH)
    pl.semaphore_wait(barrier, len(peers))

    rgs[me] = rg_ref[...]
    rg_copies = [remote(rg_ref, rgs.at[me], rg_ss.at[n], rg_rs.at[n], to) for n, to in enumerate(peers)]
    for c in rg_copies:
        c.start()

    def half(buf, b, h):
        return buf.at[b, pl.ds(h * HALF, HALF), :]

    XN, YN, DN, PN = (0, 1, 0), (1, 0, 0), (1, 1, 0), (0, 0, 1)
    FIRST = [(0, (0, 0, 0), 0, XN), (1, (0, 0, 0), 1, YN), (2, (0, 0, 0), 1, XN), (3, (0, 0, 0), 0, YN)]
    OWN2 = [(6, (0, 0, 0), 0, PN), (7, (0, 0, 0), 1, PN)]
    FWD = [(4, XN, 0, YN), (5, YN, 1, XN)]
    ARR = {0: (XN, 0), 1: (YN, 1), 2: (XN, 1), 3: (YN, 0), 4: (DN, 0), 5: (DN, 1)}
    ONWARD = {0: 8, 1: 9, 2: 10, 3: 11, 4: 12, 5: 13}

    def ag_copy(t, buf, n, f, h, to):
        r = half(buf, blk(*f), h)
        return remote(r, r, ag_ss.at[t, n], ag_rs.at[t, n], to)

    def ag_recv(t, buf, n, f, h):
        r = half(buf, blk(*f), h)
        remote(r, r, ag_ss.at[t, n], ag_rs.at[t, n], PN).wait_recv()

    def ag_start(t, buf):
        for n, f, h, to in FIRST + OWN2:
            ag_copy(t, buf, n, f, h, to).start()

    def ag_relay(t, buf, ns):
        for n in ns:
            f, h = ARR[n]
            ag_recv(t, buf, n, f, h)
            if n < 2:
                k, ff_, hh, to = FWD[n]
                ag_copy(t, buf, k, ff_, hh, to).start()
            ag_copy(t, buf, ONWARD[n], f, h, PN).start()

    def ag_finish(t, buf):
        for n, h in ((6, 0), (7, 1)):
            ag_recv(t, buf, n, PN, h)
        for n, k in ONWARD.items():
            f, h = ARR[n]
            ag_recv(t, buf, k, (f[0], f[1], 1), h)

    def ag_drain(t, buf):
        for n, f, h, to in FIRST + OWN2 + FWD:
            ag_copy(t, buf, n, f, h, to).wait_send()
        for n, k in ONWARD.items():
            f, h = ARR[n]
            ag_copy(t, buf, k, f, h, PN).wait_send()

    lx.wait()
    ld.wait()
    ag_start(0, xs)

    def zero(p, _):
        yacc[p] = jnp.zeros(yacc.shape[1:], F32)
        dxacc[p] = jnp.zeros(dxacc.shape[1:], F32)
        return 0

    lax.fori_loop(0, NP, zero, 0)

    for n, to in enumerate(peers):
        remote(rgs.at[blk(*to)], rgs.at[blk(*to)], rg_ss.at[n], rg_rs.at[n], to).wait_recv()
    top = rgs.shape[1] // 2
    tr = lax.broadcasted_iota(jnp.int32, (TOK, TOK), 0)
    tc = lax.broadcasted_iota(jnp.int32, (TOK, TOK), 1)
    tri = jnp.where(tr < tc, 1.0, 0.0).astype(BF16)
    ee = (lax.broadcasted_iota(jnp.int32, (el, TOK), 0) + e0).astype(F32)

    def prep(p, _):
        rg = rgs[p]
        m = jnp.zeros((el, TOK), F32)
        gs = jnp.zeros((el, TOK), F32)
        for j in range(top):
            hit = jnp.broadcast_to(rg[j:j + 1], (el, TOK)) == ee
            m = jnp.where(hit, 1.0, m)
            gs = jnp.where(hit, jnp.broadcast_to(rg[top + j:top + j + 1], (el, TOK)), gs)
        rank = nn(m.astype(BF16), tri)
        cm[p] = jnp.where(m > 0.0, rank, -1.0)
        gm[p] = gs
        return 0

    lax.fori_loop(0, NP, prep, 0)

    ag_relay(0, xs, (0, 1, 2, 3))
    ag_start(1, dys)
    ag_relay(0, xs, (4, 5))
    ag_finish(0, xs)
    out_copies = [pltpu.make_async_copy(xs, xa_hbm, osem.at[0]),
                  pltpu.make_async_copy(cm, cm_hbm, osem.at[1]),
                  pltpu.make_async_copy(gm, gm_hbm, osem.at[2]),
                  pltpu.make_async_copy(dys, dya_hbm, osem.at[3])]
    for c in out_copies[:3]:
        c.start()

    def gather_all(g, src):
        def step(q, _):
            def store(k, rows, val):
                xe_s[k, rows, :] = val
            gather_pair(cm, g, q, src, store)
            return 0
        lax.fori_loop(0, NP // 2, step, 0)

    def put_rows(i, val):
        zero = jnp.zeros((PAD - CAP, val.shape[1]), F32)
        for p in range(NP):
            o_s[i, p * PAD:(p + 1) * PAD, :] = jnp.concatenate([val[p * CAP:(p + 1) * CAP], zero], axis=0).astype(BF16)

    def take_rows(p):
        return jnp.concatenate([o_s[k, ds(p, PAD), :] for k in range(GRP)], axis=0)

    def combine_y(g):
        def step(p, _):
            oh = onehot(cm[p, ds(g, GRP), :], PAD)
            gr = gm[p, ds(g, GRP), :]
            g1 = gr.astype(BF16).astype(F32)
            rest = gr - g1
            g2 = rest.astype(BF16).astype(F32)
            g3 = rest - g2
            ob = take_rows(p)

            def spread(part):
                return jnp.concatenate(
                    [jnp.where(oh[k], jnp.broadcast_to(part[k:k + 1], (PAD, TOK)), 0.0) for k in range(GRP)],
                    axis=0).astype(BF16)

            gs = jnp.concatenate([spread(g1), spread(g2), spread(g3)], axis=0)
            yacc[p] += tn(gs, jnp.concatenate([ob, ob, ob], axis=0))
            return 0
        lax.fori_loop(0, NP, step, 0)

    def combine_dx(g):
        def step(p, _):
            oh = onehot(cm[p, ds(g, GRP), :], PAD)
            one = jnp.concatenate([jnp.where(m, 1.0, 0.0) for m in oh], axis=0).astype(BF16)
            dxacc[p] += tn(one, take_rows(p))
            return 0
        lax.fori_loop(0, NP, step, 0)

    def weights(n):
        for c in wcopies(n):
            c.wait()

        @pl.when(n + NBUF - 1 < 2 * el)
        def _():
            for c in wcopies(n + NBUF - 1):
                c.start()
        b = lax.rem(n, NBUF)
        return jnp.concatenate([w1b[b], w3b[b]], axis=1), w2b[b]

    def act(uv):
        u, v = uv[:, :ff], uv[:, ff:]
        sg = jax.nn.sigmoid(u)
        return u, v, sg, (u * sg * v).astype(BF16)

    ORDER = [(1, 1), (0, 1), (1, 0), (0, 0)]
    S1 = [((1, 1), 0, XN), ((1, 1), 1, YN), ((0, 1), 0, XN), ((1, 0), 1, YN)]
    IN1 = [((1, 0), 0), ((0, 1), 1), ((0, 0), 0), ((0, 0), 1)]
    S2 = [YN, XN]

    def dd_copy(t, acc, n):
        fy, fx = ORDER[n]
        return remote(acc.at[blk(fy, fx, 1)], rd.at[t, n], dd_ss.at[t, n], dd_rs.at[t, n], PN)

    def s1_copy(t, acc, n):
        (fy, fx), h, to = S1[n]
        return remote(half(acc, blk(fy, fx, 0), h), r1.at[t, n], s1_ss.at[t, n], s1_rs.at[t, n], to)

    def s2_copy(t, acc, n):
        (fy, fx), h = IN1[n]
        return remote(half(acc, blk(fy, fx, 0), h), r2.at[t, n], s2_ss.at[t, n], s2_rs.at[t, n], S2[n])

    def rs_start(t, acc):
        for n in range(4):
            dd_copy(t, acc, n).start()

    def rs_mid1(t, acc):
        for n in range(4):
            dd_copy(t, acc, n).wait_recv()
            fy, fx = ORDER[n]
            acc[blk(fy, fx, 0)] += rd[t, n]
            for k in ((0, 1), (2,), (3,), ())[n]:
                s1_copy(t, acc, k).start()

    def rs_mid2(t, acc):
        for n in range(4):
            s1_copy(t, acc, n).wait_recv()
            (fy, fx), h = IN1[n]
            acc[blk(fy, fx, 0), h * HALF:(h + 1) * HALF, :] += r1[t, n]
            if n < 2:
                s2_copy(t, acc, n).start()

    def rs_fin(t, acc, out):
        for n in range(2):
            s2_copy(t, acc, n).wait_recv()
            rows = slice(n * HALF, (n + 1) * HALF)
            out[rows, :] = (acc[me, rows, :] + r2[t, n]).astype(BF16)

    def rs_drain(t, acc):
        for n in range(4):
            dd_copy(t, acc, n).wait_send()
            s1_copy(t, acc, n).wait_send()
        for n in range(2):
            s2_copy(t, acc, n).wait_send()

    def fwd_group(g, _):
        gather_all(g, xs)

        def fwd(i, _):
            n = g * GRP + i
            w13, w2 = weights(n)
            uv = nn(xe_s[i], w13).astype(BF16)
            uv_s[n] = uv
            a = act(uv.astype(F32))[3]
            put_rows(i, nn(a, w2))
            return 0

        lax.fori_loop(0, GRP, fwd, 0)
        combine_y(g)

        @pl.when(g == 0)
        def _():
            ag_relay(1, dys, (0, 1, 2, 3))

        @pl.when(g == 1)
        def _():
            ag_relay(1, dys, (4, 5))

        @pl.when(g == 2)
        def _():
            ag_finish(1, dys)
            out_copies[3].start()
        return 0

    lax.fori_loop(0, ng, fwd_group, 0)

    def duv_copy(g):
        return pltpu.make_async_copy(uv_s.at[ds(g, GRP)], duv_hbm.at[ds(g, GRP)], osem.at[4])

    def a_copy(g):
        return pltpu.make_async_copy(a_s.at[lax.rem(g, 2)], a_hbm.at[ds(g, GRP)], osem.at[5])

    def bwd_group(g, _):
        gather_all(g, dys)
        slot = lax.rem(g, 2)

        @pl.when(g == 0)
        def _():
            rs_start(0, yacc)

        def bwd(i, _):
            e = g * GRP + i
            w13, w2 = weights(el + e)
            u, v, sg, a = act(uv_s[e].astype(F32))
            a_s[slot, i] = a
            of = nn(a, w2).astype(BF16).astype(F32)
            dyf = xe_s[i].astype(F32)
            dgc = jnp.sum(dyf * of, axis=1, keepdims=True)
            it = lax.broadcasted_iota(jnp.int32, (CAP, TOK), 0).astype(F32)
            for p in range(NP):
                m = jnp.broadcast_to(cm[p, pl.ds(e, 1), :], (CAP, TOK)) == it
                db = jnp.broadcast_to(dgc[p * CAP:(p + 1) * CAP], (CAP, TOK))
                dgm[p, pl.ds(e, 1), :] = jnp.sum(jnp.where(m, db, 0.0), axis=0, keepdims=True)
            do = (gate_column(cm, gm, e) * dyf).astype(BF16)
            da = nt(do, w2)
            du = (da * v * sg * (1.0 + u * (1.0 - sg))).astype(BF16)
            dv = (da * u * sg).astype(BF16)
            duv = jnp.concatenate([du, dv], axis=1)
            uv_s[e] = duv
            put_rows(i, nt(duv, w13))
            return 0

        @pl.when(g > 0)
        def _():
            a_copy(g - 1).wait()
            duv_copy(g - 1).wait()

        lax.fori_loop(0, GRP, bwd, 0)
        a_copy(g).start()
        duv_copy(g).start()
        combine_dx(g)

        @pl.when(g == 1)
        def _():
            rs_mid1(0, yacc)

        @pl.when(g == ng - 1)
        def _():
            rs_mid2(0, yacc)
        return 0

    lax.fori_loop(0, ng, bwd_group, 0)

    def spread_dg(p, _):
        rg = rgs[p]
        acc = jnp.zeros((top, TOK), F32)
        for e in range(el):
            ef = (e0 + e).astype(F32)
            acc = acc + jnp.where(rg[:top] == ef, jnp.broadcast_to(dgm[p, e:e + 1, :], (top, TOK)), 0.0)
        dgo[p] = acc
        return 0

    lax.fori_loop(0, NP, spread_dg, 0)
    rs_start(1, dxacc)
    rs_fin(0, yacc, y_ref)
    dg_copies = [remote(dgo.at[blk(*to)], dgr.at[n], dg_ss.at[n], dg_rs.at[n], to) for n, to in enumerate(peers)]
    for c in dg_copies:
        c.start()
    rs_mid1(1, dxacc)
    rs_mid2(1, dxacc)
    total = dgo[me]
    for n, c in enumerate(dg_copies):
        c.wait_recv()
        total = total + dgr[n]
    dg_ref[...] = total
    rs_fin(1, dxacc, dx_ref)

    ag_drain(0, xs)
    ag_drain(1, dys)
    rs_drain(0, yacc)
    rs_drain(1, dxacc)
    for c in rg_copies + dg_copies:
        c.wait_send()
    for c in out_copies:
        c.wait()
    a_copy(ng - 1).wait()
    duv_copy(ng - 1).wait()


def grad_kernel(el, eb, xa_hbm, dya_hbm, cm, gm, a_ref, duv_ref, gw1_ref, gw3_ref, gw2_ref, xs, dys, xe_s, dye_s, sem):
    s = pl.program_id(0)
    per = GRP // eb
    ff = a_ref.shape[2]

    @pl.when(s == 0)
    def _():
        cx = pltpu.make_async_copy(xa_hbm, xs, sem.at[0])
        cd = pltpu.make_async_copy(dya_hbm, dys, sem.at[1])
        cx.start()
        cd.start()
        cx.wait()
        cd.wait()

    @pl.when(s < el // eb)
    def _():
        g = lax.div(s, per)
        slot = lax.rem(g, 2)
        for k in range(NP // 2 // per):
            q = lax.rem(s, per) * (NP // 2 // per) + k
            for src, dst in ((xs, xe_s), (dys, dye_s)):
                def store(j, rows, val):
                    dst[slot, j, rows, :] = val
                gather_pair(cm, g, q, src, store)

    @pl.when(s >= per)
    def _():
        t = s - per
        g = lax.div(t, per)
        slot = lax.rem(g, 2)
        for k in range(eb):
            i = lax.rem(t, per) * eb + k
            e = g * GRP + i
            do = (gate_column(cm, gm, e) * dye_s[slot, i].astype(F32)).astype(BF16)
            gw2_ref[k] = tn(a_ref[k], do)
            g13 = tn(xe_s[slot, i], duv_ref[k])
            gw1_ref[k] = g13[:, :ff]
            gw3_ref[k] = g13[:, ff:]


def solution(mesh):
    grp = ('row', 'col')
    tspec = P(('dp', 'row', 'col'), None)
    wspec = P(grp, None, None)
    gspec = P(('dp', 'row', 'col'), None, None)

    def local(x, ridx, gates, w1, w3, w2, dy):
        tok, d = x.shape
        top = ridx.shape[1]
        el, _, ff = w1.shape
        anyspec = pl.BlockSpec(memory_space=pl.ANY)
        vm = pl.BlockSpec(memory_space=pltpu.VMEM)
        sds = jax.ShapeDtypeStruct
        rg = jnp.concatenate([ridx.T.astype(F32), gates.T], axis=0)
        dma = pltpu.SemaphoreType.DMA
        y, dx, dg, xa, dya, cm, gm, duv, a = pl.pallas_call(
            functools.partial(main_kernel, el),
            in_specs=[anyspec, anyspec, vm, anyspec, anyspec, anyspec],
            out_specs=[vm, vm, vm] + [anyspec] * 6,
            out_shape=[
                sds((tok, d), BF16), sds((tok, d), BF16), sds((top, tok), F32),
                sds((NP, tok, d), BF16), sds((NP, tok, d), BF16),
                sds((NP, el, tok), F32), sds((NP, el, tok), F32),
                sds((el, NROW, 2 * ff), BF16), sds((el, NROW, ff), BF16),
            ],
            scratch_shapes=[
                pltpu.VMEM((NP, tok, d), BF16),
                pltpu.VMEM((NP, tok, d), BF16),
                pltpu.VMEM((NP, 2 * top, tok), F32),
                pltpu.VMEM((GRP, NROW, d), BF16),
                pltpu.VMEM((GRP, NP * PAD, d), BF16),
                pltpu.VMEM((el, NROW, 2 * ff), BF16),
                pltpu.VMEM((2, GRP, NROW, ff), BF16),
                pltpu.VMEM((NP, tok, d), F32),
                pltpu.VMEM((NP, tok, d), F32),
                pltpu.VMEM((NP, el, tok), F32),
                pltpu.VMEM((NP, el, tok), F32),
                pltpu.VMEM((NP, el, tok), F32),
                pltpu.VMEM((NP, top, tok), F32),
                pltpu.VMEM((NP - 1, top, tok), F32),
                pltpu.VMEM((NBUF, d, ff), BF16),
                pltpu.VMEM((NBUF, d, ff), BF16),
                pltpu.VMEM((NBUF, ff, d), BF16),
                pltpu.VMEM((2, 4, tok, d), F32),
                pltpu.VMEM((2, 4, tok // 2, d), F32),
                pltpu.VMEM((2, 2, tok // 2, d), F32),
                dma((3, NBUF)), dma((2,)), dma((6,)),
                dma((NP - 1,)), dma((NP - 1,)),
                dma((2, 14)), dma((2, 14)),
                dma((2, 4)), dma((2, 4)),
                dma((2, 4)), dma((2, 4)),
                dma((2, 2)), dma((2, 2)),
                dma((NP - 1,)), dma((NP - 1,)),
            ],
            compiler_params=pltpu.CompilerParams(
                collective_id=0, has_side_effects=True, vmem_limit_bytes=67_000_000),
            cost_estimate=pl.CostEstimate(flops=40_000_000_000, bytes_accessed=160_000_000, transcendentals=0),
        )(x, dy, rg, w1, w3, w2)

        eb = 2
        per = GRP // eb
        steps = el // eb + per

        def eidx(s):
            return (jnp.clip(s - per, 0, el // eb - 1), 0, 0)

        gw1, gw3, gw2 = pl.pallas_call(
            functools.partial(grad_kernel, el, eb),
            grid=(steps,),
            in_specs=[anyspec, anyspec, vm, vm, pl.BlockSpec((eb, NROW, ff), eidx), pl.BlockSpec((eb, NROW, 2 * ff), eidx)],
            out_specs=[pl.BlockSpec((eb, d, ff), eidx), pl.BlockSpec((eb, d, ff), eidx), pl.BlockSpec((eb, ff, d), eidx)],
            out_shape=[sds((el, d, ff), F32), sds((el, d, ff), F32), sds((el, ff, d), F32)],
            scratch_shapes=[
                pltpu.VMEM((NP, tok, d), BF16),
                pltpu.VMEM((NP, tok, d), BF16),
                pltpu.VMEM((2, GRP, NROW, d), BF16),
                pltpu.VMEM((2, GRP, NROW, d), BF16),
                pltpu.SemaphoreType.DMA((2,)),
            ],
            compiler_params=pltpu.CompilerParams(
                dimension_semantics=('arbitrary',), vmem_limit_bytes=60_000_000),
            cost_estimate=pl.CostEstimate(flops=20_000_000_000, bytes_accessed=150_000_000, transcendentals=0),
        )(xa, dya, cm, gm, a, duv)
        return y, dx, dg.T, gw1, gw3, gw2

    return jax.shard_map(local, mesh=mesh, in_specs=(tspec, tspec, tspec, wspec, wspec, wspec, tspec), out_specs=(tspec, tspec, tspec, gspec, gspec, gspec), check_vma=False)
```

time: 917 us -> 280 us (0.31)
  local copies, waits for them, and re-layouts: 393 us -> 2.15 us
  Pallas kernels: 0 us -> 275 us
  waiting for transfers between devices: 274 us -> 0 us
  matrix products: 207 us -> 0 us
  starting transfers between devices: 17.9 us -> 0 us
  other arithmetic: 17.1 us -> 2 us
    pallas_call x0 -> x2, Pallas kernels: none -> 275 us  [the longest x1 217 us: local(): pl.pallas_call(functools.partial(main_kernel, el), in_specs=[anyspec, any...]
    all_to_all x4 -> x0, waiting for transfers between devices: 274 us -> none  [exchange(): return lax.all_to_all(buf, grp, 0, 0, tiled=True)]
    gather x17 -> x0, local copies, waits for them, and re-layouts: 250 us -> none  [the longest x12 141 us: slot_positions(): first = jnp.searchsorted(es, es, side='left').astype(jnp.int32)]
    dot_general x10 -> x0, matrix products: 207 us -> none  [the longest x1 27.6 us: expert_backward(): jnp.einsum('ecf,edf->ecd', dv, w3, preferred_element_type=jnp.float32)]
    all_to_all x2 -> x0, local copies, waits for them, and re-layouts: 49.3 us -> none  [exchange(): return lax.all_to_all(buf, grp, 0, 0, tiled=True)]
    transpose x4 -> x0, local copies, waits for them, and re-layouts: 40.4 us -> none  [the longest x2 25.3 us: from_experts(): buf.reshape(el, nd, cap, d).transpose(1, 0, 2, 3).reshape(nd, el * cap, d)]
    convert_element_type x2 -> x0, local copies, waits for them, and re-layouts: 20.4 us -> none  [the longest x1 10.2 us: expert_forward(): jnp.einsum('ecf,efd->ecd', a, w2, preferred_element_type=jnp.float32)]
    all_to_all x4 -> x0, starting transfers between devices: 17.9 us -> none  [exchange(): return lax.all_to_all(buf, grp, 0, 0, tiled=True)]
  transfers between devices with their start and end apart: 4 -> 0, of which waited for: 4 -> 0; matrix products, arithmetic and copies ran while one was open for 43% -> 0% of each run, Pallas kernels for 0% -> 0%
where the time goes in v2:
time: 280 us
  Pallas kernels  275 us (98%)
    pallas_call x1, Pallas kernels, local(): pl.pallas_call(functools.partial(main_kernel, el), in_specs=[anyspec, any...  217 us
    pallas_call x1, Pallas kernels, local(): pl.pallas_call(functools.partial(grad_kernel, el, eb), grid=(steps,), in_...  57.6 us

profile of v2, /device:TPU:0, one launch (start us, length us, event | category | flops | bytes accessed | tf_op | source)
XLA Modules:
  0.0 279.8 jit_solution(2119125284102112171)
XLA Ops:
  0.6 0.7 convert_bitcast_fusion
  1.3 1.3 pad_maximum_fusion.rg_ref
  2.6 217.3 %shard_map.118 = (bf16[256,896]{1,0:T(8,128)(2,1)}, bf16[256,896]{1,0:T(8,128)(2,1)}, f32[8,256]{1,0:T(8,128)}, bf16[8,256,896]{2,1,0:T(8,128)(2,1)}, bf16[8,256...) custom-call(bf16[256,896]{1,0:T(8,128)(2,1)} %x_hbm.1, ...), custom_call_target="tpu_custom_call" | custom-call | flops 40000000000 | bytes 160000000 | tf_op jit(solution)/shard_map/pallas_call | solution.py:503
  220.0 0.0 copy-start.1
  220.0 0.0 copy-start
  220.0 0.0 copy-start.2
  220.0 57.6 %shard_map.119 = (f32[48,896,256]{2,1,0:T(8,128)}, f32[48,896,256]{2,1,0:T(8,128)}, f32[48,256,896]{2,1,0:T(8,128)}) custom-call(bf16[8,256,896]{2,1,0:T(8,128)(2,1)} %get-tuple-element.21.xa_hbm, bf16[8,256,896]{2,1,0:T(8,128)(2,1)} %get-tuple-element.22.dya_hbm, f32[8,48,256]{2,1,0:T(8,128)} %get-tuple-element.23.cm, f32[8,48,256]{2,1,0:T(8,128)} %get-tuple-element.24.gm, ...), custom_call_target="tpu_custom_call" | custom-call | flops 20000000000 | bytes 150000000 | tf_op jit(solution)/shard_map/pallas_call | solution.py:554
  277.6 0.0 copy-done.1
  277.6 0.8 copy.16
  278.4 0.0 copy-done
  278.4 0.8 copy.17
  279.2 0.0 copy-done.2
  279.2 0.6 copy.18
Async XLA Ops:
  220.0 57.7 %copy-start.1 = (bf16[256,896]{1,0:T(8,128)(2,1)S(1)}, bf16[256,896]{1,0:T(8,128)(2,1)}, u32[]{:S(2)}) copy-start(bf16[256,896]{1,0:T(8,128)(2,1)} %get-tuple-element.36) | copy-start | bytes 1376260
  220.0 58.4 %copy-start = (bf16[256,896]{1,0:T(8,128)(2,1)S(1)}, bf16[256,896]{1,0:T(8,128)(2,1)}, u32[]{:S(2)}) copy-start(bf16[256,896]{1,0:T(8,128)(2,1)} %get-tuple-element.37) | copy-start | bytes 1376260
  220.0 59.2 %copy-start.2 = (f32[8,256]{1,0:T(8,128)S(1)}, f32[8,256]{1,0:T(8,128)}, u32[]{:S(2)}) copy-start(f32[8,256]{1,0:T(8,128)} %get-tuple-element.20) | copy-start | bytes 24580

commit v3 on v2

--- a/solution.py
+++ b/solution.py
@@ -17,7 +17,9 @@
 PAD = 32
 GRP = 8
 NROW = NP * CAP
-NBUF = 4
+NBUF = 6
+PAIR = 2
+SPLIT = 24
 
 
 def nt(a, b):
@@ -65,10 +67,10 @@
 
 
 def main_kernel(el, x_hbm, dy_hbm, rg_ref, w1_hbm, w3_hbm, w2_hbm,
-                y_ref, dx_ref, dg_ref, xa_hbm, dya_hbm, cm_hbm, gm_hbm, duv_hbm, a_hbm,
+                y_ref, dg_ref, sx_hbm, sy_hbm, ka_hbm, kb_hbm, xa_hbm, dya_hbm, cm_hbm, gm_hbm, duv_hbm, a_hbm,
                 xs, dys, rgs, xe_s, o_s, uv_s, a_s, yacc, dxacc, cm, gm, dgm, dgo, dgr,
                 w1b, w3b, w2b, rd, r1, r2,
-                wsem, lsem, osem, rg_ss, rg_rs, ag_ss, ag_rs, dd_ss, dd_rs, s1_ss, s1_rs, s2_ss, s2_rs, dg_ss, dg_rs):
+                wsem, lsem, osem, psem, rg_ss, rg_rs, ag_ss, ag_rs, dd_ss, dd_rs, s1_ss, s1_rs, s2_ss, s2_rs, dg_ss, dg_rs):
     ng = el // GRP
     ff = w2b.shape[1]
     Z = lax.axis_index('dp')
@@ -107,7 +109,7 @@
         return [pltpu.make_async_copy(h.at[k], v.at[b], wsem.at[n, b])
                 for n, (h, v) in enumerate(((w1_hbm, w1b), (w3_hbm, w3b), (w2_hbm, w2b)))]
 
-    for e in range(NBUF - 1):
+    for e in range(NBUF - PAIR):
         for c in wcopies(e):
             c.start()
 
@@ -217,7 +219,7 @@
                 xe_s[k, rows, :] = val
             gather_pair(cm, g, q, src, store)
             return 0
-        lax.fori_loop(0, NP // 2, step, 0)
+        lax.fori_loop(0, NP // 2, step, 0, unroll=2)
 
     def put_rows(i, val):
         zero = jnp.zeros((PAD - CAP, val.shape[1]), F32)
@@ -245,7 +247,7 @@
             gs = jnp.concatenate([spread(g1), spread(g2), spread(g3)], axis=0)
             yacc[p] += tn(gs, jnp.concatenate([ob, ob, ob], axis=0))
             return 0
-        lax.fori_loop(0, NP, step, 0)
+        lax.fori_loop(0, NP, step, 0, unroll=2)
 
     def combine_dx(g):
         def step(p, _):
@@ -253,18 +255,20 @@
             one = jnp.concatenate([jnp.where(m, 1.0, 0.0) for m in oh], axis=0).astype(BF16)
             dxacc[p] += tn(one, take_rows(p))
             return 0
-        lax.fori_loop(0, NP, step, 0)
+        lax.fori_loop(0, NP, step, 0, unroll=2)
 
     def weights(n):
-        for c in wcopies(n):
-            c.wait()
-
-        @pl.when(n + NBUF - 1 < 2 * el)
-        def _():
-            for c in wcopies(n + NBUF - 1):
-                c.start()
-        b = lax.rem(n, NBUF)
-        return jnp.concatenate([w1b[b], w3b[b]], axis=1), w2b[b]
+        for k in range(PAIR):
+            for c in wcopies(n + k):
+                c.wait()
+
+        @pl.when(n + NBUF - PAIR < 2 * el)
+        def _():
+            for k in range(PAIR):
+                for c in wcopies(n + NBUF - PAIR + k):
+                    c.start()
+        bufs = [lax.rem(n + k, NBUF) for k in range(PAIR)]
+        return [(jnp.concatenate([w1b[b], w3b[b]], axis=1), w2b[b]) for b in bufs]
 
     def act(uv):
         u, v = uv[:, :ff], uv[:, ff:]
@@ -324,16 +328,17 @@
     def fwd_group(g, _):
         gather_all(g, xs)
 
-        def fwd(i, _):
-            n = g * GRP + i
-            w13, w2 = weights(n)
-            uv = nn(xe_s[i], w13).astype(BF16)
-            uv_s[n] = uv
-            a = act(uv.astype(F32))[3]
-            put_rows(i, nn(a, w2))
+        def fwd(r, _):
+            n = g * GRP + r * PAIR
+            for k, (w13, w2) in enumerate(weights(n)):
+                i = r * PAIR + k
+                uv = nn(xe_s[i], w13).astype(BF16)
+                uv_s[n + k] = uv
+                a = act(uv.astype(F32))[3]
+                put_rows(i, nn(a, w2))
             return 0
 
-        lax.fori_loop(0, GRP, fwd, 0)
+        lax.fori_loop(0, GRP // PAIR, fwd, 0)
         combine_y(g)
 
         @pl.when(g == 0)
@@ -366,26 +371,28 @@
         def _():
             rs_start(0, yacc)
 
-        def bwd(i, _):
-            e = g * GRP + i
-            w13, w2 = weights(el + e)
-            u, v, sg, a = act(uv_s[e].astype(F32))
-            a_s[slot, i] = a
-            of = nn(a, w2).astype(BF16).astype(F32)
-            dyf = xe_s[i].astype(F32)
-            dgc = jnp.sum(dyf * of, axis=1, keepdims=True)
-            it = lax.broadcasted_iota(jnp.int32, (CAP, TOK), 0).astype(F32)
-            for p in range(NP):
-                m = jnp.broadcast_to(cm[p, pl.ds(e, 1), :], (CAP, TOK)) == it
-                db = jnp.broadcast_to(dgc[p * CAP:(p + 1) * CAP], (CAP, TOK))
-                dgm[p, pl.ds(e, 1), :] = jnp.sum(jnp.where(m, db, 0.0), axis=0, keepdims=True)
-            do = (gate_column(cm, gm, e) * dyf).astype(BF16)
-            da = nt(do, w2)
-            du = (da * v * sg * (1.0 + u * (1.0 - sg))).astype(BF16)
-            dv = (da * u * sg).astype(BF16)
-            duv = jnp.concatenate([du, dv], axis=1)
-            uv_s[e] = duv
-            put_rows(i, nt(duv, w13))
+        def bwd(r, _):
+            n = g * GRP + r * PAIR
+            for k, (w13, w2) in enumerate(weights(el + n)):
+                i = r * PAIR + k
+                e = n + k
+                u, v, sg, a = act(uv_s[e].astype(F32))
+                a_s[slot, i] = a
+                of = nn(a, w2).astype(BF16).astype(F32)
+                dyf = xe_s[i].astype(F32)
+                dgc = jnp.sum(dyf * of, axis=1, keepdims=True)
+                it = lax.broadcasted_iota(jnp.int32, (CAP, TOK), 0).astype(F32)
+                for p in range(NP):
+                    m = jnp.broadcast_to(cm[p, pl.ds(e, 1), :], (CAP, TOK)) == it
+                    db = jnp.broadcast_to(dgc[p * CAP:(p + 1) * CAP], (CAP, TOK))
+                    dgm[p, pl.ds(e, 1), :] = jnp.sum(jnp.where(m, db, 0.0), axis=0, keepdims=True)
+                do = (gate_column(cm, gm, e) * dyf).astype(BF16)
+                da = nt(do, w2)
+                du = (da * v * sg * (1.0 + u * (1.0 - sg))).astype(BF16)
+                dv = (da * u * sg).astype(BF16)
+                duv = jnp.concatenate([du, dv], axis=1)
+                uv_s[e] = duv
+                put_rows(i, nt(duv, w13))
             return 0
 
         @pl.when(g > 0)
@@ -393,7 +400,7 @@
             a_copy(g - 1).wait()
             duv_copy(g - 1).wait()
 
-        lax.fori_loop(0, GRP, bwd, 0)
+        lax.fori_loop(0, GRP // PAIR, bwd, 0)
         a_copy(g).start()
         duv_copy(g).start()
         combine_dx(g)
@@ -424,19 +431,31 @@
     dg_copies = [remote(dgo.at[blk(*to)], dgr.at[n], dg_ss.at[n], dg_rs.at[n], to) for n, to in enumerate(peers)]
     for c in dg_copies:
         c.start()
-    rs_mid1(1, dxacc)
-    rs_mid2(1, dxacc)
+    part_copies = []
+    for n in range(4):
+        dd_copy(1, dxacc, n).wait_recv()
+        fy, fx = ORDER[n]
+        b = blk(fy, fx, 0)
+        dxacc[b] += rd[1, n]
+        to_b = (sy_hbm.at[0], kb_hbm.at[0], sy_hbm.at[1], kb_hbm.at[1])[n]
+        to_a = (sx_hbm.at[0], sx_hbm.at[1], ka_hbm.at[0], ka_hbm.at[1])[n]
+        for h, to in enumerate((to_a, to_b)):
+            c = pltpu.make_async_copy(half(dxacc, b, h), to, psem.at[n, h])
+            c.start()
+            part_copies.append(c)
     total = dgo[me]
     for n, c in enumerate(dg_copies):
         c.wait_recv()
         total = total + dgr[n]
     dg_ref[...] = total
-    rs_fin(1, dxacc, dx_ref)
 
     ag_drain(0, xs)
     ag_drain(1, dys)
     rs_drain(0, yacc)
-    rs_drain(1, dxacc)
+    for n in range(4):
+        dd_copy(1, dxacc, n).wait_send()
+    for c in part_copies:
+        c.wait()
     for c in rg_copies + dg_copies:
         c.wait_send()
     for c in out_copies:
@@ -445,7 +464,8 @@
     duv_copy(ng - 1).wait()
 
 
-def grad_kernel(el, eb, xa_hbm, dya_hbm, cm, gm, a_ref, duv_ref, gw1_ref, gw3_ref, gw2_ref, xs, dys, xe_s, dye_s, sem):
+def grad_kernel(first, count, eb, nprev, xa_hbm, dya_hbm, cm, gm, a_ref, duv_ref, *refs):
+    gw1_ref, gw3_ref, gw2_ref, xs, dys, xe_s, dye_s, sem = refs[nprev:]
     s = pl.program_id(0)
     per = GRP // eb
     ff = a_ref.shape[2]
@@ -459,7 +479,7 @@
         cx.wait()
         cd.wait()
 
-    @pl.when(s < el // eb)
+    @pl.when(s < count // eb)
     def _():
         g = lax.div(s, per)
         slot = lax.rem(g, 2)
@@ -468,7 +488,7 @@
             for src, dst in ((xs, xe_s), (dys, dye_s)):
                 def store(j, rows, val):
                     dst[slot, j, rows, :] = val
-                gather_pair(cm, g, q, src, store)
+                gather_pair(cm, first // GRP + g, q, src, store)
 
     @pl.when(s >= per)
     def _():
@@ -477,7 +497,7 @@
         slot = lax.rem(g, 2)
         for k in range(eb):
             i = lax.rem(t, per) * eb + k
-            e = g * GRP + i
+            e = first + g * GRP + i
             do = (gate_column(cm, gm, e) * dye_s[slot, i].astype(F32)).astype(BF16)
             gw2_ref[k] = tn(a_ref[k], do)
             g13 = tn(xe_s[slot, i], duv_ref[k])
@@ -500,12 +520,12 @@
         sds = jax.ShapeDtypeStruct
         rg = jnp.concatenate([ridx.T.astype(F32), gates.T], axis=0)
         dma = pltpu.SemaphoreType.DMA
-        y, dx, dg, xa, dya, cm, gm, duv, a = pl.pallas_call(
+        y, dg, sx, sy, ka, kb, xa, dya, cm, gm, duv, a = pl.pallas_call(
             functools.partial(main_kernel, el),
             in_specs=[anyspec, anyspec, vm, anyspec, anyspec, anyspec],
-            out_specs=[vm, vm, vm] + [anyspec] * 6,
+            out_specs=[vm, vm] + [anyspec] * 10,
             out_shape=[
-                sds((tok, d), BF16), sds((tok, d), BF16), sds((top, tok), F32),
+                sds((tok, d), BF16), sds((top, tok), F32)] + [sds((2, tok // 2, d), F32)] * 4 + [
                 sds((NP, tok, d), BF16), sds((NP, tok, d), BF16),
                 sds((NP, el, tok), F32), sds((NP, el, tok), F32),
                 sds((el, NROW, 2 * ff), BF16), sds((el, NROW, ff), BF16),
@@ -529,14 +549,14 @@
                 pltpu.VMEM((NBUF, d, ff), BF16),
                 pltpu.VMEM((NBUF, ff, d), BF16),
                 pltpu.VMEM((2, 4, tok, d), F32),
-                pltpu.VMEM((2, 4, tok // 2, d), F32),
-                pltpu.VMEM((2, 2, tok // 2, d), F32),
-                dma((3, NBUF)), dma((2,)), dma((6,)),
+                pltpu.VMEM((1, 4, tok // 2, d), F32),
+                pltpu.VMEM((1, 2, tok // 2, d), F32),
+                dma((3, NBUF)), dma((2,)), dma((6,)), dma((4, 2)),
                 dma((NP - 1,)), dma((NP - 1,)),
                 dma((2, 14)), dma((2, 14)),
                 dma((2, 4)), dma((2, 4)),
-                dma((2, 4)), dma((2, 4)),
-                dma((2, 2)), dma((2, 2)),
+                dma((1, 4)), dma((1, 4)),
+                dma((1, 2)), dma((1, 2)),
                 dma((NP - 1,)), dma((NP - 1,)),
             ],
             compiler_params=pltpu.CompilerParams(
@@ -544,30 +564,49 @@
             cost_estimate=pl.CostEstimate(flops=40_000_000_000, bytes_accessed=160_000_000, transcendentals=0),
         )(x, dy, rg, w1, w3, w2)
 
+        def perm(fy, fx):
+            out = []
+            for p in range(NP):
+                yy, xx, cc = p // 4, (p // 2) % 2, p % 2
+                out.append((p, (yy ^ fy) * 4 + (xx ^ fx) * 2 + cc))
+            return out
+
         eb = 2
         per = GRP // eb
-        steps = el // eb + per
-
-        def eidx(s):
-            return (jnp.clip(s - per, 0, el // eb - 1), 0, 0)
-
-        gw1, gw3, gw2 = pl.pallas_call(
-            functools.partial(grad_kernel, el, eb),
-            grid=(steps,),
-            in_specs=[anyspec, anyspec, vm, vm, pl.BlockSpec((eb, NROW, ff), eidx), pl.BlockSpec((eb, NROW, 2 * ff), eidx)],
-            out_specs=[pl.BlockSpec((eb, d, ff), eidx), pl.BlockSpec((eb, d, ff), eidx), pl.BlockSpec((eb, ff, d), eidx)],
-            out_shape=[sds((el, d, ff), F32), sds((el, d, ff), F32), sds((el, ff, d), F32)],
-            scratch_shapes=[
-                pltpu.VMEM((NP, tok, d), BF16),
-                pltpu.VMEM((NP, tok, d), BF16),
-                pltpu.VMEM((2, GRP, NROW, d), BF16),
-                pltpu.VMEM((2, GRP, NROW, d), BF16),
-                pltpu.SemaphoreType.DMA((2,)),
-            ],
-            compiler_params=pltpu.CompilerParams(
-                dimension_semantics=('arbitrary',), vmem_limit_bytes=60_000_000),
-            cost_estimate=pl.CostEstimate(flops=20_000_000_000, bytes_accessed=150_000_000, transcendentals=0),
-        )(xa, dya, cm, gm, a, duv)
+
+        def grads(first, count, prev):
+            steps = count // eb + per
+
+            def eidx(s):
+                return (first // eb + jnp.clip(s - per, 0, count // eb - 1), 0, 0)
+
+            return pl.pallas_call(
+                functools.partial(grad_kernel, first, count, eb, len(prev)),
+                grid=(steps,),
+                in_specs=[anyspec, anyspec, vm, vm, pl.BlockSpec((eb, NROW, ff), eidx), pl.BlockSpec((eb, NROW, 2 * ff), eidx)] + [anyspec] * len(prev),
+                out_specs=[pl.BlockSpec((eb, d, ff), eidx), pl.BlockSpec((eb, d, ff), eidx), pl.BlockSpec((eb, ff, d), eidx)],
+                out_shape=[sds((el, d, ff), F32), sds((el, d, ff), F32), sds((el, ff, d), F32)],
+                input_output_aliases={6 + k: k for k in range(len(prev))},
+                scratch_shapes=[
+                    pltpu.VMEM((NP, tok, d), BF16),
+                    pltpu.VMEM((NP, tok, d), BF16),
+                    pltpu.VMEM((2, GRP, NROW, d), BF16),
+                    pltpu.VMEM((2, GRP, NROW, d), BF16),
+                    pltpu.SemaphoreType.DMA((2,)),
+                ],
+                compiler_params=pltpu.CompilerParams(
+                    dimension_semantics=('arbitrary',), vmem_limit_bytes=60_000_000),
+                cost_estimate=pl.CostEstimate(flops=20_000_000_000 * count // el, bytes_accessed=150_000_000 * count // el, transcendentals=0),
+            )(xa, dya, cm, gm, a, duv, *prev)
+
+        r1x = lax.ppermute(sx, grp, perm(0, 1))
+        r1y = lax.ppermute(sy, grp, perm(1, 0))
+        prev = grads(0, SPLIT, ())
+        prev, r1x, r1y = lax.optimization_barrier((prev, r1x, r1y))
+        r2a = lax.ppermute(ka[0] + r1x[0], grp, perm(1, 0))
+        r2b = lax.ppermute(kb[0] + r1y[0], grp, perm(0, 1))
+        gw1, gw3, gw2 = grads(SPLIT, el - SPLIT, tuple(prev))
+        dx = jnp.concatenate([ka[1] + r1x[1] + r2a, kb[1] + r1y[1] + r2b], axis=0).astype(BF16)
         return y, dx, dg.T, gw1, gw3, gw2
 
     return jax.shard_map(local, mesh=mesh, in_specs=(tspec, tspec, tspec, wspec, wspec, wspec, tspec), out_specs=(tspec, tspec, tspec, gspec, gspec, gspec), check_vma=False)

time: 280 us -> 241 us (0.86)
  Pallas kernels: 275 us -> 232 us
  starting transfers between devices: 0 us -> 4.12 us
    pallas_call x1, Pallas kernels: 217 us -> 166 us  [local(): pl.pallas_call(functools.partial(main_kernel, el), in_specs=[anyspec, any...]
    pallas_call x1 -> x2, Pallas kernels: 57.6 us -> 65.2 us  [grads(): pl.pallas_call(functools.partial(grad_kernel, first, count, eb, len(prev)...]
    ppermute x0 -> x4, starting transfers between devices: none -> 4.12 us  [the longest x1 1.15 us: local(): r2a = lax.ppermute(ka[0] + r1x[0], grp, perm(1, 0))]
  transfers between devices with their start and end apart: 0 -> 4, of which waited for: 0 -> 0; matrix products, arithmetic and copies ran while one was open for 0% -> 0% of each run, Pallas kernels for 0% -> 27%
where the time goes in v3:
time: 241 us
  Pallas kernels  232 us (96%)
  starting transfers between devices  4.12 us (2%)
  other arithmetic  3.04 us (1%)
    pallas_call x1, Pallas kernels, local(): pl.pallas_call(functools.partial(main_kernel, el), in_specs=[anyspec, any...  166 us
    pallas_call x2, Pallas kernels, grads(): pl.pallas_call(functools.partial(grad_kernel, first, count, eb, len(prev)...  65.2 us
  transfers between devices with their start and end apart: 4, of which 0 were waited for; matrix products, arithmetic and copies ran while one was open for 0% of the time, Pallas kernels for 27%

profile of v3, /device:TPU:0, one launch (start us, length us, event | category | flops | bytes accessed | tf_op | source)
XLA Modules:
  0.0 240.9 jit_solution(15317127006812422001)
XLA Ops:
  0.6 0.7 convert_bitcast_fusion
  1.3 1.3 pad_maximum_fusion.1.rg_ref
  2.6 166.4 %shard_map.118 = (bf16[256,896]{1,0:T(8,128)(2,1)}, f32[8,256]{1,0:T(8,128)}, f32[2,128,896]{2,1,0:T(8,128)}, f32[2,128,896]{2,1,0:T(8,128)}, f32[2,128,896]{2,1...) custom-call(bf16[256,896]{1,0:T(8,128)(2,1)} %x_hbm.1, ...), custom_call_target="tpu_custom_call" | custom-call | flops 40000000000 | bytes 160000000 | tf_op jit(solution)/shard_map/pallas_call | solution.py:523
  169.0 0.0 copy-start.1
  169.1 0.0 copy-start
  169.1 0.9 collective-permute-start
  170.0 1.1 collective-permute-start.1
  171.1 32.6 %shard_map.119 = (f32[48,896,256]{2,1,0:T(8,128)}, f32[48,896,256]{2,1,0:T(8,128)}, f32[48,256,896]{2,1,0:T(8,128)}) custom-call(bf16[8,256,896]{2,1,0:T(8,128)(2,1)} %get-tuple-element.31.xa_hbm, bf16[8,256,896]{2,1,0:T(8,128)(2,1)} %get-tuple-element.32.dya_hbm, f32[8,48,256]{2,1,0:T(8,128)} %get-tuple-element.33.cm, f32[8,48,256]{2,1,0:T(8,128)} %get-tuple-element.34.gm, ...), custom_call_target="tpu_custom_call" | custom-call | flops 10000000000 | bytes 75000000 | tf_op jit(solution)/shard_map/pallas_call | solution.py:583
  203.7 0.0 collective-permute-done
  203.7 0.0 collective-permute-done.1
  203.7 0.0 copy-done.1
  203.8 0.9 collective-permute-start.3
  204.7 0.0 copy-done
  204.8 0.0 copy-start.2
  204.8 0.0 copy-start.3
  204.8 1.2 collective-permute-start.2
  205.9 32.6 %shard_map.120 = (f32[48,896,256]{2,1,0:T(8,128)}, f32[48,896,256]{2,1,0:T(8,128)}, f32[48,256,896]{2,1,0:T(8,128)}) custom-call(bf16[8,256,896]{2,1,0:T(8,128)(2,1)} %get-tuple-element.31.xa_hbm, bf16[8,256,896]{2,1,0:T(8,128)(2,1)} %get-tuple-element.32.dya_hbm, ...), custom_call_target="tpu_custom_call", output_to_operand_aliasing={{0}: (6, {}), {1}: (7, {}), {2}: (8, {})} | custom-call | flops 10000000000 | bytes 75000000 | tf_op jit(solution)/shard_map/pallas_call | solution.py:583
  238.6 0.0 collective-permute-done.3
  238.6 0.1 fusion
  238.7 0.0 collective-permute-done.2
  238.7 0.1 fusion.1
  238.8 0.8 pad_maximum_fusion
  239.6 0.0 copy-done.2
  239.6 0.8 copy.21
  240.3 0.0 copy-done.3
  240.3 0.6 copy.22
  (2 shorter events, 0.1 us)
Async XLA Ops:
  169.0 34.7 %copy-start.1 = (f32[2,128,896]{2,1,0:T(8,128)S(1)}, f32[2,128,896]{2,1,0:T(8,128)}, u32[]{:S(2)}) copy-start(f32[2,128,896]{2,1,0:T(8,128)} %get-tuple-element.43) | copy-start | bytes 2752516
  169.1 35.7 %copy-start = (f32[2,128,896]{2,1,0:T(8,128)S(1)}, f32[2,128,896]{2,1,0:T(8,128)}, u32[]{:S(2)}) copy-start(f32[2,128,896]{2,1,0:T(8,128)} %get-tuple-element.30) | copy-start | bytes 2752516
  169.1 34.6 %collective-permute-start = (f32[2,128,896]{2,1,0:T(8,128)}, f32[2,128,896]{2,1,0:T(8,128)S(1)}, u32[]{:S(2)}, u32[]{:S(2)}) collective-permute-start(f32[2,128,896]{2,1,0:T(8,128)} %get-tuple-element.40), channel_id=1, source_target_pairs={{0,2},{1,3},{2,0},{3,1},{4,6},{5,7},{6,4},{7,5}} | collective-permute-start | bytes 2752520 | tf_op jit(solution)/shard_map/ppermute | solution.py:602
  170.0 33.7 %collective-permute-start.1 = (f32[2,128,896]{2,1,0:T(8,128)}, f32[2,128,896]{2,1,0:T(8,128)S(1)}, u32[]{:S(2)}, u32[]{:S(2)}) collective-permute-start(f32[2,128,896]{2,1,0:T(8,128)} %get-tuple-element.41), channel_id=1, source_target_pairs={{0,4},{1,5},{2,6},{3,7},{4,0},{5,1},{6,2},{7,3}} | collective-permute-start | bytes 2752520 | tf_op jit(solution)/shard_map/ppermute | solution.py:603
  203.8 34.8 %collective-permute-start.3 = (f32[128,896]{1,0:T(8,128)S(1)}, f32[128,896]{1,0:T(8,128)S(1)}, u32[]{:S(2)}, u32[]{:S(2)}) collective-permute-start(f32[128,896]{1,0:T(8,128)S(1)} %add_bitcast_fusion), channel_id=1, source_target_pairs={{0,2},{1,3},{2,0},{3,1},{4,6},{5,7},{6,4},{7,5}} | collective-permute-start | bytes 1376264 | tf_op jit(solution)/shard_map/ppermute | solution.py:607
  204.8 34.8 %copy-start.2 = (bf16[256,896]{1,0:T(8,128)(2,1)S(1)}, bf16[256,896]{1,0:T(8,128)(2,1)}, u32[]{:S(2)}) copy-start(bf16[256,896]{1,0:T(8,128)(2,1)} %get-tuple-element.58) | copy-start | bytes 1376260
  204.8 35.5 %copy-start.3 = (f32[8,256]{1,0:T(8,128)S(1)}, f32[8,256]{1,0:T(8,128)}, u32[]{:S(2)}) copy-start(f32[8,256]{1,0:T(8,128)} %get-tuple-element.45) | copy-start | bytes 24580
  204.8 33.9 %collective-permute-start.2 = (f32[128,896]{1,0:T(8,128)S(1)}, f32[128,896]{1,0:T(8,128)S(1)}, u32[]{:S(2)}, u32[]{:S(2)}) collective-permute-start(f32[128,896]{1,0:T(8,128)S(1)} %add_bitcast_fusion.1), channel_id=1, source_target_pairs={{0,4},{1,5},{2,6},{3,7},{4,0},{5,1},{6,2},{7,3}} | collective-permute-start | bytes 1376264 | tf_op jit(solution)/shard_map/ppermute | solution.py:606

commit v4 on v3

--- a/solution.py
+++ b/solution.py
@@ -17,7 +17,7 @@
 PAD = 32
 GRP = 8
 NROW = NP * CAP
-NBUF = 6
+NBUF = 8
 PAIR = 2
 SPLIT = 24
 
@@ -56,6 +56,25 @@
         store(k, ds(q, 2 * CAP), blk.astype(BF16))
 
 
+def gather_dy_pair(cm, gm, g, q, src, store, store_scaled):
+    res, scaled = [], []
+    for h in range(2):
+        p = q * 2 + h
+        oh = onehot(cm[p, ds(g, GRP), :], CAP)
+        gr = gm[p, ds(g, GRP), :]
+        col = jnp.concatenate(
+            [jnp.sum(jnp.where(m, jnp.broadcast_to(gr[k:k + 1], (CAP, TOK)), 0.0), axis=1, keepdims=True)
+             for k, m in enumerate(oh)], axis=0)
+        oh = jnp.concatenate([jnp.where(m, 1.0, 0.0) for m in oh], axis=0).astype(BF16)
+        r = nn(oh, src[p])
+        res.append(r)
+        scaled.append(col * r)
+    for parts, put in ((res, store), (scaled, store_scaled)):
+        for k in range(GRP):
+            blk = jnp.concatenate([r[k * CAP:(k + 1) * CAP] for r in parts], axis=0)
+            put(k, ds(q, 2 * CAP), blk.astype(BF16))
+
+
 def gate_column(cm, gm, e):
     it = lax.broadcasted_iota(jnp.int32, (CAP, TOK), 0).astype(F32)
     cols = []
@@ -68,9 +87,9 @@
 
 def main_kernel(el, x_hbm, dy_hbm, rg_ref, w1_hbm, w3_hbm, w2_hbm,
                 y_ref, dg_ref, sx_hbm, sy_hbm, ka_hbm, kb_hbm, xa_hbm, dya_hbm, cm_hbm, gm_hbm, duv_hbm, a_hbm,
-                xs, dys, rgs, xe_s, o_s, uv_s, a_s, yacc, dxacc, cm, gm, dgm, dgo, dgr,
+                xs, dys, rgs, xe_s, do_s, dgc_s, o_s, uv_s, a_s, yacc, dxacc, cm, gm, dgm, dgo, dgr,
                 w1b, w3b, w2b, rd, r1, r2,
-                wsem, lsem, osem, psem, rg_ss, rg_rs, ag_ss, ag_rs, dd_ss, dd_rs, s1_ss, s1_rs, s2_ss, s2_rs, dg_ss, dg_rs):
+                wsem, lsem, osem, psem, credit, rg_ss, rg_rs, ag_ss, ag_rs, dd_ss, dd_rs, s1_ss, s1_rs, s2_ss, s2_rs, dg_ss, dg_rs):
     ng = el // GRP
     ff = w2b.shape[1]
     Z = lax.axis_index('dp')
@@ -109,7 +128,7 @@
         return [pltpu.make_async_copy(h.at[k], v.at[b], wsem.at[n, b])
                 for n, (h, v) in enumerate(((w1_hbm, w1b), (w3_hbm, w3b), (w2_hbm, w2b)))]
 
-    for e in range(NBUF - PAIR):
+    for e in range(2 * PAIR):
         for c in wcopies(e):
             c.start()
 
@@ -219,7 +238,18 @@
                 xe_s[k, rows, :] = val
             gather_pair(cm, g, q, src, store)
             return 0
-        lax.fori_loop(0, NP // 2, step, 0, unroll=2)
+        lax.fori_loop(0, NP // 2, step, 0, unroll=4)
+
+    def gather_dy(g):
+        def step(q, _):
+            def store(k, rows, val):
+                xe_s[k, rows, :] = val
+
+            def store_scaled(k, rows, val):
+                do_s[k, rows, :] = val
+            gather_dy_pair(cm, gm, g, q, dys, store, store_scaled)
+            return 0
+        lax.fori_loop(0, NP // 2, step, 0, unroll=4)
 
     def put_rows(i, val):
         zero = jnp.zeros((PAD - CAP, val.shape[1]), F32)
@@ -247,28 +277,52 @@
             gs = jnp.concatenate([spread(g1), spread(g2), spread(g3)], axis=0)
             yacc[p] += tn(gs, jnp.concatenate([ob, ob, ob], axis=0))
             return 0
-        lax.fori_loop(0, NP, step, 0, unroll=2)
+        lax.fori_loop(0, NP, step, 0, unroll=4)
 
     def combine_dx(g):
         def step(p, _):
             oh = onehot(cm[p, ds(g, GRP), :], PAD)
             one = jnp.concatenate([jnp.where(m, 1.0, 0.0) for m in oh], axis=0).astype(BF16)
             dxacc[p] += tn(one, take_rows(p))
+            rows = []
+            for k in range(GRP):
+                db = jnp.broadcast_to(dgc_s[k, ds(p, CAP), :], (CAP, TOK))
+                rows.append(jnp.sum(jnp.where(oh[k][:CAP], db, 0.0), axis=0, keepdims=True))
+            dgm[p, ds(g, GRP), :] = jnp.concatenate(rows, axis=0)
             return 0
-        lax.fori_loop(0, NP, step, 0, unroll=2)
-
-    def weights(n):
+        lax.fori_loop(0, NP, step, 0, unroll=4)
+
+    def fetch(n):
         for k in range(PAIR):
             for c in wcopies(n + k):
                 c.wait()
 
-        @pl.when(n + NBUF - PAIR < 2 * el)
+        @pl.when(n + 2 * PAIR < 2 * el)
         def _():
             for k in range(PAIR):
-                for c in wcopies(n + NBUF - PAIR + k):
+                for c in wcopies(n + 2 * PAIR + k):
                     c.start()
-        bufs = [lax.rem(n + k, NBUF) for k in range(PAIR)]
-        return [(jnp.concatenate([w1b[b], w3b[b]], axis=1), w2b[b]) for b in bufs]
+
+    def w13_of(n):
+        b = lax.rem(n, NBUF)
+        return jnp.concatenate([w1b[b], w3b[b]], axis=1)
+
+    def w2_of(n):
+        return w2b[lax.rem(n, NBUF)]
+
+    def skewed(g, first, base, second):
+        npair = GRP // PAIR
+        fetch(base)
+        first(0)
+
+        def step(r, _):
+            fetch(base + r * PAIR)
+            second(r - 1)
+            first(r)
+            return 0
+
+        lax.fori_loop(1, npair, step, 0)
+        second(npair - 1)
 
     def act(uv):
         u, v = uv[:, :ff], uv[:, ff:]
@@ -282,7 +336,7 @@
 
     def dd_copy(t, acc, n):
         fy, fx = ORDER[n]
-        return remote(acc.at[blk(fy, fx, 1)], rd.at[t, n], dd_ss.at[t, n], dd_rs.at[t, n], PN)
+        return remote(acc.at[blk(fy, fx, 1)], rd.at[n], dd_ss.at[t, n], dd_rs.at[t, n], PN)
 
     def s1_copy(t, acc, n):
         (fy, fx), h, to = S1[n]
@@ -300,7 +354,7 @@
         for n in range(4):
             dd_copy(t, acc, n).wait_recv()
             fy, fx = ORDER[n]
-            acc[blk(fy, fx, 0)] += rd[t, n]
+            acc[blk(fy, fx, 0)] += rd[n]
             for k in ((0, 1), (2,), (3,), ())[n]:
                 s1_copy(t, acc, k).start()
 
@@ -328,17 +382,18 @@
     def fwd_group(g, _):
         gather_all(g, xs)
 
-        def fwd(r, _):
-            n = g * GRP + r * PAIR
-            for k, (w13, w2) in enumerate(weights(n)):
+        def f1(r):
+            for k in range(PAIR):
                 i = r * PAIR + k
-                uv = nn(xe_s[i], w13).astype(BF16)
-                uv_s[n + k] = uv
-                a = act(uv.astype(F32))[3]
-                put_rows(i, nn(a, w2))
-            return 0
-
-        lax.fori_loop(0, GRP // PAIR, fwd, 0)
+                uv_s[g * GRP + i] = nn(xe_s[i], w13_of(g * GRP + i)).astype(BF16)
+
+        def f2(r):
+            uvs = [uv_s[g * GRP + r * PAIR + k].astype(F32) for k in range(PAIR)]
+            for k in range(PAIR):
+                i = r * PAIR + k
+                put_rows(i, nn(act(uvs[k])[3], w2_of(g * GRP + i)))
+
+        skewed(g, f1, g * GRP, f2)
         combine_y(g)
 
         @pl.when(g == 0)
@@ -361,46 +416,42 @@
         return pltpu.make_async_copy(uv_s.at[ds(g, GRP)], duv_hbm.at[ds(g, GRP)], osem.at[4])
 
     def a_copy(g):
-        return pltpu.make_async_copy(a_s.at[lax.rem(g, 2)], a_hbm.at[ds(g, GRP)], osem.at[5])
+        return pltpu.make_async_copy(a_s, a_hbm.at[ds(g, GRP)], osem.at[5])
 
     def bwd_group(g, _):
-        gather_all(g, dys)
-        slot = lax.rem(g, 2)
+        gather_dy(g)
 
         @pl.when(g == 0)
         def _():
             rs_start(0, yacc)
 
-        def bwd(r, _):
-            n = g * GRP + r * PAIR
-            for k, (w13, w2) in enumerate(weights(el + n)):
+        def b1(r):
+            uvs = [uv_s[g * GRP + r * PAIR + k] for k in range(PAIR)]
+            for k in range(PAIR):
                 i = r * PAIR + k
-                e = n + k
-                u, v, sg, a = act(uv_s[e].astype(F32))
-                a_s[slot, i] = a
+                e = g * GRP + i
+                w2 = w2_of(el + e)
+                da = nt(do_s[i], w2)
+                u, v, sg, a = act(uvs[k].astype(F32))
+                a_s[i] = a
                 of = nn(a, w2).astype(BF16).astype(F32)
-                dyf = xe_s[i].astype(F32)
-                dgc = jnp.sum(dyf * of, axis=1, keepdims=True)
-                it = lax.broadcasted_iota(jnp.int32, (CAP, TOK), 0).astype(F32)
-                for p in range(NP):
-                    m = jnp.broadcast_to(cm[p, pl.ds(e, 1), :], (CAP, TOK)) == it
-                    db = jnp.broadcast_to(dgc[p * CAP:(p + 1) * CAP], (CAP, TOK))
-                    dgm[p, pl.ds(e, 1), :] = jnp.sum(jnp.where(m, db, 0.0), axis=0, keepdims=True)
-                do = (gate_column(cm, gm, e) * dyf).astype(BF16)
-                da = nt(do, w2)
+                dgc_s[i] = jnp.sum(xe_s[i].astype(F32) * of, axis=1, keepdims=True)
                 du = (da * v * sg * (1.0 + u * (1.0 - sg))).astype(BF16)
                 dv = (da * u * sg).astype(BF16)
-                duv = jnp.concatenate([du, dv], axis=1)
-                uv_s[e] = duv
-                put_rows(i, nt(duv, w13))
-            return 0
+                uv_s[e] = jnp.concatenate([du, dv], axis=1)
+
+        def b2(r):
+            duvs = [uv_s[g * GRP + r * PAIR + k] for k in range(PAIR)]
+            for k in range(PAIR):
+                i = r * PAIR + k
+                put_rows(i, nt(duvs[k], w13_of(el + g * GRP + i)))
 
         @pl.when(g > 0)
         def _():
             a_copy(g - 1).wait()
             duv_copy(g - 1).wait()
 
-        lax.fori_loop(0, GRP // PAIR, bwd, 0)
+        skewed(g, b1, el + g * GRP, b2)
         a_copy(g).start()
         duv_copy(g).start()
         combine_dx(g)
@@ -408,6 +459,7 @@
         @pl.when(g == 1)
         def _():
             rs_mid1(0, yacc)
+            pl.semaphore_signal(credit, inc=1, device_id=dev(*PN), device_id_type=MESH)
 
         @pl.when(g == ng - 1)
         def _():
@@ -426,6 +478,7 @@
         return 0
 
     lax.fori_loop(0, NP, spread_dg, 0)
+    pl.semaphore_wait(credit, 1)
     rs_start(1, dxacc)
     rs_fin(0, yacc, y_ref)
     dg_copies = [remote(dgo.at[blk(*to)], dgr.at[n], dg_ss.at[n], dg_rs.at[n], to) for n, to in enumerate(peers)]
@@ -436,7 +489,7 @@
         dd_copy(1, dxacc, n).wait_recv()
         fy, fx = ORDER[n]
         b = blk(fy, fx, 0)
-        dxacc[b] += rd[1, n]
+        dxacc[b] += rd[n]
         to_b = (sy_hbm.at[0], kb_hbm.at[0], sy_hbm.at[1], kb_hbm.at[1])[n]
         to_a = (sx_hbm.at[0], sx_hbm.at[1], ka_hbm.at[0], ka_hbm.at[1])[n]
         for h, to in enumerate((to_a, to_b)):
@@ -535,9 +588,11 @@
                 pltpu.VMEM((NP, tok, d), BF16),
                 pltpu.VMEM((NP, 2 * top, tok), F32),
                 pltpu.VMEM((GRP, NROW, d), BF16),
+                pltpu.VMEM((GRP, NROW, d), BF16),
+                pltpu.VMEM((GRP, NROW, 1), F32),
                 pltpu.VMEM((GRP, NP * PAD, d), BF16),
                 pltpu.VMEM((el, NROW, 2 * ff), BF16),
-                pltpu.VMEM((2, GRP, NROW, ff), BF16),
+                pltpu.VMEM((GRP, NROW, ff), BF16),
                 pltpu.VMEM((NP, tok, d), F32),
                 pltpu.VMEM((NP, tok, d), F32),
                 pltpu.VMEM((NP, el, tok), F32),
@@ -548,10 +603,10 @@
                 pltpu.VMEM((NBUF, d, ff), BF16),
                 pltpu.VMEM((NBUF, d, ff), BF16),
                 pltpu.VMEM((NBUF, ff, d), BF16),
-                pltpu.VMEM((2, 4, tok, d), F32),
+                pltpu.VMEM((4, tok, d), F32),
                 pltpu.VMEM((1, 4, tok // 2, d), F32),
                 pltpu.VMEM((1, 2, tok // 2, d), F32),
-                dma((3, NBUF)), dma((2,)), dma((6,)), dma((4, 2)),
+                dma((3, NBUF)), dma((2,)), dma((6,)), dma((4, 2)), pltpu.SemaphoreType.REGULAR,
                 dma((NP - 1,)), dma((NP - 1,)),
                 dma((2, 14)), dma((2, 14)),
                 dma((2, 4)), dma((2, 4)),

time: 241 us -> 221 us (0.917)
  Pallas kernels: 232 us -> 212 us
    pallas_call x1, Pallas kernels: 166 us -> 146 us  [local(): pl.pallas_call(functools.partial(main_kernel, el), in_specs=[anyspec, any...]
  transfers between devices with their start and end apart: 4 -> 4, of which waited for: 0 -> 0; matrix products, arithmetic and copies ran while one was open for 0% -> 0% of each run, Pallas kernels for 27% -> 30%
where the time goes in v4:
time: 221 us
  Pallas kernels  212 us (96%)
  starting transfers between devices  4.12 us (2%)
  other arithmetic  3.04 us (1%)
    pallas_call x1, Pallas kernels, local(): pl.pallas_call(functools.partial(main_kernel, el), in_specs=[anyspec, any...  146 us
    pallas_call x2, Pallas kernels, grads(): pl.pallas_call(functools.partial(grad_kernel, first, count, eb, len(prev)...  65.2 us
  transfers between devices with their start and end apart: 4, of which 0 were waited for; matrix products, arithmetic and copies ran while one was open for 0% of the time, Pallas kernels for 30%

profile of v4, /device:TPU:0, one launch (start us, length us, event | category | flops | bytes accessed | tf_op | source)
XLA Modules:
  0.0 221.0 jit_solution(8972856286173295283)
XLA Ops:
  0.6 0.7 convert_bitcast_fusion
  1.3 1.3 pad_maximum_fusion.1.rg_ref
  2.6 146.5 %shard_map.118 = (bf16[256,896]{1,0:T(8,128)(2,1)}, f32[8,256]{1,0:T(8,128)}, f32[2,128,896]{2,1,0:T(8,128)}, f32[2,128,896]{2,1,0:T(8,128)}, f32[2,128,896]{2,1...) custom-call(bf16[256,896]{1,0:T(8,128)(2,1)} %x_hbm.1, ...), custom_call_target="tpu_custom_call" | custom-call | flops 40000000000 | bytes 160000000 | tf_op jit(solution)/shard_map/pallas_call | solution.py:576
  149.1 0.0 copy-start.1
  149.1 0.0 copy-start
  149.1 1.0 collective-permute-start
  150.1 1.1 collective-permute-start.1
  151.2 32.6 %shard_map.119 = (f32[48,896,256]{2,1,0:T(8,128)}, f32[48,896,256]{2,1,0:T(8,128)}, f32[48,256,896]{2,1,0:T(8,128)}) custom-call(bf16[8,256,896]{2,1,0:T(8,128)(2,1)} %get-tuple-element.31.xa_hbm, bf16[8,256,896]{2,1,0:T(8,128)(2,1)} %get-tuple-element.32.dya_hbm, f32[8,48,256]{2,1,0:T(8,128)} %get-tuple-element.33.cm, f32[8,48,256]{2,1,0:T(8,128)} %get-tuple-element.34.gm, ...), custom_call_target="tpu_custom_call" | custom-call | flops 10000000000 | bytes 75000000 | tf_op jit(solution)/shard_map/pallas_call | solution.py:638
  183.8 0.0 collective-permute-done
  183.8 0.0 collective-permute-done.1
  183.8 0.0 copy-done.1
  183.9 1.0 collective-permute-start.3
  184.9 0.0 copy-done
  184.9 0.0 copy-start.2
  184.9 0.0 copy-start.3
  184.9 1.1 collective-permute-start.2
  186.0 32.6 %shard_map.120 = (f32[48,896,256]{2,1,0:T(8,128)}, f32[48,896,256]{2,1,0:T(8,128)}, f32[48,256,896]{2,1,0:T(8,128)}) custom-call(bf16[8,256,896]{2,1,0:T(8,128)(2,1)} %get-tuple-element.31.xa_hbm, bf16[8,256,896]{2,1,0:T(8,128)(2,1)} %get-tuple-element.32.dya_hbm, ...), custom_call_target="tpu_custom_call", output_to_operand_aliasing={{0}: (6, {}), {1}: (7, {}), {2}: (8, {})} | custom-call | flops 10000000000 | bytes 75000000 | tf_op jit(solution)/shard_map/pallas_call | solution.py:638
  218.7 0.0 collective-permute-done.3
  218.7 0.1 fusion
  218.8 0.0 collective-permute-done.2
  218.8 0.1 fusion.1
  218.8 0.8 pad_maximum_fusion
  219.6 0.0 copy-done.2
  219.6 0.8 copy.21
  220.4 0.0 copy-done.3
  220.4 0.6 copy.22
  (2 shorter events, 0.1 us)
Async XLA Ops:
  149.1 34.7 %copy-start.1 = (f32[2,128,896]{2,1,0:T(8,128)S(1)}, f32[2,128,896]{2,1,0:T(8,128)}, u32[]{:S(2)}) copy-start(f32[2,128,896]{2,1,0:T(8,128)} %get-tuple-element.43) | copy-start | bytes 2752516
  149.1 35.7 %copy-start = (f32[2,128,896]{2,1,0:T(8,128)S(1)}, f32[2,128,896]{2,1,0:T(8,128)}, u32[]{:S(2)}) copy-start(f32[2,128,896]{2,1,0:T(8,128)} %get-tuple-element.30) | copy-start | bytes 2752516
  149.1 34.6 %collective-permute-start = (f32[2,128,896]{2,1,0:T(8,128)}, f32[2,128,896]{2,1,0:T(8,128)S(1)}, u32[]{:S(2)}, u32[]{:S(2)}) collective-permute-start(f32[2,128,896]{2,1,0:T(8,128)} %get-tuple-element.40), channel_id=1, source_target_pairs={{0,2},{1,3},{2,0},{3,1},{4,6},{5,7},{6,4},{7,5}} | collective-permute-start | bytes 2752520 | tf_op jit(solution)/shard_map/ppermute | solution.py:657
  150.1 33.7 %collective-permute-start.1 = (f32[2,128,896]{2,1,0:T(8,128)}, f32[2,128,896]{2,1,0:T(8,128)S(1)}, u32[]{:S(2)}, u32[]{:S(2)}) collective-permute-start(f32[2,128,896]{2,1,0:T(8,128)} %get-tuple-element.41), channel_id=1, source_target_pairs={{0,4},{1,5},{2,6},{3,7},{4,0},{5,1},{6,2},{7,3}} | collective-permute-start | bytes 2752520 | tf_op jit(solution)/shard_map/ppermute | solution.py:658
  183.9 34.8 %collective-permute-start.3 = (f32[128,896]{1,0:T(8,128)S(1)}, f32[128,896]{1,0:T(8,128)S(1)}, u32[]{:S(2)}, u32[]{:S(2)}) collective-permute-start(f32[128,896]{1,0:T(8,128)S(1)} %add_bitcast_fusion), channel_id=1, source_target_pairs={{0,2},{1,3},{2,0},{3,1},{4,6},{5,7},{6,4},{7,5}} | collective-permute-start | bytes 1376264 | tf_op jit(solution)/shard_map/ppermute | solution.py:662
  184.9 34.7 %copy-start.2 = (bf16[256,896]{1,0:T(8,128)(2,1)S(1)}, bf16[256,896]{1,0:T(8,128)(2,1)}, u32[]{:S(2)}) copy-start(bf16[256,896]{1,0:T(8,128)(2,1)} %get-tuple-element.58) | copy-start | bytes 1376260
  184.9 35.5 %copy-start.3 = (f32[8,256]{1,0:T(8,128)S(1)}, f32[8,256]{1,0:T(8,128)}, u32[]{:S(2)}) copy-start(f32[8,256]{1,0:T(8,128)} %get-tuple-element.45) | copy-start | bytes 24580
  184.9 33.8 %collective-permute-start.2 = (f32[128,896]{1,0:T(8,128)S(1)}, f32[128,896]{1,0:T(8,128)S(1)}, u32[]{:S(2)}, u32[]{:S(2)}) collective-permute-start(f32[128,896]{1,0:T(8,128)S(1)} %add_bitcast_fusion.1), channel_id=1, source_target_pairs={{0,4},{1,5},{2,6},{3,7},{4,0},{5,1},{6,2},{7,3}} | collective-permute-start | bytes 1376264 | tf_op jit(solution)/shard_map/ppermute | solution.py:661

commit v5 on v4

--- a/solution.py
+++ b/solution.py
@@ -70,23 +70,15 @@
         res.append(r)
         scaled.append(col * r)
     for parts, put in ((res, store), (scaled, store_scaled)):
+        if put is None:
+            continue
         for k in range(GRP):
             blk = jnp.concatenate([r[k * CAP:(k + 1) * CAP] for r in parts], axis=0)
             put(k, ds(q, 2 * CAP), blk.astype(BF16))
 
 
-def gate_column(cm, gm, e):
-    it = lax.broadcasted_iota(jnp.int32, (CAP, TOK), 0).astype(F32)
-    cols = []
-    for p in range(NP):
-        m = jnp.broadcast_to(cm[p, pl.ds(e, 1), :], (CAP, TOK)) == it
-        gb = jnp.broadcast_to(gm[p, pl.ds(e, 1), :], (CAP, TOK))
-        cols.append(jnp.sum(jnp.where(m, gb, 0.0), axis=1, keepdims=True))
-    return jnp.concatenate(cols, axis=0)
-
-
 def main_kernel(el, x_hbm, dy_hbm, rg_ref, w1_hbm, w3_hbm, w2_hbm,
-                y_ref, dg_ref, sx_hbm, sy_hbm, ka_hbm, kb_hbm, xa_hbm, dya_hbm, cm_hbm, gm_hbm, duv_hbm, a_hbm,
+                y_ref, dg_ref, sx_hbm, sy_hbm, ka_hbm, kb_hbm, xa_hbm, dya_hbm, cm_hbm, gm_hbm, duv_hbm, a_hbm, xef_hbm, dof_hbm,
                 xs, dys, rgs, xe_s, do_s, dgc_s, o_s, uv_s, a_s, yacc, dxacc, cm, gm, dgm, dgo, dgr,
                 w1b, w3b, w2b, rd, r1, r2,
                 wsem, lsem, osem, psem, credit, rg_ss, rg_rs, ag_ss, ag_rs, dd_ss, dd_rs, s1_ss, s1_rs, s2_ss, s2_rs, dg_ss, dg_rs):
@@ -379,8 +371,20 @@
         for n in range(2):
             s2_copy(t, acc, n).wait_send()
 
+    gs = SPLIT // GRP
+
+    def xef_copy(g):
+        return pltpu.make_async_copy(xe_s, xef_hbm.at[lax.div(g, gs)], osem.at[6])
+
+    def dof_copy(g):
+        return pltpu.make_async_copy(do_s, dof_hbm.at[lax.div(g, gs)], osem.at[7])
+
     def fwd_group(g, _):
         gather_all(g, xs)
+
+        @pl.when(lax.rem(g, gs) == 0)
+        def _():
+            xef_copy(g).start()
 
         def f1(r):
             for k in range(PAIR):
@@ -396,6 +400,10 @@
         skewed(g, f1, g * GRP, f2)
         combine_y(g)
 
+        @pl.when(lax.rem(g, gs) == 0)
+        def _():
+            xef_copy(g).wait()
+
         @pl.when(g == 0)
         def _():
             ag_relay(1, dys, (0, 1, 2, 3))
@@ -420,6 +428,10 @@
 
     def bwd_group(g, _):
         gather_dy(g)
+
+        @pl.when(lax.rem(g, gs) == 0)
+        def _():
+            dof_copy(g).start()
 
         @pl.when(g == 0)
         def _():
@@ -455,6 +467,10 @@
         a_copy(g).start()
         duv_copy(g).start()
         combine_dx(g)
+
+        @pl.when(lax.rem(g, gs) == 0)
+        def _():
+            dof_copy(g).wait()
 
         @pl.when(g == 1)
         def _():
@@ -517,45 +533,62 @@
     duv_copy(ng - 1).wait()
 
 
-def grad_kernel(first, count, eb, nprev, xa_hbm, dya_hbm, cm, gm, a_ref, duv_ref, *refs):
-    gw1_ref, gw3_ref, gw2_ref, xs, dys, xe_s, dye_s, sem = refs[nprev:]
+def grad_kernel(first, count, eb, nprev, xa_hbm, dya_hbm, cm, gm, a_ref, duv_ref, xef_ref, dof_ref, *refs):
+    gw1_ref, gw3_ref, gw2_ref, xs, dys, xe_s, do_s, sem = refs[nprev:]
     s = pl.program_id(0)
     per = GRP // eb
     ff = a_ref.shape[2]
+    g = lax.div(s, per)
+    i = lax.rem(s, per)
+    loads = [pltpu.make_async_copy(xa_hbm, xs, sem.at[0]), pltpu.make_async_copy(dya_hbm, dys, sem.at[1])]
 
     @pl.when(s == 0)
     def _():
-        cx = pltpu.make_async_copy(xa_hbm, xs, sem.at[0])
-        cd = pltpu.make_async_copy(dya_hbm, dys, sem.at[1])
-        cx.start()
-        cd.start()
-        cx.wait()
-        cd.wait()
-
-    @pl.when(s < count // eb)
+        for c in loads:
+            c.start()
+
+    @pl.when(s == 1)
     def _():
-        g = lax.div(s, per)
-        slot = lax.rem(g, 2)
-        for k in range(NP // 2 // per):
-            q = lax.rem(s, per) * (NP // 2 // per) + k
-            for src, dst in ((xs, xe_s), (dys, dye_s)):
-                def store(j, rows, val):
-                    dst[slot, j, rows, :] = val
-                gather_pair(cm, first // GRP + g, q, src, store)
-
-    @pl.when(s >= per)
+        for c in loads:
+            c.wait()
+
+    def gather(q):
+        n = g + 1
+        slot = lax.rem(n, 2)
+
+        def store(j, rows, val):
+            xe_s[slot, j, rows, :] = val
+
+        def store_scaled(j, rows, val):
+            do_s[slot, j, rows, :] = val
+        gather_pair(cm, first // GRP + n, q, xs, store)
+        gather_dy_pair(cm, gm, first // GRP + n, q, dys, None, store_scaled)
+
+    more = g + 1 < count // GRP
+
+    @pl.when(jnp.logical_and(more, i == 1))
     def _():
-        t = s - per
-        g = lax.div(t, per)
-        slot = lax.rem(g, 2)
+        gather(0)
+
+    @pl.when(jnp.logical_and(more, i >= 1))
+    def _():
+        gather(i)
+
+    def core(xe, do):
         for k in range(eb):
-            i = lax.rem(t, per) * eb + k
-            e = first + g * GRP + i
-            do = (gate_column(cm, gm, e) * dye_s[slot, i].astype(F32)).astype(BF16)
-            gw2_ref[k] = tn(a_ref[k], do)
-            g13 = tn(xe_s[slot, i], duv_ref[k])
+            g13 = tn(xe[k], duv_ref[k])
             gw1_ref[k] = g13[:, :ff]
             gw3_ref[k] = g13[:, ff:]
+            gw2_ref[k] = tn(a_ref[k], do[k])
+
+    @pl.when(g == 0)
+    def _():
+        core([xef_ref[0, k] for k in range(eb)], [dof_ref[0, k] for k in range(eb)])
+
+    @pl.when(g > 0)
+    def _():
+        slot = lax.rem(g, 2)
+        core([xe_s[slot, i * eb + k] for k in range(eb)], [do_s[slot, i * eb + k] for k in range(eb)])
 
 
 def solution(mesh):
@@ -573,15 +606,16 @@
         sds = jax.ShapeDtypeStruct
         rg = jnp.concatenate([ridx.T.astype(F32), gates.T], axis=0)
         dma = pltpu.SemaphoreType.DMA
-        y, dg, sx, sy, ka, kb, xa, dya, cm, gm, duv, a = pl.pallas_call(
+        y, dg, sx, sy, ka, kb, xa, dya, cm, gm, duv, a, xef, dof = pl.pallas_call(
             functools.partial(main_kernel, el),
             in_specs=[anyspec, anyspec, vm, anyspec, anyspec, anyspec],
-            out_specs=[vm, vm] + [anyspec] * 10,
+            out_specs=[vm, vm] + [anyspec] * 12,
             out_shape=[
                 sds((tok, d), BF16), sds((top, tok), F32)] + [sds((2, tok // 2, d), F32)] * 4 + [
                 sds((NP, tok, d), BF16), sds((NP, tok, d), BF16),
                 sds((NP, el, tok), F32), sds((NP, el, tok), F32),
                 sds((el, NROW, 2 * ff), BF16), sds((el, NROW, ff), BF16),
+                sds((el // SPLIT, GRP, NROW, d), BF16), sds((el // SPLIT, GRP, NROW, d), BF16),
             ],
             scratch_shapes=[
                 pltpu.VMEM((NP, tok, d), BF16),
@@ -606,7 +640,7 @@
                 pltpu.VMEM((4, tok, d), F32),
                 pltpu.VMEM((1, 4, tok // 2, d), F32),
                 pltpu.VMEM((1, 2, tok // 2, d), F32),
-                dma((3, NBUF)), dma((2,)), dma((6,)), dma((4, 2)), pltpu.SemaphoreType.REGULAR,
+                dma((3, NBUF)), dma((2,)), dma((8,)), dma((4, 2)), pltpu.SemaphoreType.REGULAR,
                 dma((NP - 1,)), dma((NP - 1,)),
                 dma((2, 14)), dma((2, 14)),
                 dma((2, 4)), dma((2, 4)),
@@ -630,18 +664,17 @@
         per = GRP // eb
 
         def grads(first, count, prev):
-            steps = count // eb + per
-
             def eidx(s):
-                return (first // eb + jnp.clip(s - per, 0, count // eb - 1), 0, 0)
-
+                return (first // eb + s, 0, 0)
+
+            head = pl.BlockSpec((1, eb, NROW, d), lambda s: (first // SPLIT, jnp.minimum(s, per - 1), 0, 0))
             return pl.pallas_call(
                 functools.partial(grad_kernel, first, count, eb, len(prev)),
-                grid=(steps,),
-                in_specs=[anyspec, anyspec, vm, vm, pl.BlockSpec((eb, NROW, ff), eidx), pl.BlockSpec((eb, NROW, 2 * ff), eidx)] + [anyspec] * len(prev),
+                grid=(count // eb,),
+                in_specs=[anyspec, anyspec, vm, vm, pl.BlockSpec((eb, NROW, ff), eidx), pl.BlockSpec((eb, NROW, 2 * ff), eidx), head, head] + [anyspec] * len(prev),
                 out_specs=[pl.BlockSpec((eb, d, ff), eidx), pl.BlockSpec((eb, d, ff), eidx), pl.BlockSpec((eb, ff, d), eidx)],
                 out_shape=[sds((el, d, ff), F32), sds((el, d, ff), F32), sds((el, ff, d), F32)],
-                input_output_aliases={6 + k: k for k in range(len(prev))},
+                input_output_aliases={8 + k: k for k in range(len(prev))},
                 scratch_shapes=[
                     pltpu.VMEM((NP, tok, d), BF16),
                     pltpu.VMEM((NP, tok, d), BF16),
@@ -652,7 +685,7 @@
                 compiler_params=pltpu.CompilerParams(
                     dimension_semantics=('arbitrary',), vmem_limit_bytes=60_000_000),
                 cost_estimate=pl.CostEstimate(flops=20_000_000_000 * count // el, bytes_accessed=150_000_000 * count // el, transcendentals=0),
-            )(xa, dya, cm, gm, a, duv, *prev)
+            )(xa, dya, cm, gm, a, duv, xef, dof, *prev)
 
         r1x = lax.ppermute(sx, grp, perm(0, 1))
         r1y = lax.ppermute(sy, grp, perm(1, 0))

time: 221 us -> 223 us (level)
    pallas_call x1, Pallas kernels: 146 us -> 149 us  [local(): pl.pallas_call(functools.partial(main_kernel, el), in_specs=[anyspec, any...]
  transfers between devices with their start and end apart: 4 -> 4, of which waited for: 0 -> 0; matrix products, arithmetic and copies ran while one was open for 0% -> 0% of each run, Pallas kernels for 30% -> 29%
where the time goes in v5:
time: 223 us; the launch traced here: 222 us
  Pallas kernels  213 us (96%)
  starting transfers between devices  4.11 us (2%)
  other arithmetic  3.05 us (1%)
    pallas_call x1, Pallas kernels, local(): pl.pallas_call(functools.partial(main_kernel, el), in_specs=[anyspec, any...  149 us
    pallas_call x2, Pallas kernels, grads(): pl.pallas_call(functools.partial(grad_kernel, first, count, eb, len(prev)...  63.9 us
  transfers between devices with their start and end apart: 4, of which 0 were waited for; matrix products, arithmetic and copies ran while one was open for 0% of the time, Pallas kernels for 29%

profile of v5, /device:TPU:0, one launch (start us, length us, event | category | flops | bytes accessed | tf_op | source)
XLA Modules:
  0.0 222.5 jit_solution(12980293924275638115)
XLA Ops:
  0.6 0.7 convert_bitcast_fusion
  1.3 1.3 pad_maximum_fusion.1.rg_ref
  2.6 149.3 %shard_map.118 = (bf16[256,896]{1,0:T(8,128)(2,1)}, f32[8,256]{1,0:T(8,128)}, f32[2,128,896]{2,1,0:T(8,128)}, f32[2,128,896]{2,1,0:T(8,128)}, f32[2,128,896]{2,1...) custom-call(bf16[256,896]{1,0:T(8,128)(2,1)} %x_hbm.1, ...), custom_call_target="tpu_custom_call" | custom-call | flops 40000000000 | bytes 160000000 | tf_op jit(solution)/shard_map/pallas_call | solution.py:609
  151.9 0.0 copy-start.1
  151.9 0.0 copy-start
  151.9 0.9 collective-permute-start
  152.9 1.1 collective-permute-start.1
  154.0 31.9 %shard_map.119 = (f32[48,896,256]{2,1,0:T(8,128)}, f32[48,896,256]{2,1,0:T(8,128)}, f32[48,256,896]{2,1,0:T(8,128)}) custom-call(bf16[8,256,896]{2,1,0:T(8,128)(2,1)} %get-tuple-element.33.xa_hbm, bf16[8,256,896]{2,1,0:T(8,128)(2,1)} %get-tuple-element.34.dya_hbm, f32[8,48,256]{2,1,0:T(8,128)} %get-tuple-element.35.cm, f32[8,48,256]{2,1,0:T(8,128)} %get-tuple-element.36.gm, ...), custom_call_target="tpu_custom_call" | custom-call | flops 10000000000 | bytes 75000000 | tf_op jit(solution)/shard_map/pallas_call | solution.py:671
  185.9 0.0 collective-permute-done
  185.9 0.0 collective-permute-done.1
  186.0 0.0 copy-done.1
  186.0 0.9 collective-permute-start.3
  186.9 0.0 copy-done
  187.0 0.0 copy-start.2
  187.0 0.0 copy-start.3
  187.0 1.1 collective-permute-start.2
  188.2 31.9 %shard_map.120 = (f32[48,896,256]{2,1,0:T(8,128)}, f32[48,896,256]{2,1,0:T(8,128)}, f32[48,256,896]{2,1,0:T(8,128)}) custom-call(bf16[8,256,896]{2,1,0:T(8,128)(2,1)} %get-tuple-element.33.xa_hbm, bf16[8,256,896]{2,1,0:T(8,128)(2,1)} %get-tuple-element.34.dya_hbm, ...), custom_call_target="tpu_custom_call", output_to_operand_aliasing={{0}: (8, {}), {1}: (9, {}), {2}: (10, {})} | custom-call | flops 10000000000 | bytes 75000000 | tf_op jit(solution)/shard_map/pallas_call | solution.py:671
  220.1 0.0 collective-permute-done.3
  220.1 0.1 fusion
  220.2 0.0 collective-permute-done.2
  220.2 0.1 fusion.1
  220.3 0.8 pad_maximum_fusion
  221.1 0.0 copy-done.2
  221.1 0.8 copy.21
  221.9 0.0 copy-done.3
  221.9 0.6 copy.22
  (2 shorter events, 0.1 us)
Async XLA Ops:
  151.9 34.0 %copy-start.1 = (f32[2,128,896]{2,1,0:T(8,128)S(1)}, f32[2,128,896]{2,1,0:T(8,128)}, u32[]{:S(2)}) copy-start(f32[2,128,896]{2,1,0:T(8,128)} %get-tuple-element.47) | copy-start | bytes 2752516
  151.9 35.0 %copy-start = (f32[2,128,896]{2,1,0:T(8,128)S(1)}, f32[2,128,896]{2,1,0:T(8,128)}, u32[]{:S(2)}) copy-start(f32[2,128,896]{2,1,0:T(8,128)} %get-tuple-element.32) | copy-start | bytes 2752516
  151.9 34.0 %collective-permute-start = (f32[2,128,896]{2,1,0:T(8,128)}, f32[2,128,896]{2,1,0:T(8,128)S(1)}, u32[]{:S(2)}, u32[]{:S(2)}) collective-permute-start(f32[2,128,896]{2,1,0:T(8,128)} %get-tuple-element.44), channel_id=1, source_target_pairs={{0,2},{1,3},{2,0},{3,1},{4,6},{5,7},{6,4},{7,5}} | collective-permute-start | bytes 2752520 | tf_op jit(solution)/shard_map/ppermute | solution.py:690
  152.9 33.1 %collective-permute-start.1 = (f32[2,128,896]{2,1,0:T(8,128)}, f32[2,128,896]{2,1,0:T(8,128)S(1)}, u32[]{:S(2)}, u32[]{:S(2)}) collective-permute-start(f32[2,128,896]{2,1,0:T(8,128)} %get-tuple-element.45), channel_id=1, source_target_pairs={{0,4},{1,5},{2,6},{3,7},{4,0},{5,1},{6,2},{7,3}} | collective-permute-start | bytes 2752520 | tf_op jit(solution)/shard_map/ppermute | solution.py:691
  186.0 34.1 %collective-permute-start.3 = (f32[128,896]{1,0:T(8,128)S(1)}, f32[128,896]{1,0:T(8,128)S(1)}, u32[]{:S(2)}, u32[]{:S(2)}) collective-permute-start(f32[128,896]{1,0:T(8,128)S(1)} %add_bitcast_fusion), channel_id=1, source_target_pairs={{0,2},{1,3},{2,0},{3,1},{4,6},{5,7},{6,4},{7,5}} | collective-permute-start | bytes 1376264 | tf_op jit(solution)/shard_map/ppermute | solution.py:695
  187.0 34.1 %copy-start.2 = (bf16[256,896]{1,0:T(8,128)(2,1)S(1)}, bf16[256,896]{1,0:T(8,128)(2,1)}, u32[]{:S(2)}) copy-start(bf16[256,896]{1,0:T(8,128)(2,1)} %get-tuple-element.62) | copy-start | bytes 1376260
  187.0 34.9 %copy-start.3 = (f32[8,256]{1,0:T(8,128)S(1)}, f32[8,256]{1,0:T(8,128)}, u32[]{:S(2)}) copy-start(f32[8,256]{1,0:T(8,128)} %get-tuple-element.49) | copy-start | bytes 24580
  187.0 33.2 %collective-permute-start.2 = (f32[128,896]{1,0:T(8,128)S(1)}, f32[128,896]{1,0:T(8,128)S(1)}, u32[]{:S(2)}, u32[]{:S(2)}) collective-permute-start(f32[128,896]{1,0:T(8,128)S(1)} %add_bitcast_fusion.1), channel_id=1, source_target_pairs={{0,4},{1,5},{2,6},{3,7},{4,0},{5,1},{6,2},{7,3}} | collective-permute-start | bytes 1376264 | tf_op jit(solution)/shard_map/ppermute | solution.py:694

commit v6 on v5

--- a/solution.py
+++ b/solution.py
@@ -19,7 +19,6 @@
 NROW = NP * CAP
 NBUF = 8
 PAIR = 2
-SPLIT = 24
 
 
 def nt(a, b):
@@ -77,8 +76,8 @@
             put(k, ds(q, 2 * CAP), blk.astype(BF16))
 
 
-def main_kernel(el, x_hbm, dy_hbm, rg_ref, w1_hbm, w3_hbm, w2_hbm,
-                y_ref, dg_ref, sx_hbm, sy_hbm, ka_hbm, kb_hbm, xa_hbm, dya_hbm, cm_hbm, gm_hbm, duv_hbm, a_hbm, xef_hbm, dof_hbm,
+def main_kernel(el, x_hbm, dy_hbm, id_ref, gate_ref, w1_hbm, w3_hbm, w2_hbm,
+                y_ref, dg_ref, sd_hbm, sx_hbm, sy_hbm, ka_hbm, xa_hbm, dya_hbm, cm_hbm, gm_hbm, duv_hbm, a_hbm, xef_hbm, dof_hbm,
                 xs, dys, rgs, xe_s, do_s, dgc_s, o_s, uv_s, a_s, yacc, dxacc, cm, gm, dgm, dgo, dgr,
                 w1b, w3b, w2b, rd, r1, r2,
                 wsem, lsem, osem, psem, credit, rg_ss, rg_rs, ag_ss, ag_rs, dd_ss, dd_rs, s1_ss, s1_rs, s2_ss, s2_rs, dg_ss, dg_rs):
@@ -124,13 +123,13 @@
         for c in wcopies(e):
             c.start()
 
+    rgs[me] = jnp.concatenate([id_ref[...].astype(F32), gate_ref[...]], axis=0)
     barrier = pltpu.get_barrier_semaphore()
     for to in peers:
         pl.semaphore_signal(barrier, inc=1, device_id=dev(*to), device_id_type=MESH)
     pl.semaphore_wait(barrier, len(peers))
 
-    rgs[me] = rg_ref[...]
-    rg_copies = [remote(rg_ref, rgs.at[me], rg_ss.at[n], rg_rs.at[n], to) for n, to in enumerate(peers)]
+    rg_copies = [remote(rgs.at[me], rgs.at[me], rg_ss.at[n], rg_rs.at[n], to) for n, to in enumerate(peers)]
     for c in rg_copies:
         c.start()
 
@@ -271,8 +270,9 @@
             return 0
         lax.fori_loop(0, NP, step, 0, unroll=4)
 
-    def combine_dx(g):
-        def step(p, _):
+    def combine_dx(g, cc):
+        for j in range(NP // 2):
+            p = 2 * j + cc
             oh = onehot(cm[p, ds(g, GRP), :], PAD)
             one = jnp.concatenate([jnp.where(m, 1.0, 0.0) for m in oh], axis=0).astype(BF16)
             dxacc[p] += tn(one, take_rows(p))
@@ -281,8 +281,6 @@
                 db = jnp.broadcast_to(dgc_s[k, ds(p, CAP), :], (CAP, TOK))
                 rows.append(jnp.sum(jnp.where(oh[k][:CAP], db, 0.0), axis=0, keepdims=True))
             dgm[p, ds(g, GRP), :] = jnp.concatenate(rows, axis=0)
-            return 0
-        lax.fori_loop(0, NP, step, 0, unroll=4)
 
     def fetch(n):
         for k in range(PAIR):
@@ -371,20 +369,15 @@
         for n in range(2):
             s2_copy(t, acc, n).wait_send()
 
-    gs = SPLIT // GRP
-
-    def xef_copy(g):
-        return pltpu.make_async_copy(xe_s, xef_hbm.at[lax.div(g, gs)], osem.at[6])
-
-    def dof_copy(g):
-        return pltpu.make_async_copy(do_s, dof_hbm.at[lax.div(g, gs)], osem.at[7])
+    xef_copy = pltpu.make_async_copy(xe_s, xef_hbm, osem.at[6])
+    dof_copy = pltpu.make_async_copy(do_s, dof_hbm, osem.at[7])
 
     def fwd_group(g, _):
         gather_all(g, xs)
 
-        @pl.when(lax.rem(g, gs) == 0)
-        def _():
-            xef_copy(g).start()
+        @pl.when(g == 0)
+        def _():
+            xef_copy.start()
 
         def f1(r):
             for k in range(PAIR):
@@ -400,9 +393,9 @@
         skewed(g, f1, g * GRP, f2)
         combine_y(g)
 
-        @pl.when(lax.rem(g, gs) == 0)
-        def _():
-            xef_copy(g).wait()
+        @pl.when(g == 0)
+        def _():
+            xef_copy.wait()
 
         @pl.when(g == 0)
         def _():
@@ -429,9 +422,9 @@
     def bwd_group(g, _):
         gather_dy(g)
 
-        @pl.when(lax.rem(g, gs) == 0)
-        def _():
-            dof_copy(g).start()
+        @pl.when(g == 0)
+        def _():
+            dof_copy.start()
 
         @pl.when(g == 0)
         def _():
@@ -466,11 +459,17 @@
         skewed(g, b1, el + g * GRP, b2)
         a_copy(g).start()
         duv_copy(g).start()
-        combine_dx(g)
-
-        @pl.when(lax.rem(g, gs) == 0)
-        def _():
-            dof_copy(g).wait()
+        combine_dx(g, 1 - C)
+
+        @pl.when(g == ng - 1)
+        def _():
+            pl.semaphore_wait(credit, 1)
+            rs_start(1, dxacc)
+        combine_dx(g, C)
+
+        @pl.when(g == 0)
+        def _():
+            dof_copy.wait()
 
         @pl.when(g == 1)
         def _():
@@ -494,8 +493,6 @@
         return 0
 
     lax.fori_loop(0, NP, spread_dg, 0)
-    pl.semaphore_wait(credit, 1)
-    rs_start(1, dxacc)
     rs_fin(0, yacc, y_ref)
     dg_copies = [remote(dgo.at[blk(*to)], dgr.at[n], dg_ss.at[n], dg_rs.at[n], to) for n, to in enumerate(peers)]
     for c in dg_copies:
@@ -503,15 +500,11 @@
     part_copies = []
     for n in range(4):
         dd_copy(1, dxacc, n).wait_recv()
-        fy, fx = ORDER[n]
-        b = blk(fy, fx, 0)
+        b = blk(*ORDER[n], 0)
         dxacc[b] += rd[n]
-        to_b = (sy_hbm.at[0], kb_hbm.at[0], sy_hbm.at[1], kb_hbm.at[1])[n]
-        to_a = (sx_hbm.at[0], sx_hbm.at[1], ka_hbm.at[0], ka_hbm.at[1])[n]
-        for h, to in enumerate((to_a, to_b)):
-            c = pltpu.make_async_copy(half(dxacc, b, h), to, psem.at[n, h])
-            c.start()
-            part_copies.append(c)
+        c = pltpu.make_async_copy(dxacc.at[b], (sd_hbm, sx_hbm, sy_hbm, ka_hbm)[n], psem.at[n])
+        c.start()
+        part_copies.append(c)
     total = dgo[me]
     for n, c in enumerate(dg_copies):
         c.wait_recv()
@@ -533,8 +526,8 @@
     duv_copy(ng - 1).wait()
 
 
-def grad_kernel(first, count, eb, nprev, xa_hbm, dya_hbm, cm, gm, a_ref, duv_ref, xef_ref, dof_ref, *refs):
-    gw1_ref, gw3_ref, gw2_ref, xs, dys, xe_s, do_s, sem = refs[nprev:]
+def grad_kernel(count, eb, y_ref, dg_ref, xa_hbm, dya_hbm, cm, gm, a_ref, duv_ref, xef_ref, dof_ref,
+                yo_ref, dgo_ref, gw1_ref, gw3_ref, gw2_ref, xs, dys, xe_s, do_s, sem):
     s = pl.program_id(0)
     per = GRP // eb
     ff = a_ref.shape[2]
@@ -546,6 +539,8 @@
     def _():
         for c in loads:
             c.start()
+        yo_ref[...] = y_ref[...]
+        dgo_ref[...] = dg_ref[...]
 
     @pl.when(s == 1)
     def _():
@@ -561,18 +556,14 @@
 
         def store_scaled(j, rows, val):
             do_s[slot, j, rows, :] = val
-        gather_pair(cm, first // GRP + n, q, xs, store)
-        gather_dy_pair(cm, gm, first // GRP + n, q, dys, None, store_scaled)
+        gather_pair(cm, n, q, xs, store)
+        gather_dy_pair(cm, gm, n, q, dys, None, store_scaled)
 
     more = g + 1 < count // GRP
 
-    @pl.when(jnp.logical_and(more, i == 1))
+    @pl.when(jnp.logical_and(more, jnp.logical_and(i >= 1, i <= NP // 2)))
     def _():
-        gather(0)
-
-    @pl.when(jnp.logical_and(more, i >= 1))
-    def _():
-        gather(i)
+        gather(i - 1)
 
     def core(xe, do):
         for k in range(eb):
@@ -583,7 +574,7 @@
 
     @pl.when(g == 0)
     def _():
-        core([xef_ref[0, k] for k in range(eb)], [dof_ref[0, k] for k in range(eb)])
+        core([xef_ref[k] for k in range(eb)], [dof_ref[k] for k in range(eb)])
 
     @pl.when(g > 0)
     def _():
@@ -604,18 +595,17 @@
         anyspec = pl.BlockSpec(memory_space=pl.ANY)
         vm = pl.BlockSpec(memory_space=pltpu.VMEM)
         sds = jax.ShapeDtypeStruct
-        rg = jnp.concatenate([ridx.T.astype(F32), gates.T], axis=0)
         dma = pltpu.SemaphoreType.DMA
-        y, dg, sx, sy, ka, kb, xa, dya, cm, gm, duv, a, xef, dof = pl.pallas_call(
+        y, dg, sd, sx, sy, ka, xa, dya, cm, gm, duv, a, xef, dof = pl.pallas_call(
             functools.partial(main_kernel, el),
-            in_specs=[anyspec, anyspec, vm, anyspec, anyspec, anyspec],
+            in_specs=[anyspec, anyspec, vm, vm, anyspec, anyspec, anyspec],
             out_specs=[vm, vm] + [anyspec] * 12,
             out_shape=[
-                sds((tok, d), BF16), sds((top, tok), F32)] + [sds((2, tok // 2, d), F32)] * 4 + [
+                sds((tok, d), BF16), sds((top, tok), F32)] + [sds((tok, d), F32)] * 4 + [
                 sds((NP, tok, d), BF16), sds((NP, tok, d), BF16),
                 sds((NP, el, tok), F32), sds((NP, el, tok), F32),
                 sds((el, NROW, 2 * ff), BF16), sds((el, NROW, ff), BF16),
-                sds((el // SPLIT, GRP, NROW, d), BF16), sds((el // SPLIT, GRP, NROW, d), BF16),
+                sds((GRP, NROW, d), BF16), sds((GRP, NROW, d), BF16),
             ],
             scratch_shapes=[
                 pltpu.VMEM((NP, tok, d), BF16),
@@ -640,7 +630,7 @@
                 pltpu.VMEM((4, tok, d), F32),
                 pltpu.VMEM((1, 4, tok // 2, d), F32),
                 pltpu.VMEM((1, 2, tok // 2, d), F32),
-                dma((3, NBUF)), dma((2,)), dma((8,)), dma((4, 2)), pltpu.SemaphoreType.REGULAR,
+                dma((3, NBUF)), dma((2,)), dma((8,)), dma((4,)), pltpu.SemaphoreType.REGULAR,
                 dma((NP - 1,)), dma((NP - 1,)),
                 dma((2, 14)), dma((2, 14)),
                 dma((2, 4)), dma((2, 4)),
@@ -651,7 +641,7 @@
             compiler_params=pltpu.CompilerParams(
                 collective_id=0, has_side_effects=True, vmem_limit_bytes=67_000_000),
             cost_estimate=pl.CostEstimate(flops=40_000_000_000, bytes_accessed=160_000_000, transcendentals=0),
-        )(x, dy, rg, w1, w3, w2)
+        )(x, dy, ridx.T, gates.T, w1, w3, w2)
 
         def perm(fy, fx):
             out = []
@@ -660,41 +650,34 @@
                 out.append((p, (yy ^ fy) * 4 + (xx ^ fx) * 2 + cc))
             return out
 
-        eb = 2
+        rd = lax.ppermute(sd, grp, perm(1, 1))
+        rx = lax.ppermute(sx, grp, perm(0, 1))
+        ry = lax.ppermute(sy, grp, perm(1, 0))
+        eb = 1
         per = GRP // eb
 
-        def grads(first, count, prev):
-            def eidx(s):
-                return (first // eb + s, 0, 0)
-
-            head = pl.BlockSpec((1, eb, NROW, d), lambda s: (first // SPLIT, jnp.minimum(s, per - 1), 0, 0))
-            return pl.pallas_call(
-                functools.partial(grad_kernel, first, count, eb, len(prev)),
-                grid=(count // eb,),
-                in_specs=[anyspec, anyspec, vm, vm, pl.BlockSpec((eb, NROW, ff), eidx), pl.BlockSpec((eb, NROW, 2 * ff), eidx), head, head] + [anyspec] * len(prev),
-                out_specs=[pl.BlockSpec((eb, d, ff), eidx), pl.BlockSpec((eb, d, ff), eidx), pl.BlockSpec((eb, ff, d), eidx)],
-                out_shape=[sds((el, d, ff), F32), sds((el, d, ff), F32), sds((el, ff, d), F32)],
-                input_output_aliases={8 + k: k for k in range(len(prev))},
-                scratch_shapes=[
-                    pltpu.VMEM((NP, tok, d), BF16),
-                    pltpu.VMEM((NP, tok, d), BF16),
-                    pltpu.VMEM((2, GRP, NROW, d), BF16),
-                    pltpu.VMEM((2, GRP, NROW, d), BF16),
-                    pltpu.SemaphoreType.DMA((2,)),
-                ],
-                compiler_params=pltpu.CompilerParams(
-                    dimension_semantics=('arbitrary',), vmem_limit_bytes=60_000_000),
-                cost_estimate=pl.CostEstimate(flops=20_000_000_000 * count // el, bytes_accessed=150_000_000 * count // el, transcendentals=0),
-            )(xa, dya, cm, gm, a, duv, xef, dof, *prev)
-
-        r1x = lax.ppermute(sx, grp, perm(0, 1))
-        r1y = lax.ppermute(sy, grp, perm(1, 0))
-        prev = grads(0, SPLIT, ())
-        prev, r1x, r1y = lax.optimization_barrier((prev, r1x, r1y))
-        r2a = lax.ppermute(ka[0] + r1x[0], grp, perm(1, 0))
-        r2b = lax.ppermute(kb[0] + r1y[0], grp, perm(0, 1))
-        gw1, gw3, gw2 = grads(SPLIT, el - SPLIT, tuple(prev))
-        dx = jnp.concatenate([ka[1] + r1x[1] + r2a, kb[1] + r1y[1] + r2b], axis=0).astype(BF16)
+        def eidx(s):
+            return (s, 0, 0)
+
+        head = pl.BlockSpec((eb, NROW, d), lambda s: (jnp.minimum(s, per - 1), 0, 0))
+        y, dg, gw1, gw3, gw2 = pl.pallas_call(
+            functools.partial(grad_kernel, el, eb),
+            grid=(el // eb,),
+            in_specs=[vm, vm, anyspec, anyspec, vm, vm, pl.BlockSpec((eb, NROW, ff), eidx), pl.BlockSpec((eb, NROW, 2 * ff), eidx), head, head],
+            out_specs=[vm, vm, pl.BlockSpec((eb, d, ff), eidx), pl.BlockSpec((eb, d, ff), eidx), pl.BlockSpec((eb, ff, d), eidx)],
+            out_shape=[sds((tok, d), BF16), sds((top, tok), F32), sds((el, d, ff), F32), sds((el, d, ff), F32), sds((el, ff, d), F32)],
+            scratch_shapes=[
+                pltpu.VMEM((NP, tok, d), BF16),
+                pltpu.VMEM((NP, tok, d), BF16),
+                pltpu.VMEM((2, GRP, NROW, d), BF16),
+                pltpu.VMEM((2, GRP, NROW, d), BF16),
+                pltpu.SemaphoreType.DMA((2,)),
+            ],
+            compiler_params=pltpu.CompilerParams(
+                dimension_semantics=('arbitrary',), vmem_limit_bytes=56_000_000),
+            cost_estimate=pl.CostEstimate(flops=40_000_000_000, bytes_accessed=160_000_000, transcendentals=0),
+        )(y, dg, xa, dya, cm, gm, a, duv, xef, dof)
+        dx = (ka + rx + ry + rd).astype(BF16)
         return y, dx, dg.T, gw1, gw3, gw2
 
     return jax.shard_map(local, mesh=mesh, in_specs=(tspec, tspec, tspec, wspec, wspec, wspec, tspec), out_specs=(tspec, tspec, tspec, gspec, gspec, gspec), check_vma=False)

time: 223 us -> 223 us (level)
    pallas_call x2 -> x1, Pallas kernels: 63.9 us -> 67 us  [local(): pl.pallas_call(functools.partial(grad_kernel, el, eb), grid=(el // eb,),...]
  transfers between devices with their start and end apart: 4 -> 3, of which waited for: 0 -> 0; matrix products, arithmetic and copies ran while one was open for 0% -> 0% of each run, Pallas kernels for 29% -> 30%
where the time goes in v6:
time: 223 us; the launch traced here: 221 us
  Pallas kernels  214 us (96%)
  starting transfers between devices  3.51 us (2%)
    pallas_call x1, Pallas kernels, local(): pl.pallas_call(functools.partial(main_kernel, el), in_specs=[anyspec, any...  147 us
    pallas_call x1, Pallas kernels, local(): pl.pallas_call(functools.partial(grad_kernel, el, eb), grid=(el // eb,),...  67 us
  transfers between devices with their start and end apart: 3, of which 0 were waited for; matrix products, arithmetic and copies ran while one was open for 0% of the time, Pallas kernels for 30%

profile of v6, /device:TPU:0, one launch (start us, length us, event | category | flops | bytes accessed | tf_op | source)
XLA Modules:
  0.0 221.2 jit_solution(12072810106097989087)
XLA Ops:
  0.6 147.4 %shard_map.118 = (bf16[256,896]{1,0:T(8,128)(2,1)}, f32[8,256]{1,0:T(8,128)}, f32[256,896]{1,0:T(8,128)}, f32[256,896]{1,0:T(8,128)}, f32[256,896]{1,0:T(8,128)}...) custom-call(bf16[256,896]{1,0:T(8,128)(2,1)} %x_hbm.1, ...), custom_call_target="tpu_custom_call" | custom-call | flops 40000000000 | bytes 160000000 | tf_op jit(solution)/shard_map/pallas_call | solution.py:599
  148.0 0.8 collective-permute-start
  148.8 1.3 collective-permute-start.1
  150.1 1.5 collective-permute-start.2
  151.6 0.0 copy-start
  151.6 1.0 copy-done
  152.6 0.0 copy-start.1
  152.6 0.7 copy-done.1
  153.2 0.0 copy-start.2
  153.3 67.0 %shard_map.119 = (bf16[256,896]{1,0:T(8,128)(2,1)}, f32[8,256]{1,0:T(8,128)}, f32[48,896,256]{2,1,0:T(8,128)}, f32[48,896,256]{2,1,0:T(8,128)}, f32[48,256,896]{2,1,0:T(8,128)}) custom-call(bf16[256,896]{1,0:T(8,128)(2,1)} %get-tuple-element.25.y_ref, f32[8,256]{1,0:T(8,128)S(1)} %copy-done.1, bf16[8,256,896]{2,1,0:T(8,128)(2,1)} %get-tuple-element.27.xa_hbm, ...), custom_call_target="tpu_custom_call" | custom-call | flops 40000000000 | bytes 160000000 | tf_op jit(solution)/shard_map/pallas_call | solution.py:663
  220.3 0.0 collective-permute-done
  220.3 0.0 collective-permute-done.1
  220.3 0.0 collective-permute-done.2
  220.3 0.0 copy-done.2
  220.3 0.9 add_convert_fusion
Async XLA Ops:
  148.0 72.2 %collective-permute-start = (f32[256,896]{1,0:T(8,128)}, f32[256,896]{1,0:T(8,128)S(1)}, u32[]{:S(2)}, u32[]{:S(2)}) collective-permute-start(f32[256,896]{1,0:T(8,128)} %get-tuple-element.37), channel_id=1, source_target_pairs={{0,2},{1,3},{2,0},{3,1},{4,6},{5,7},{6,4},{7,5}} | collective-permute-start | bytes 2752520 | tf_op jit(solution)/shard_map/ppermute | solution.py:654
  148.8 71.5 %collective-permute-start.1 = (f32[256,896]{1,0:T(8,128)}, f32[256,896]{1,0:T(8,128)S(1)}, u32[]{:S(2)}, u32[]{:S(2)}) collective-permute-start(f32[256,896]{1,0:T(8,128)} %get-tuple-element.38), channel_id=1, source_target_pairs={{0,4},{1,5},{2,6},{3,7},{4,0},{5,1},{6,2},{7,3}} | collective-permute-start | bytes 2752520 | tf_op jit(solution)/shard_map/ppermute | solution.py:655
  150.1 70.2 %collective-permute-start.2 = (f32[256,896]{1,0:T(8,128)}, f32[256,896]{1,0:T(8,128)S(1)}, u32[]{:S(2)}, u32[]{:S(2)}) collective-permute-start(f32[256,896]{1,0:T(8,128)} %get-tuple-element.39), channel_id=1, source_target_pairs={{0,6},{1,7},{2,4},{3,5},{4,2},{5,3},{6,0},{7,1}} | collective-permute-start | bytes 2752520 | tf_op jit(solution)/shard_map/ppermute | solution.py:653
  151.6 1.0 copy-start
  152.6 0.7 copy-start.1
  153.2 67.0 %copy-start.2 = (f32[256,896]{1,0:T(8,128)S(1)}, f32[256,896]{1,0:T(8,128)}, u32[]{:S(2)}) copy-start(f32[256,896]{1,0:T(8,128)} %get-tuple-element.36) | copy-start | bytes 2752516

commit v7 on v6

--- a/solution.py
+++ b/solution.py
@@ -19,6 +19,7 @@
 NROW = NP * CAP
 NBUF = 8
 PAIR = 2
+NOUT = 3
 
 
 def nt(a, b):
@@ -526,60 +527,108 @@
     duv_copy(ng - 1).wait()
 
 
-def grad_kernel(count, eb, y_ref, dg_ref, xa_hbm, dya_hbm, cm, gm, a_ref, duv_ref, xef_ref, dof_ref,
-                yo_ref, dgo_ref, gw1_ref, gw3_ref, gw2_ref, xs, dys, xe_s, do_s, sem):
-    s = pl.program_id(0)
-    per = GRP // eb
-    ff = a_ref.shape[2]
-    g = lax.div(s, per)
-    i = lax.rem(s, per)
-    loads = [pltpu.make_async_copy(xa_hbm, xs, sem.at[0]), pltpu.make_async_copy(dya_hbm, dys, sem.at[1])]
-
-    @pl.when(s == 0)
-    def _():
-        for c in loads:
-            c.start()
-        yo_ref[...] = y_ref[...]
-        dgo_ref[...] = dg_ref[...]
-
-    @pl.when(s == 1)
-    def _():
-        for c in loads:
-            c.wait()
-
-    def gather(q):
-        n = g + 1
-        slot = lax.rem(n, 2)
+def grad_kernel(el, y_ref, dg_ref, xa_hbm, dya_hbm, cm, gm, a_hbm, duv_hbm, xef_hbm, dof_hbm,
+                yo_ref, dgo_ref, gw1_hbm, gw3_hbm, gw2_hbm,
+                xs, dys, xe_s, do_s, a_s, duv_s, g1b, g3b, g2b, lsem, isem, gsem):
+    ng = el // GRP
+    npair = GRP // PAIR
+    ff = a_s.shape[3]
+
+    def inputs(g):
+        slot = lax.rem(g, 2)
+        return [pltpu.make_async_copy(a_hbm.at[ds(g, GRP)], a_s.at[slot], isem.at[0, slot]),
+                pltpu.make_async_copy(duv_hbm.at[ds(g, GRP)], duv_s.at[slot], isem.at[1, slot])]
+
+    def outputs(m):
+        slot = lax.rem(m, NOUT)
+        return [pltpu.make_async_copy(v.at[slot], h.at[ds(m, PAIR)], gsem.at[n, slot])
+                for n, (h, v) in enumerate(((gw1_hbm, g1b), (gw3_hbm, g3b), (gw2_hbm, g2b)))]
+
+    heads = [pltpu.make_async_copy(xef_hbm, xe_s.at[0], lsem.at[2]), pltpu.make_async_copy(dof_hbm, do_s.at[0], lsem.at[3])]
+    loads = [pltpu.make_async_copy(xa_hbm, xs, lsem.at[0]), pltpu.make_async_copy(dya_hbm, dys, lsem.at[1])]
+    for c in heads + inputs(0) + loads:
+        c.start()
+    yo_ref[...] = y_ref[...]
+    dgo_ref[...] = dg_ref[...]
+
+    def gather(g, q):
+        slot = lax.rem(g, 2)
 
         def store(j, rows, val):
             xe_s[slot, j, rows, :] = val
 
         def store_scaled(j, rows, val):
             do_s[slot, j, rows, :] = val
-        gather_pair(cm, n, q, xs, store)
-        gather_dy_pair(cm, gm, n, q, dys, None, store_scaled)
-
-    more = g + 1 < count // GRP
-
-    @pl.when(jnp.logical_and(more, jnp.logical_and(i >= 1, i <= NP // 2)))
-    def _():
-        gather(i - 1)
-
-    def core(xe, do):
-        for k in range(eb):
-            g13 = tn(xe[k], duv_ref[k])
-            gw1_ref[k] = g13[:, :ff]
-            gw3_ref[k] = g13[:, ff:]
-            gw2_ref[k] = tn(a_ref[k], do[k])
-
-    @pl.when(g == 0)
-    def _():
-        core([xef_ref[k] for k in range(eb)], [dof_ref[k] for k in range(eb)])
-
-    @pl.when(g > 0)
-    def _():
+        gather_pair(cm, g, q, xs, store)
+        gather_dy_pair(cm, gm, g, q, dys, None, store_scaled)
+
+    def core(g, r):
         slot = lax.rem(g, 2)
-        core([xe_s[slot, i * eb + k] for k in range(eb)], [do_s[slot, i * eb + k] for k in range(eb)])
+        o = lax.rem(g * npair + r, NOUT)
+        for k in range(PAIR):
+            i = r * PAIR + k
+            g13 = tn(xe_s[slot, i], duv_s[slot, i])
+            g1b[o, k] = g13[:, :ff]
+            g3b[o, k] = g13[:, ff:]
+            g2b[o, k] = tn(a_s[slot, i], do_s[slot, i])
+
+    def finish(g, r):
+        for c in outputs(g * npair + r):
+            c.start()
+
+    for c in heads + inputs(0):
+        c.wait()
+    for c in inputs(1):
+        c.start()
+    for r in range(npair):
+        if r == 1:
+            for c in loads:
+                c.wait()
+        if r == NOUT:
+            for c in outputs(0):
+                c.wait()
+        core(0, r)
+        for q in ((), (0, 1), (2,), (3,))[r]:
+            gather(1, q)
+        finish(0, r)
+
+    def group(g, _):
+        for c in inputs(g):
+            c.wait()
+
+        @pl.when(g + 1 < ng)
+        def _():
+            for c in inputs(g + 1):
+                c.start()
+
+        def step(r, _):
+            for c in outputs(g * npair + r - NOUT):
+                c.wait()
+            core(g, r)
+            gather(g + 1, r)
+            finish(g, r)
+            return 0
+
+        def last(r, _):
+            for c in outputs(g * npair + r - NOUT):
+                c.wait()
+            core(g, r)
+            finish(g, r)
+            return 0
+
+        @pl.when(g + 1 < ng)
+        def _():
+            lax.fori_loop(0, npair, step, 0)
+
+        @pl.when(g + 1 == ng)
+        def _():
+            lax.fori_loop(0, npair, last, 0)
+        return 0
+
+    lax.fori_loop(1, ng, group, 0)
+    for m in range(NOUT):
+        for c in outputs(ng * npair - NOUT + m):
+            c.wait()
 
 
 def solution(mesh):
@@ -653,28 +702,24 @@
         rd = lax.ppermute(sd, grp, perm(1, 1))
         rx = lax.ppermute(sx, grp, perm(0, 1))
         ry = lax.ppermute(sy, grp, perm(1, 0))
-        eb = 1
-        per = GRP // eb
-
-        def eidx(s):
-            return (s, 0, 0)
-
-        head = pl.BlockSpec((eb, NROW, d), lambda s: (jnp.minimum(s, per - 1), 0, 0))
         y, dg, gw1, gw3, gw2 = pl.pallas_call(
-            functools.partial(grad_kernel, el, eb),
-            grid=(el // eb,),
-            in_specs=[vm, vm, anyspec, anyspec, vm, vm, pl.BlockSpec((eb, NROW, ff), eidx), pl.BlockSpec((eb, NROW, 2 * ff), eidx), head, head],
-            out_specs=[vm, vm, pl.BlockSpec((eb, d, ff), eidx), pl.BlockSpec((eb, d, ff), eidx), pl.BlockSpec((eb, ff, d), eidx)],
+            functools.partial(grad_kernel, el),
+            in_specs=[vm, vm, anyspec, anyspec, vm, vm] + [anyspec] * 4,
+            out_specs=[vm, vm, anyspec, anyspec, anyspec],
             out_shape=[sds((tok, d), BF16), sds((top, tok), F32), sds((el, d, ff), F32), sds((el, d, ff), F32), sds((el, ff, d), F32)],
             scratch_shapes=[
                 pltpu.VMEM((NP, tok, d), BF16),
                 pltpu.VMEM((NP, tok, d), BF16),
                 pltpu.VMEM((2, GRP, NROW, d), BF16),
                 pltpu.VMEM((2, GRP, NROW, d), BF16),
-                pltpu.SemaphoreType.DMA((2,)),
+                pltpu.VMEM((2, GRP, NROW, ff), BF16),
+                pltpu.VMEM((2, GRP, NROW, 2 * ff), BF16),
+                pltpu.VMEM((NOUT, PAIR, d, ff), F32),
+                pltpu.VMEM((NOUT, PAIR, d, ff), F32),
+                pltpu.VMEM((NOUT, PAIR, ff, d), F32),
+                dma((4,)), dma((2, 2)), dma((3, NOUT)),
             ],
-            compiler_params=pltpu.CompilerParams(
-                dimension_semantics=('arbitrary',), vmem_limit_bytes=56_000_000),
+            compiler_params=pltpu.CompilerParams(vmem_limit_bytes=56_000_000),
             cost_estimate=pl.CostEstimate(flops=40_000_000_000, bytes_accessed=160_000_000, transcendentals=0),
         )(y, dg, xa, dya, cm, gm, a, duv, xef, dof)
         dx = (ka + rx + ry + rd).astype(BF16)

time: 223 us -> 205 us (0.919)
  Pallas kernels: 214 us -> 198 us
    pallas_call x1, Pallas kernels: 67 us -> 50.6 us  [local(): pl.pallas_call(functools.partial(grad_kernel, el), in_specs=[vm, vm, anys...]
  transfers between devices with their start and end apart: 3 -> 3, of which waited for: 0 -> 0; matrix products, arithmetic and copies ran while one was open for 0% -> 0% of each run, Pallas kernels for 30% -> 25%
where the time goes in v7:
time: 205 us
  Pallas kernels  198 us (97%)
  starting transfers between devices  3.51 us (2%)
    pallas_call x1, Pallas kernels, local(): pl.pallas_call(functools.partial(main_kernel, el), in_specs=[anyspec, any...  147 us
    pallas_call x1, Pallas kernels, local(): pl.pallas_call(functools.partial(grad_kernel, el), in_specs=[vm, vm, anys...  50.6 us
  transfers between devices with their start and end apart: 3, of which 0 were waited for; matrix products, arithmetic and copies ran while one was open for 0% of the time, Pallas kernels for 25%

profile of v7, /device:TPU:0, one launch (start us, length us, event | category | flops | bytes accessed | tf_op | source)
XLA Modules:
  0.0 204.9 jit_solution(18127278131172036845)
XLA Ops:
  0.6 147.4 %shard_map.118 = (bf16[256,896]{1,0:T(8,128)(2,1)}, f32[8,256]{1,0:T(8,128)}, f32[256,896]{1,0:T(8,128)}, f32[256,896]{1,0:T(8,128)}, f32[256,896]{1,0:T(8,128)}...) custom-call(bf16[256,896]{1,0:T(8,128)(2,1)} %x_hbm.1, ...), custom_call_target="tpu_custom_call" | custom-call | flops 40000000000 | bytes 160000000 | tf_op jit(solution)/shard_map/pallas_call | solution.py:648
  148.0 0.8 collective-permute-start
  148.8 1.2 collective-permute-start.1
  150.1 1.5 collective-permute-start.2
  151.5 0.0 copy-start
  151.6 1.0 copy-done
  152.5 0.0 copy-start.1
  152.5 0.7 copy-done.1
  153.2 0.0 copy-start.2
  153.2 50.6 %shard_map.119 = (bf16[256,896]{1,0:T(8,128)(2,1)}, f32[8,256]{1,0:T(8,128)}, f32[48,896,256]{2,1,0:T(8,128)}, f32[48,896,256]{2,1,0:T(8,128)}, f32[48,256,896]{2,1,0:T(8,128)}) custom-call(bf16[256,896]{1,0:T(8,128)(2,1)} %get-tuple-element.25.y_ref, f32[8,256]{1,0:T(8,128)S(1)} %copy-done.1, bf16[8,256,896]{2,1,0:T(8,128)(2,1)} %get-tuple-element.27.xa_hbm, ...), custom_call_target="tpu_custom_call" | custom-call | flops 40000000000 | bytes 160000000 | tf_op jit(solution)/shard_map/pallas_call | solution.py:705
  203.9 0.0 collective-permute-done
  203.9 0.0 collective-permute-done.1
  203.9 0.0 collective-permute-done.2
  203.9 0.0 copy-done.2
  203.9 0.9 add_convert_fusion
Async XLA Ops:
  148.0 55.8 %collective-permute-start = (f32[256,896]{1,0:T(8,128)}, f32[256,896]{1,0:T(8,128)S(1)}, u32[]{:S(2)}, u32[]{:S(2)}) collective-permute-start(f32[256,896]{1,0:T(8,128)} %get-tuple-element.37), channel_id=1, source_target_pairs={{0,2},{1,3},{2,0},{3,1},{4,6},{5,7},{6,4},{7,5}} | collective-permute-start | bytes 2752520 | tf_op jit(solution)/shard_map/ppermute | solution.py:703
  148.8 55.0 %collective-permute-start.1 = (f32[256,896]{1,0:T(8,128)}, f32[256,896]{1,0:T(8,128)S(1)}, u32[]{:S(2)}, u32[]{:S(2)}) collective-permute-start(f32[256,896]{1,0:T(8,128)} %get-tuple-element.38), channel_id=1, source_target_pairs={{0,4},{1,5},{2,6},{3,7},{4,0},{5,1},{6,2},{7,3}} | collective-permute-start | bytes 2752520 | tf_op jit(solution)/shard_map/ppermute | solution.py:704
  150.1 53.8 %collective-permute-start.2 = (f32[256,896]{1,0:T(8,128)}, f32[256,896]{1,0:T(8,128)S(1)}, u32[]{:S(2)}, u32[]{:S(2)}) collective-permute-start(f32[256,896]{1,0:T(8,128)} %get-tuple-element.39), channel_id=1, source_target_pairs={{0,6},{1,7},{2,4},{3,5},{4,2},{5,3},{6,0},{7,1}} | collective-permute-start | bytes 2752520 | tf_op jit(solution)/shard_map/ppermute | solution.py:702
  151.5 1.0 copy-start
  152.5 0.7 copy-start.1
  153.2 50.7 %copy-start.2 = (f32[256,896]{1,0:T(8,128)S(1)}, f32[256,896]{1,0:T(8,128)}, u32[]{:S(2)}) copy-start(f32[256,896]{1,0:T(8,128)} %get-tuple-element.36) | copy-start | bytes 2752516

commit v8 on v7

--- a/solution.py
+++ b/solution.py
@@ -120,7 +120,7 @@
         return [pltpu.make_async_copy(h.at[k], v.at[b], wsem.at[n, b])
                 for n, (h, v) in enumerate(((w1_hbm, w1b), (w3_hbm, w3b), (w2_hbm, w2b)))]
 
-    for e in range(2 * PAIR):
+    for e in range(NBUF):
         for c in wcopies(e):
             c.start()
 
@@ -288,10 +288,11 @@
             for c in wcopies(n + k):
                 c.wait()
 
-        @pl.when(n + 2 * PAIR < 2 * el)
+    def release(n):
+        @pl.when(n + NBUF < 2 * el)
         def _():
             for k in range(PAIR):
-                for c in wcopies(n + 2 * PAIR + k):
+                for c in wcopies(n + NBUF + k):
                     c.start()
 
     def w13_of(n):
@@ -310,10 +311,12 @@
             fetch(base + r * PAIR)
             second(r - 1)
             first(r)
+            release(base + (r - 1) * PAIR)
             return 0
 
         lax.fori_loop(1, npair, step, 0)
         second(npair - 1)
+        release(base + (npair - 1) * PAIR)
 
     def act(uv):
         u, v = uv[:, :ff], uv[:, ff:]
@@ -527,9 +530,9 @@
     duv_copy(ng - 1).wait()
 
 
-def grad_kernel(el, y_ref, dg_ref, xa_hbm, dya_hbm, cm, gm, a_hbm, duv_hbm, xef_hbm, dof_hbm,
+def grad_kernel(el, y_hbm, dg_hbm, xa_hbm, dya_hbm, cm_hbm, gm_hbm, a_hbm, duv_hbm, xef_hbm, dof_hbm,
                 yo_ref, dgo_ref, gw1_hbm, gw3_hbm, gw2_hbm,
-                xs, dys, xe_s, do_s, a_s, duv_s, g1b, g3b, g2b, lsem, isem, gsem):
+                xs, dys, cm, gm, xe_s, do_s, a_s, duv_s, g1b, g3b, g2b, lsem, isem, gsem):
     ng = el // GRP
     npair = GRP // PAIR
     ff = a_s.shape[3]
@@ -545,11 +548,10 @@
                 for n, (h, v) in enumerate(((gw1_hbm, g1b), (gw3_hbm, g3b), (gw2_hbm, g2b)))]
 
     heads = [pltpu.make_async_copy(xef_hbm, xe_s.at[0], lsem.at[2]), pltpu.make_async_copy(dof_hbm, do_s.at[0], lsem.at[3])]
-    loads = [pltpu.make_async_copy(xa_hbm, xs, lsem.at[0]), pltpu.make_async_copy(dya_hbm, dys, lsem.at[1])]
+    loads = [pltpu.make_async_copy(h, v, lsem.at[n]) for n, h, v in (
+        (0, xa_hbm, xs), (1, dya_hbm, dys), (4, cm_hbm, cm), (5, gm_hbm, gm), (6, y_hbm, yo_ref), (7, dg_hbm, dgo_ref))]
     for c in heads + inputs(0) + loads:
         c.start()
-    yo_ref[...] = y_ref[...]
-    dgo_ref[...] = dg_ref[...]
 
     def gather(g, q):
         slot = lax.rem(g, 2)
@@ -704,12 +706,14 @@
         ry = lax.ppermute(sy, grp, perm(1, 0))
         y, dg, gw1, gw3, gw2 = pl.pallas_call(
             functools.partial(grad_kernel, el),
-            in_specs=[vm, vm, anyspec, anyspec, vm, vm] + [anyspec] * 4,
+            in_specs=[anyspec] * 10,
             out_specs=[vm, vm, anyspec, anyspec, anyspec],
             out_shape=[sds((tok, d), BF16), sds((top, tok), F32), sds((el, d, ff), F32), sds((el, d, ff), F32), sds((el, ff, d), F32)],
             scratch_shapes=[
                 pltpu.VMEM((NP, tok, d), BF16),
                 pltpu.VMEM((NP, tok, d), BF16),
+                pltpu.VMEM((NP, el, tok), F32),
+                pltpu.VMEM((NP, el, tok), F32),
                 pltpu.VMEM((2, GRP, NROW, d), BF16),
                 pltpu.VMEM((2, GRP, NROW, d), BF16),
                 pltpu.VMEM((2, GRP, NROW, ff), BF16),
@@ -717,7 +721,7 @@
                 pltpu.VMEM((NOUT, PAIR, d, ff), F32),
                 pltpu.VMEM((NOUT, PAIR, d, ff), F32),
                 pltpu.VMEM((NOUT, PAIR, ff, d), F32),
-                dma((4,)), dma((2, 2)), dma((3, NOUT)),
+                dma((8,)), dma((2, 2)), dma((3, NOUT)),
             ],
             compiler_params=pltpu.CompilerParams(vmem_limit_bytes=56_000_000),
             cost_estimate=pl.CostEstimate(flops=40_000_000_000, bytes_accessed=160_000_000, transcendentals=0),

time: 205 us -> 202 us (0.985)
  Pallas kernels: 198 us -> 194 us
    pallas_call x1, Pallas kernels: 147 us -> 144 us  [local(): pl.pallas_call(functools.partial(main_kernel, el), in_specs=[anyspec, any...]
where the time goes in v8:
time: 202 us; the launch traced here: 201 us
  Pallas kernels  194 us (96%)
  starting transfers between devices  3.51 us (2%)
    pallas_call x1, Pallas kernels, local(): pl.pallas_call(functools.partial(main_kernel, el), in_specs=[anyspec, any...  144 us
    pallas_call x1, Pallas kernels, local(): pl.pallas_call(functools.partial(grad_kernel, el), in_specs=[anyspec] * 1...  50 us
  transfers between devices with their start and end apart: 3, of which 0 were waited for; matrix products, arithmetic and copies ran while one was open for 0% of the time, Pallas kernels for 25%

profile of v8, /device:TPU:0, one launch (start us, length us, event | category | flops | bytes accessed | tf_op | source)
XLA Modules:
  0.0 201.2 jit_solution(8212803511197538142)
XLA Ops:
  0.6 144.4 %shard_map.118 = (bf16[256,896]{1,0:T(8,128)(2,1)}, f32[8,256]{1,0:T(8,128)}, f32[256,896]{1,0:T(8,128)}, f32[256,896]{1,0:T(8,128)}, f32[256,896]{1,0:T(8,128)}...) custom-call(bf16[256,896]{1,0:T(8,128)(2,1)} %x_hbm.1, ...), custom_call_target="tpu_custom_call" | custom-call | flops 40000000000 | bytes 160000000 | tf_op jit(solution)/shard_map/pallas_call | solution.py:650
  145.1 0.6 collective-permute-start
  145.7 1.5 collective-permute-start.1
  147.1 1.5 collective-permute-start.2
  148.6 0.0 copy-start
  148.6 1.0 copy-done
  149.6 0.0 copy-start.1
  149.6 0.7 copy-done.1
  150.3 0.0 copy-start.2
  150.3 50.0 %shard_map.119 = (bf16[256,896]{1,0:T(8,128)(2,1)}, f32[8,256]{1,0:T(8,128)}, f32[48,896,256]{2,1,0:T(8,128)}, f32[48,896,256]{2,1,0:T(8,128)}, f32[48,256,896]{2,1,0:T(8,128)}) custom-call(bf16[256,896]{1,0:T(8,128)(2,1)} %get-tuple-element.25.y_hbm, f32[8,256]{1,0:T(8,128)S(1)} %copy-done.1, bf16[8,256,896]{2,1,0:T(8,128)(2,1)} %get-tuple-element.27.xa_hbm, ...), custom_call_target="tpu_custom_call" | custom-call | flops 40000000000 | bytes 160000000 | tf_op jit(solution)/shard_map/pallas_call | solution.py:707
  200.3 0.0 collective-permute-done
  200.3 0.0 collective-permute-done.1
  200.3 0.0 collective-permute-done.2
  200.3 0.0 copy-done.2
  200.3 0.9 add_convert_fusion
Async XLA Ops:
  145.1 55.2 %collective-permute-start = (f32[256,896]{1,0:T(8,128)}, f32[256,896]{1,0:T(8,128)S(1)}, u32[]{:S(2)}, u32[]{:S(2)}) collective-permute-start(f32[256,896]{1,0:T(8,128)} %get-tuple-element.37), channel_id=1, source_target_pairs={{0,2},{1,3},{2,0},{3,1},{4,6},{5,7},{6,4},{7,5}} | collective-permute-start | bytes 2752520 | tf_op jit(solution)/shard_map/ppermute | solution.py:705
  145.7 54.6 %collective-permute-start.1 = (f32[256,896]{1,0:T(8,128)}, f32[256,896]{1,0:T(8,128)S(1)}, u32[]{:S(2)}, u32[]{:S(2)}) collective-permute-start(f32[256,896]{1,0:T(8,128)} %get-tuple-element.38), channel_id=1, source_target_pairs={{0,4},{1,5},{2,6},{3,7},{4,0},{5,1},{6,2},{7,3}} | collective-permute-start | bytes 2752520 | tf_op jit(solution)/shard_map/ppermute | solution.py:706
  147.1 53.2 %collective-permute-start.2 = (f32[256,896]{1,0:T(8,128)}, f32[256,896]{1,0:T(8,128)S(1)}, u32[]{:S(2)}, u32[]{:S(2)}) collective-permute-start(f32[256,896]{1,0:T(8,128)} %get-tuple-element.39), channel_id=1, source_target_pairs={{0,6},{1,7},{2,4},{3,5},{4,2},{5,3},{6,0},{7,1}} | collective-permute-start | bytes 2752520 | tf_op jit(solution)/shard_map/ppermute | solution.py:704
  148.6 1.0 copy-start
  149.6 0.7 copy-start.1
  150.3 50.0 %copy-start.2 = (f32[256,896]{1,0:T(8,128)S(1)}, f32[256,896]{1,0:T(8,128)}, u32[]{:S(2)}) copy-start(f32[256,896]{1,0:T(8,128)} %get-tuple-element.36) | copy-start | bytes 2752516

commit v9 on v8

--- a/solution.py
+++ b/solution.py
@@ -304,7 +304,6 @@
 
     def skewed(g, first, base, second):
         npair = GRP // PAIR
-        fetch(base)
         first(0)
 
         def step(r, _):
@@ -316,7 +315,6 @@
 
         lax.fori_loop(1, npair, step, 0)
         second(npair - 1)
-        release(base + (npair - 1) * PAIR)
 
     def act(uv):
         u, v = uv[:, :ff], uv[:, ff:]
@@ -377,11 +375,8 @@
     dof_copy = pltpu.make_async_copy(do_s, dof_hbm, osem.at[7])
 
     def fwd_group(g, _):
+        fetch(g * GRP)
         gather_all(g, xs)
-
-        @pl.when(g == 0)
-        def _():
-            xef_copy.start()
 
         def f1(r):
             for k in range(PAIR):
@@ -395,7 +390,12 @@
                 put_rows(i, nn(act(uvs[k])[3], w2_of(g * GRP + i)))
 
         skewed(g, f1, g * GRP, f2)
+
+        @pl.when(g == 0)
+        def _():
+            xef_copy.start()
         combine_y(g)
+        release(g * GRP + GRP - PAIR)
 
         @pl.when(g == 0)
         def _():
@@ -424,15 +424,12 @@
         return pltpu.make_async_copy(a_s, a_hbm.at[ds(g, GRP)], osem.at[5])
 
     def bwd_group(g, _):
+        @pl.when(g > 0)
+        def _():
+            a_copy(g - 1).wait()
+            duv_copy(g - 1).wait()
+        fetch(el + g * GRP)
         gather_dy(g)
-
-        @pl.when(g == 0)
-        def _():
-            dof_copy.start()
-
-        @pl.when(g == 0)
-        def _():
-            rs_start(0, yacc)
 
         def b1(r):
             uvs = [uv_s[g * GRP + r * PAIR + k] for k in range(PAIR)]
@@ -455,11 +452,6 @@
                 i = r * PAIR + k
                 put_rows(i, nt(duvs[k], w13_of(el + g * GRP + i)))
 
-        @pl.when(g > 0)
-        def _():
-            a_copy(g - 1).wait()
-            duv_copy(g - 1).wait()
-
         skewed(g, b1, el + g * GRP, b2)
         a_copy(g).start()
         duv_copy(g).start()
@@ -470,9 +462,12 @@
             pl.semaphore_wait(credit, 1)
             rs_start(1, dxacc)
         combine_dx(g, C)
+        release(el + g * GRP + GRP - PAIR)
 
         @pl.when(g == 0)
         def _():
+            dof_copy.start()
+            rs_start(0, yacc)
             dof_copy.wait()
 
         @pl.when(g == 1)
@@ -706,7 +701,7 @@
         ry = lax.ppermute(sy, grp, perm(1, 0))
         y, dg, gw1, gw3, gw2 = pl.pallas_call(
             functools.partial(grad_kernel, el),
-            in_specs=[anyspec] * 10,
+            in_specs=[pl.BlockSpec(memory_space=pltpu.HBM)] * 10,
             out_specs=[vm, vm, anyspec, anyspec, anyspec],
             out_shape=[sds((tok, d), BF16), sds((top, tok), F32), sds((el, d, ff), F32), sds((el, d, ff), F32), sds((el, ff, d), F32)],
             scratch_shapes=[
@@ -723,7 +718,7 @@
                 pltpu.VMEM((NOUT, PAIR, ff, d), F32),
                 dma((8,)), dma((2, 2)), dma((3, NOUT)),
             ],
-            compiler_params=pltpu.CompilerParams(vmem_limit_bytes=56_000_000),
+            compiler_params=pltpu.CompilerParams(vmem_limit_bytes=67_000_000),
             cost_estimate=pl.CostEstimate(flops=40_000_000_000, bytes_accessed=160_000_000, transcendentals=0),
         )(y, dg, xa, dya, cm, gm, a, duv, xef, dof)
         dx = (ka + rx + ry + rd).astype(BF16)

time: 202 us -> 203 us (level)
  no operation moved by 1% of the time
where the time goes in v9:
time: 203 us
  Pallas kernels  196 us (97%)
  starting transfers between devices  3.51 us (2%)
  other arithmetic  2.94 us (1%)
    pallas_call x1, Pallas kernels, local(): pl.pallas_call(functools.partial(main_kernel, el), in_specs=[anyspec, any...  145 us
    pallas_call x1, Pallas kernels, local(): pl.pallas_call(functools.partial(grad_kernel, el), in_specs=[pl.BlockSpec...  50.8 us
  transfers between devices with their start and end apart: 3, of which 0 were waited for; matrix products, arithmetic and copies ran while one was open for 0% of the time, Pallas kernels for 25%

profile of v9, /device:TPU:0, one launch (start us, length us, event | category | flops | bytes accessed | tf_op | source)
XLA Modules:
  0.0 203.1 jit_solution(17414964727708043701)
XLA Ops:
  0.6 145.2 %shard_map.118 = (bf16[256,896]{1,0:T(8,128)(2,1)}, f32[8,256]{1,0:T(8,128)}, f32[256,896]{1,0:T(8,128)}, f32[256,896]{1,0:T(8,128)}, f32[256,896]{1,0:T(8,128)}...) custom-call(bf16[256,896]{1,0:T(8,128)(2,1)} %x_hbm.1, ...), custom_call_target="tpu_custom_call" | custom-call | flops 40000000000 | bytes 160000000 | tf_op jit(solution)/shard_map/pallas_call | solution.py:645
  145.8 0.7 collective-permute-start
  146.5 1.3 collective-permute-start.1
  147.9 1.5 collective-permute-start.2
  149.3 50.8 %shard_map.119 = (bf16[256,896]{1,0:T(8,128)(2,1)}, f32[8,256]{1,0:T(8,128)}, f32[48,896,256]{2,1,0:T(8,128)}, f32[48,896,256]{2,1,0:T(8,128)}, f32[48,256,896]{2,1,0:T(8,128)}) custom-call(bf16[256,896]{1,0:T(8,128)(2,1)} %get-tuple-element.25.y_hbm, f32[8,256]{1,0:T(8,128)} %get-tuple-element.26.dg_hbm, bf16[8,256,896]{2,1,0:T(8,128)(2,1)} %get-tuple-element.27.xa_hbm, ...), custom_call_target="tpu_custom_call" | custom-call | flops 40000000000 | bytes 160000000 | tf_op jit(solution)/shard_map/pallas_call | solution.py:702
  200.2 0.0 collective-permute-done
  200.2 0.0 collective-permute-done.1
  200.2 0.0 collective-permute-done.2
  200.2 2.9 %add_convert_fusion = bf16[256,896]{1,0:T(8,128)(2,1)} fusion(f32[256,896]{1,0:T(8,128)} %collective-permute-done.2, f32[256,896]{1,0:T(8,128)} %collective-permute-done.1, f32[256,896]{1,0:T(8,128)} %get-tuple-element.36, f32[256,896]{1,0:T(8,128)} %collective-permute-done), kind=kLoop, calls=%fused_computation | loop fusion | flops 917504 | bytes 4128768 | tf_op jit(solution)/shard_map/convert_element_type | solution.py:724
Async XLA Ops:
  145.8 54.4 %collective-permute-start = (f32[256,896]{1,0:T(8,128)}, f32[256,896]{1,0:T(8,128)}, u32[]{:S(2)}, u32[]{:S(2)}) collective-permute-start(f32[256,896]{1,0:T(8,128)} %get-tuple-element.37), channel_id=1, source_target_pairs={{0,2},{1,3},{2,0},{3,1},{4,6},{5,7},{6,4},{7,5}} | collective-permute-start | bytes 2752520 | tf_op jit(solution)/shard_map/ppermute | solution.py:700
  146.5 53.6 %collective-permute-start.1 = (f32[256,896]{1,0:T(8,128)}, f32[256,896]{1,0:T(8,128)}, u32[]{:S(2)}, u32[]{:S(2)}) collective-permute-start(f32[256,896]{1,0:T(8,128)} %get-tuple-element.38), channel_id=1, source_target_pairs={{0,4},{1,5},{2,6},{3,7},{4,0},{5,1},{6,2},{7,3}} | collective-permute-start | bytes 2752520 | tf_op jit(solution)/shard_map/ppermute | solution.py:701
  147.9 52.3 %collective-permute-start.2 = (f32[256,896]{1,0:T(8,128)}, f32[256,896]{1,0:T(8,128)}, u32[]{:S(2)}, u32[]{:S(2)}) collective-permute-start(f32[256,896]{1,0:T(8,128)} %get-tuple-element.39), channel_id=1, source_target_pairs={{0,6},{1,7},{2,4},{3,5},{4,2},{5,3},{6,0},{7,1}} | collective-permute-start | bytes 2752520 | tf_op jit(solution)/shard_map/ppermute | solution.py:699

commit v10 on v9

--- a/solution.py
+++ b/solution.py
@@ -390,12 +390,12 @@
                 put_rows(i, nn(act(uvs[k])[3], w2_of(g * GRP + i)))
 
         skewed(g, f1, g * GRP, f2)
+        release(g * GRP + GRP - PAIR)
 
         @pl.when(g == 0)
         def _():
             xef_copy.start()
         combine_y(g)
-        release(g * GRP + GRP - PAIR)
 
         @pl.when(g == 0)
         def _():
@@ -718,7 +718,7 @@
                 pltpu.VMEM((NOUT, PAIR, ff, d), F32),
                 dma((8,)), dma((2, 2)), dma((3, NOUT)),
             ],
-            compiler_params=pltpu.CompilerParams(vmem_limit_bytes=67_000_000),
+            compiler_params=pltpu.CompilerParams(vmem_limit_bytes=56_000_000),
             cost_estimate=pl.CostEstimate(flops=40_000_000_000, bytes_accessed=160_000_000, transcendentals=0),
         )(y, dg, xa, dya, cm, gm, a, duv, xef, dof)
         dx = (ka + rx + ry + rd).astype(BF16)

time: 203 us -> 202 us (level)
  no operation moved by 1% of the time
where the time goes in v10:
time: 202 us
  Pallas kernels  195 us (97%)
  starting transfers between devices  3.51 us (2%)
    pallas_call x1, Pallas kernels, local(): pl.pallas_call(functools.partial(main_kernel, el), in_specs=[anyspec, any...  145 us
    pallas_call x1, Pallas kernels, local(): pl.pallas_call(functools.partial(grad_kernel, el), in_specs=[pl.BlockSpec...  50 us
  transfers between devices with their start and end apart: 3, of which 0 were waited for; matrix products, arithmetic and copies ran while one was open for 0% of the time, Pallas kernels for 25%

profile of v10, /device:TPU:0, one launch (start us, length us, event | category | flops | bytes accessed | tf_op | source)
XLA Modules:
  0.0 202.0 jit_solution(10389846365642636013)
XLA Ops:
  0.6 145.2 %shard_map.118 = (bf16[256,896]{1,0:T(8,128)(2,1)}, f32[8,256]{1,0:T(8,128)}, f32[256,896]{1,0:T(8,128)}, f32[256,896]{1,0:T(8,128)}, f32[256,896]{1,0:T(8,128)}...) custom-call(bf16[256,896]{1,0:T(8,128)(2,1)} %x_hbm.1, ...), custom_call_target="tpu_custom_call" | custom-call | flops 40000000000 | bytes 160000000 | tf_op jit(solution)/shard_map/pallas_call | solution.py:645
  145.8 0.8 collective-permute-start
  146.6 1.3 collective-permute-start.1
  147.8 1.5 collective-permute-start.2
  149.3 0.0 copy-start
  149.3 1.0 copy-done
  150.3 0.0 copy-start.1
  150.3 0.7 copy-done.1
  151.0 0.0 copy-start.2
  151.0 50.0 %shard_map.119 = (bf16[256,896]{1,0:T(8,128)(2,1)}, f32[8,256]{1,0:T(8,128)}, f32[48,896,256]{2,1,0:T(8,128)}, f32[48,896,256]{2,1,0:T(8,128)}, f32[48,256,896]{2,1,0:T(8,128)}) custom-call(bf16[256,896]{1,0:T(8,128)(2,1)} %get-tuple-element.25.y_hbm, f32[8,256]{1,0:T(8,128)S(1)} %copy-done.1, bf16[8,256,896]{2,1,0:T(8,128)(2,1)} %get-tuple-element.27.xa_hbm, ...), custom_call_target="tpu_custom_call" | custom-call | flops 40000000000 | bytes 160000000 | tf_op jit(solution)/shard_map/pallas_call | solution.py:702
  201.0 0.0 collective-permute-done
  201.0 0.0 collective-permute-done.1
  201.0 0.0 collective-permute-done.2
  201.0 0.0 copy-done.2
  201.0 0.9 add_convert_fusion
Async XLA Ops:
  145.8 55.2 %collective-permute-start = (f32[256,896]{1,0:T(8,128)}, f32[256,896]{1,0:T(8,128)S(1)}, u32[]{:S(2)}, u32[]{:S(2)}) collective-permute-start(f32[256,896]{1,0:T(8,128)} %get-tuple-element.37), channel_id=1, source_target_pairs={{0,2},{1,3},{2,0},{3,1},{4,6},{5,7},{6,4},{7,5}} | collective-permute-start | bytes 2752520 | tf_op jit(solution)/shard_map/ppermute | solution.py:700
  146.6 54.4 %collective-permute-start.1 = (f32[256,896]{1,0:T(8,128)}, f32[256,896]{1,0:T(8,128)S(1)}, u32[]{:S(2)}, u32[]{:S(2)}) collective-permute-start(f32[256,896]{1,0:T(8,128)} %get-tuple-element.38), channel_id=1, source_target_pairs={{0,4},{1,5},{2,6},{3,7},{4,0},{5,1},{6,2},{7,3}} | collective-permute-start | bytes 2752520 | tf_op jit(solution)/shard_map/ppermute | solution.py:701
  147.8 53.2 %collective-permute-start.2 = (f32[256,896]{1,0:T(8,128)}, f32[256,896]{1,0:T(8,128)S(1)}, u32[]{:S(2)}, u32[]{:S(2)}) collective-permute-start(f32[256,896]{1,0:T(8,128)} %get-tuple-element.39), channel_id=1, source_target_pairs={{0,6},{1,7},{2,4},{3,5},{4,2},{5,3},{6,0},{7,1}} | collective-permute-start | bytes 2752520 | tf_op jit(solution)/shard_map/ppermute | solution.py:699
  149.3 1.0 copy-start
  150.3 0.7 copy-start.1
  151.0 50.0 %copy-start.2 = (f32[256,896]{1,0:T(8,128)S(1)}, f32[256,896]{1,0:T(8,128)}, u32[]{:S(2)}) copy-start(f32[256,896]{1,0:T(8,128)} %get-tuple-element.36) | copy-start | bytes 2752516
